TPU v7x, 32 devices: a whole 2x2x4 slice. The times are simulated.
32 devices in a mesh: dp: 8 (over z, x), tensor: 4 (over y, core).
Axes of the slice: x: 2, y: 2, z: 4, core: 2. Of those that a mesh axis runs over, the one named last changes fastest.
Arguments:
- hidden_in: bfloat16 [4096, 2048], P('dp'), may hold values from -40 to 40
- seq_lens: int32 [8, 8], P('dp'), may hold values from 0 to 512, as said below
- norm1_gain: float32 [2048], replicated, may hold values from 0.5 to 1.5
- query_weight: bfloat16 [2048, 4096], P(None, 'tensor'), may hold values from -0.125 to 0.125
- key_weight: bfloat16 [2048, 512], P(None, 'tensor'), may hold values from -0.125 to 0.125
- value_weight: bfloat16 [2048, 512], P(None, 'tensor'), may hold values from -0.125 to 0.125
- query_gain: float32 [128], replicated, may hold values from 0.5 to 1.5
- key_gain: float32 [128], replicated, may hold values from 0.5 to 1.5
- out_weight: bfloat16 [4096, 2048], P('tensor'), may hold values from -0.75 to 0.75
- norm2_gain: float32 [2048], replicated, may hold values from 0.5 to 1.5
- w_gate_up: bfloat16 [16, 2048, 2, 768], P('dp', None, None, 'tensor'), may hold values from -0.125 to 0.125
- w_down: bfloat16 [16, 768, 2048], P('dp', 'tensor'), may hold values from -0.875 to 0.875
- routes: int32 [4096, 8], P('dp'), may hold values from 0 to 15, all different within a row; in each aligned block of 512 rows (0 to 511, 512 to 1023, ...) at most 384 rows name the same one
- route_weights: float32 [4096, 8], P('dp'), may hold values from 0.05 to 0.25
- out_grad: bfloat16 [4096, 2048], P('dp'), may hold values from -6 to 6
Outputs:
- hidden_out: bfloat16 [4096, 2048], P('dp')
- hidden_grad: bfloat16 [4096, 2048], P('dp')
- grad_norm1_gain: float32 [2048], replicated
- grad_query_weight: float32 [2048, 4096], P(None, 'tensor')
- grad_key_weight: float32 [2048, 512], P(None, 'tensor')
- grad_value_weight: float32 [2048, 512], P(None, 'tensor')
- grad_query_gain: float32 [128], replicated
- grad_key_gain: float32 [128], replicated
- grad_out_weight: float32 [4096, 2048], P('tensor')
- grad_norm2_gain: float32 [2048], replicated
- grad_w_gate_up: float32 [16, 2048, 2, 768], P('dp', None, None, 'tensor')
- grad_w_down: float32 [16, 768, 2048], P('dp', 'tensor')
Inputs may be any that keep to these rules, and one draw needn't show every extreme that they name: `seq_lens`: each row sums to 512; zeros are empty slots; some row holds a single sequence of 512. `routes`: A row names 8 different experts. In the rows of one index of dp no expert is named by more than 384 rows, a bound that some block reaches.
All inputs are finite; a program needn't handle non-finite values.
Results may differ from a plain program's by a relative error of at most 0.028.
Values may be sent and summed in bfloat16 or wider, within the bound.
A program may use at most 384 MiB of HBM per device.

v0:
```python
import math

import jax
import jax.numpy as jnp
from jax import lax
from jax.sharding import PartitionSpec as P

EPSILON = 1e-06
ROPE_BASE = 1000000.0


def rms_parts(values):
    inverse = lax.rsqrt(jnp.mean(values * values, axis=-1, keepdims=True) + EPSILON)
    return (values * inverse, inverse)


def rms_back(grad_hat, normal_hat, inverse):
    return inverse * (
        grad_hat - normal_hat * jnp.mean(grad_hat * normal_hat, axis=-1, keepdims=True)
    )


def rotary_tables(positions, head_dim):
    halves = jnp.arange(head_dim // 2, dtype=jnp.float32)
    inverse = jnp.exp(halves * (-2.0 * math.log(ROPE_BASE) / head_dim))
    angles = positions.astype(jnp.float32)[:, None] * inverse[None, :]
    return (jnp.cos(angles), jnp.sin(angles))


def rotate(values, cosine_table, sine_table):
    middle_index = values.shape[-1] // 2
    first_half = values[..., :middle_index]
    second = values[..., middle_index:]
    return jnp.concatenate(
        [
            first_half * cosine_table - second * sine_table,
            second * cosine_table + first_half * sine_table,
        ],
        axis=-1,
    )


def rotate_back(gradient, cosine_table, sine_table):
    middle_index = gradient.shape[-1] // 2
    first_half = gradient[..., :middle_index]
    second = gradient[..., middle_index:]
    return jnp.concatenate(
        [
            first_half * cosine_table + second * sine_table,
            second * cosine_table - first_half * sine_table,
        ],
        axis=-1,
    )


def sequence_layout(lengths, token_count):
    endings = jnp.cumsum(lengths)
    places = jnp.arange(token_count, dtype=jnp.int32)
    starts = jnp.sum(jnp.where(endings[None, :] <= places[:, None], lengths[None, :], 0), axis=1)
    return (places, starts)


def local(
    hidden_in,
    seq_lens,
    norm1_gain,
    query_weight,
    key_weight,
    value_weight,
    query_gain,
    key_gain,
    out_weight,
    norm2_gain,
    w_gate_up,
    w_down,
    routes,
    route_weights,
    out_grad,
):
    tokens, model_width = hidden_in.shape
    per_token = routes.shape[1]
    local_experts = w_gate_up.shape[0]
    hidden_part = w_gate_up.shape[3]
    head_dim = query_gain.shape[0]
    local_heads = query_weight.shape[1] // head_dim
    data_size = lax.axis_size("dp")
    capacity = 3 * tokens * per_token // (2 * local_experts * data_size)
    score_scale = head_dim ** (-0.5)
    hidden = hidden_in.astype(jnp.float32)
    hat_one, inv_one = rms_parts(hidden)
    normed = (hat_one * norm1_gain).astype(jnp.bfloat16)
    query_proj = jnp.dot(normed, query_weight, preferred_element_type=jnp.float32).reshape(
        tokens, local_heads, head_dim
    )
    key_proj = jnp.dot(normed, key_weight, preferred_element_type=jnp.float32)
    value_low = jnp.dot(normed, value_weight, preferred_element_type=jnp.float32).astype(
        jnp.bfloat16
    )
    places, starts = sequence_layout(seq_lens[0], tokens)
    cosine_table, sine_table = rotary_tables(places - starts, head_dim)
    query_hat, query_inv = rms_parts(query_proj)
    query_low = rotate(
        query_hat * query_gain, cosine_table[:, None, :], sine_table[:, None, :]
    ).astype(jnp.bfloat16)
    key_hat, key_inv = rms_parts(key_proj)
    key_low = rotate(key_hat * key_gain, cosine_table, sine_table).astype(jnp.bfloat16)
    visible = (places[None, :] <= places[:, None]) & (places[None, :] >= starts[:, None])
    scores = (
        jnp.einsum("thd,sd->hts", query_low, key_low, preferred_element_type=jnp.float32)
        * score_scale
    )
    exponent = jnp.where(visible[None], jnp.exp(scores), 0.0)
    totals = jnp.sum(exponent, axis=-1, keepdims=True)
    log_totals = jnp.log(totals)
    soft_low = (exponent / totals).astype(jnp.bfloat16)
    mixed_low = (
        jnp.einsum("hts,sd->thd", soft_low, value_low, preferred_element_type=jnp.float32)
        .reshape(tokens, local_heads * head_dim)
        .astype(jnp.bfloat16)
    )
    attention = lax.psum(
        jnp.dot(mixed_low, out_weight, preferred_element_type=jnp.float32), "tensor"
    )
    middle = hidden + attention
    hat_two, inv_two = rms_parts(middle)
    normed_two = (hat_two * norm2_gain).astype(jnp.bfloat16)
    flat_experts = routes.reshape(-1)
    owners = flat_experts // local_experts
    resident = flat_experts % local_experts
    onehot = (
        flat_experts[:, None] == jnp.arange(local_experts * data_size, dtype=jnp.int32)[None, :]
    ).astype(jnp.int32)
    rank_within = jnp.sum(jnp.cumsum(onehot, axis=0) * onehot, axis=1) - 1
    slot_index = (resident * data_size + owners) * capacity + rank_within
    sources = jnp.arange(tokens * per_token, dtype=jnp.int32) // per_token

    def scatter_rows(source_rows, columns):
        buffer = jnp.zeros((local_experts * data_size * capacity, columns), jnp.bfloat16)
        return (
            buffer.at[slot_index]
            .set(source_rows)
            .reshape(local_experts, data_size, capacity, columns)
        )

    arrived = lax.all_to_all(
        scatter_rows(normed_two[sources], model_width),
        "dp",
        split_axis=1,
        concat_axis=1,
        tiled=True,
    )
    inputs = arrived.reshape(local_experts, data_size * capacity, model_width)
    stacked = w_gate_up.reshape(local_experts, model_width, 2 * hidden_part)
    gate_up = jnp.einsum("erd,edf->erf", inputs, stacked, preferred_element_type=jnp.float32)
    gate_act = gate_up[..., :hidden_part]
    upward = gate_up[..., hidden_part:]
    sigmoid_gate = jax.nn.sigmoid(gate_act)
    active_low = (gate_act * sigmoid_gate * upward).astype(jnp.bfloat16)
    expert_out = jnp.einsum(
        "erf,efd->erd", active_low, w_down, preferred_element_type=jnp.float32
    ).astype(jnp.bfloat16)
    expert_out = expert_out.reshape(local_experts, data_size, capacity, model_width)
    returned = (
        lax.all_to_all(expert_out, "dp", split_axis=1, concat_axis=1, tiled=True)
        .reshape(-1, model_width)[slot_index]
        .reshape(tokens, per_token, model_width)
    )
    mixture_part = jnp.sum(route_weights[:, :, None] * returned, axis=1)
    mixture = lax.psum(mixture_part.astype(jnp.bfloat16), "tensor").astype(jnp.float32)
    hidden_out = (middle + mixture).astype(jnp.bfloat16)
    grad_out = out_grad.astype(jnp.float32)
    grad_routes = (
        (route_weights[:, :, None] * grad_out[:, None, :])
        .astype(jnp.bfloat16)
        .reshape(tokens * per_token, model_width)
    )
    grads_in = lax.all_to_all(
        scatter_rows(grad_routes, model_width), "dp", split_axis=1, concat_axis=1, tiled=True
    )
    grads_in = grads_in.reshape(local_experts, data_size * capacity, model_width)
    grad_active = jnp.einsum("erd,efd->erf", grads_in, w_down, preferred_element_type=jnp.float32)
    grad_gate = grad_active * upward * sigmoid_gate * (1.0 + gate_act * (1.0 - sigmoid_gate))
    grad_up = grad_active * gate_act * sigmoid_gate
    grad_gate_up = jnp.concatenate([grad_gate, grad_up], axis=-1).astype(jnp.bfloat16)
    grad_w_down = jnp.einsum(
        "erf,erd->efd", active_low, grads_in, preferred_element_type=jnp.float32
    )
    grad_w_gate_up = jnp.einsum(
        "erd,erf->edf", inputs, grad_gate_up, preferred_element_type=jnp.float32
    ).reshape(w_gate_up.shape)
    grad_inputs = jnp.einsum(
        "erf,edf->erd", grad_gate_up, stacked, preferred_element_type=jnp.float32
    ).astype(jnp.bfloat16)
    grad_inputs = grad_inputs.reshape(local_experts, data_size, capacity, model_width)
    grad_back = (
        lax.all_to_all(grad_inputs, "dp", split_axis=1, concat_axis=1, tiled=True)
        .reshape(-1, model_width)[slot_index]
        .reshape(tokens, per_token, model_width)
    )
    grad_normed_part = jnp.sum(grad_back, axis=1, dtype=jnp.float32)
    grad_normed_two = lax.psum(grad_normed_part.astype(jnp.bfloat16), "tensor").astype(jnp.float32)
    grad_gain_two = jnp.sum(grad_normed_two * hat_two, axis=0)
    grad_middle = grad_out + rms_back(grad_normed_two * norm2_gain, hat_two, inv_two)
    grad_mid_low = grad_middle.astype(jnp.bfloat16)
    grad_out_weight = jnp.einsum(
        "ti,td->id", mixed_low, grad_mid_low, preferred_element_type=jnp.float32
    )
    grad_mixed = (
        jnp.einsum("td,id->ti", grad_mid_low, out_weight, preferred_element_type=jnp.float32)
        .astype(jnp.bfloat16)
        .reshape(tokens, local_heads, head_dim)
    )
    scores_again = (
        jnp.einsum("thd,sd->hts", query_low, key_low, preferred_element_type=jnp.float32)
        * score_scale
    )
    soft_again = jnp.where(visible[None], jnp.exp(scores_again - log_totals), 0.0)
    grad_soft = jnp.einsum("thd,sd->hts", grad_mixed, value_low, preferred_element_type=jnp.float32)
    grad_scores = (
        soft_again * (grad_soft - jnp.sum(soft_again * grad_soft, axis=-1, keepdims=True))
    ).astype(jnp.bfloat16)
    grad_values = jnp.einsum(
        "hts,thd->sd",
        soft_again.astype(jnp.bfloat16),
        grad_mixed,
        preferred_element_type=jnp.float32,
    ).astype(jnp.bfloat16)
    grad_query_rot = score_scale * jnp.einsum(
        "hts,sd->thd", grad_scores, key_low, preferred_element_type=jnp.float32
    )
    grad_key_rot = score_scale * jnp.einsum(
        "hts,thd->sd", grad_scores, query_low, preferred_element_type=jnp.float32
    )
    grad_query_norm = rotate_back(grad_query_rot, cosine_table[:, None, :], sine_table[:, None, :])
    grad_query_gain = jnp.sum(grad_query_norm * query_hat, axis=(0, 1))
    grad_query_low = (
        rms_back(grad_query_norm * query_gain, query_hat, query_inv)
        .reshape(tokens, local_heads * head_dim)
        .astype(jnp.bfloat16)
    )
    grad_key_norm = rotate_back(grad_key_rot, cosine_table, sine_table)
    grad_key_gain = jnp.sum(grad_key_norm * key_hat, axis=0)
    grad_key_low = rms_back(grad_key_norm * key_gain, key_hat, key_inv).astype(jnp.bfloat16)
    grad_query_weight = jnp.einsum(
        "ti,tj->ij", normed, grad_query_low, preferred_element_type=jnp.float32
    )
    grad_key_weight = jnp.einsum(
        "ti,tj->ij", normed, grad_key_low, preferred_element_type=jnp.float32
    )
    grad_value_weight = jnp.einsum(
        "ti,tj->ij", normed, grad_values, preferred_element_type=jnp.float32
    )
    grad_normed_one = jnp.einsum(
        "tj,ij->ti", grad_query_low, query_weight, preferred_element_type=jnp.float32
    )
    grad_normed_one = grad_normed_one + jnp.einsum(
        "tj,ij->ti", grad_key_low, key_weight, preferred_element_type=jnp.float32
    )
    grad_normed_one = grad_normed_one + jnp.einsum(
        "tj,ij->ti", grad_values, value_weight, preferred_element_type=jnp.float32
    )
    grad_normed_one, grad_query_gain, grad_key_gain = (
        lax.psum(grad_normed_one.astype(jnp.bfloat16), "tensor").astype(jnp.float32),
        lax.psum(grad_query_gain.astype(jnp.bfloat16), "tensor").astype(jnp.float32),
        lax.psum(grad_key_gain.astype(jnp.bfloat16), "tensor").astype(jnp.float32),
    )
    grad_gain_one = jnp.sum(grad_normed_one * hat_one, axis=0)
    grad_hidden = grad_middle + rms_back(grad_normed_one * norm1_gain, hat_one, inv_one)
    summed = (
        lax.psum(grad_query_weight.astype(jnp.bfloat16), "dp").astype(jnp.float32),
        lax.psum(grad_key_weight.astype(jnp.bfloat16), "dp").astype(jnp.float32),
        lax.psum(grad_value_weight.astype(jnp.bfloat16), "dp").astype(jnp.float32),
        lax.psum(grad_out_weight.astype(jnp.bfloat16), "dp").astype(jnp.float32),
        lax.psum(grad_query_gain.astype(jnp.bfloat16), "dp").astype(jnp.float32),
        lax.psum(grad_key_gain.astype(jnp.bfloat16), "dp").astype(jnp.float32),
        lax.psum(grad_gain_one.astype(jnp.bfloat16), "dp").astype(jnp.float32),
        lax.psum(grad_gain_two.astype(jnp.bfloat16), "dp").astype(jnp.float32),
    )
    return (
        hidden_out,
        grad_hidden.astype(jnp.bfloat16),
        summed[6],
        summed[0],
        summed[1],
        summed[2],
        summed[4],
        summed[5],
        summed[3],
        summed[7],
        grad_w_gate_up,
        grad_w_down,
    )


def solution(mesh):
    in_specs = (
        P("dp", None),
        P("dp", None),
        P(),
        P(None, "tensor"),
        P(None, "tensor"),
        P(None, "tensor"),
        P(),
        P(),
        P("tensor", None),
        P(),
        P("dp", None, None, "tensor"),
        P("dp", "tensor", None),
        P("dp", None),
        P("dp", None),
        P("dp", None),
    )
    out_specs = (
        P("dp", None),
        P("dp", None),
        P(),
        P(None, "tensor"),
        P(None, "tensor"),
        P(None, "tensor"),
        P(),
        P(),
        P("tensor", None),
        P(),
        P("dp", None, None, "tensor"),
        P("dp", "tensor", None),
    )
    return jax.shard_map(local, mesh=mesh, in_specs=in_specs, out_specs=out_specs, check_vma=False)
```

profile of v0, /device:TPU:0, one launch (start us, length us, event | category | flops | bytes accessed | tf_op | source)
XLA Modules:
  0.0 2910.1 jit_solution(18050270653580437253)
XLA Ops:
  9.4 8.3 reduce-window.19
  19.7 2.1 convert_element_type.174
  22.0 7.8 fusion.1
  29.7 38.0 %scatter_custom_fusion.1 = bf16[6144,2048]{1,0:T(8,128)(2,1)} fusion(s32[4096]{0:T(1024)S(1)} %bitcast.203, bf16[4096,2048]{1,0:T(8,128)(2,1)} %fusion.1, bf16[]{:T(256)} %constant.76.clone.1), kind=kCustom, calls=%fused_computation.12 | custom fusion | bytes 25166336 | tf_op jit(solution)/shard_map/scatter | solution.py:141
  67.8 21.0 copy.205
  88.8 7.4 all-to-all-start.2
  97.2 2.1 fusion.31
  99.3 2.6 multiply_reduce_fusion.5
  105.8 5.2 fusion.93
  115.4 2.6 fusion.51
  120.1 2.6 fusion.12
  122.8 2.4 fusion.42
  128.1 4.4 fusion.98
  132.6 87.5 %all-reduce.9.cloned.1.call-done = f32[512,2048]{1,0:T(8,128)} async-done(((f32[512,2048]{1,0:T(8,128)}), f32[512,2048]{1,0:T(8,128)}) %all-reduce.9.cloned.1.call-update) | async-done | bytes 4194320 | tf_op jit(solution)/shard_map/psum | solution.py:121
  220.1 3.5 multiply_reduce_fusion
  223.6 2.0 copy-done.2
  227.3 33.3 %gather_fusion = bf16[4096,2048]{1,0:T(8,128)(2,1)} fusion(bf16[512,2048]{1,0:T(8,128)(2,1)} %multiply_convert_fusion.3, s32[4096]{0:T(1024)S(1)} %broadcast_clamp_fusion.1), kind=kCustom, calls=%fused_computation | custom fusion | bytes 33570816 | tf_op jit(solution)/shard_map/gather | solution.py:146
  260.7 38.1 %scatter_custom_fusion = bf16[6144,2048]{1,0:T(8,128)(2,1)} fusion(s32[4096]{0:T(1024)S(1)} %bitcast.204, bf16[4096,2048]{1,0:T(8,128)(2,1)} %gather_fusion, bf16[]{:T(256)} %constant.76.clone.1), kind=kCustom, calls=%fused_computation.14 | custom fusion | bytes 25166336 | tf_op jit(solution)/shard_map/scatter | solution.py:141
  298.7 21.0 copy.200
  319.8 320.5 %all-to-all-done.2 = bf16[2,8,384,2048]{3,2,0,1:T(8,128)(2,1)} async-done(((bf16[2,8,384,2048]{3,2,0,1:T(8,128)(2,1)}), bf16[2,8,384,2048]{3,2,0,1:T(8,128)(2,1)}, u32[]{:S(2)}, u32[]{:S(2)}) %all-to-all-start.2) | async-done | bytes 25165856 | tf_op jit(solution)/shard_map/all_to_all | solution.py:177
  640.3 6.4 all-to-all-start
  646.7 21.0 copy.206
  667.7 521.3 %all-to-all-done = bf16[2,8,384,2048]{3,2,0,1:T(8,128)(2,1)} async-done(((bf16[2,8,384,2048]{3,2,0,1:T(8,128)(2,1)}), bf16[2,8,384,2048]{3,2,0,1:T(8,128)(2,1)}, u32[]{:S(2)}, u32[]{:S(2)}) %all-to-all-start) | async-done | bytes 25165856 | tf_op jit(solution)/shard_map/all_to_all | solution.py:145
  1189.0 21.0 copy.201
  1210.0 17.3 fusion.99
  1227.3 17.5 multiply_convert_fusion.1
  1244.8 19.2 convolution_convert_fusion
  1264.1 21.1 copy.209
  1285.2 6.9 all-to-all-start.3
  1292.1 13.2 convolution_convert_fusion.1
  1305.4 21.0 copy.202
  1326.4 507.2 %all-to-all-done.3 = bf16[2,8,384,2048]{3,2,0,1:T(8,128)(2,1)} async-done(((bf16[2,8,384,2048]{3,2,0,1:T(8,128)(2,1)}), bf16[2,8,384,2048]{3,2,0,1:T(8,128)(2,1)}, u32[]{:S(2)}, u32[]{:S(2)}) %all-to-all-start.3) | async-done | bytes 25165856 | tf_op jit(solution)/shard_map/all_to_all | solution.py:196
  1833.6 6.4 all-to-all-start.1
  1841.5 21.0 copy.210
  1862.6 42.7 %gather_fusion.2 = bf16[4096,2048]{1,0:T(8,128)(2,1)} fusion(bf16[6144,2048]{1,0:T(8,128)(2,1)} %bitcast.185, s32[4096]{0:T(1024)S(1)} %broadcast_clamp_fusion), kind=kCustom, calls=%fused_computation.2 | custom fusion | bytes 33570816 | tf_op jit(solution)/shard_map/gather | solution.py:196
  1905.3 14.9 bitcast_reduce_fusion
  1920.4 460.3 %all-to-all-done.1 = bf16[2,8,384,2048]{3,2,0,1:T(8,128)(2,1)} async-done(((bf16[2,8,384,2048]{3,2,0,1:T(8,128)(2,1)}), bf16[2,8,384,2048]{3,2,0,1:T(8,128)(2,1)}, u32[]{:S(2)}, u32[]{:S(2)}) %all-to-all-start.1) | async-done | bytes 25165856 | tf_op jit(solution)/shard_map/all_to_all | solution.py:164
  2380.7 21.0 copy.203
  2401.7 42.8 %gather_fusion.1 = bf16[4096,2048]{1,0:T(8,128)(2,1)} fusion(bf16[6144,2048]{1,0:T(8,128)(2,1)} %bitcast.184, s32[4096]{0:T(1024)S(1)} %broadcast_clamp_fusion), kind=kCustom, calls=%fused_computation.1 | custom fusion | bytes 33570816 | tf_op jit(solution)/shard_map/gather | solution.py:164
  2444.5 16.5 fusion
  2461.1 4.1 fusion.27
  2465.7 3.0 fusion.26
  2468.8 2.4 fusion.43
  2474.4 2.9 fusion.6
  2477.3 3.1 fusion.8
  2480.4 1.9 fusion.44
  2486.8 2.8 fusion.60
  2494.0 2.4 fusion.100
  2496.4 2.1 add_convert_fusion
  2500.0 1.8 convolution_convert_fusion.4
  2503.7 4.5 convolution_convert_fusion.3
  2508.2 4.4 convolution_convert_fusion.2
  2512.6 17.9 fusion.36
  2530.5 13.2 fusion.102
  2543.7 6.0 all-reduce.2
  2549.7 34.3 %all-reduce.15.cloned.1.call-done = (bf16[512,2048]{1,0:T(8,128)(2,1)}, bf16[512,2048]{1,0:T(8,128)(2,1)}) async-done(((bf16[512,2048]{1,0:T(8,128)(2,1)}, bf16[512,2048]{1,0:T(8,128)(2,1)}), (bf16[512,2048]{1,0:T(8,128)(2,1)}, bf16[512,2048]{1,0:T(8,128)(2,1)})) %all-reduce.15.cloned.1.call-update) | async-done | bytes 4194320 | tf_op jit(solution)/shard_map/psum | solution.py:169
  2584.0 2.9 fusion.30
  2586.9 23.1 all-reduce
  2612.2 7.2 fusion.23
  2619.4 268.5 %all-reduce.13.cloned.1.call-done = (bf16[2048,1024]{1,0:T(8,128)(2,1)}, bf16[2048,128]{1,0:T(8,128)(2,1)}, bf16[2048,128]{1,0:T(8,128)(2,1)}, bf16[1024,2048]{1,0:T(8,128)(2,1)}) async-done(((bf16[2048,1024]{1,0:T(8,128)(2,1)}, bf16[2048,128]{1,0:T(8,128)(2,1)}, bf16[2048,128]{1,0:T(8,128)(2,1)}, bf16[1024,2048]{1,0:T(8,128)(2,1)}), (bf16[2048,1024]{1,0:T(8,128)(2,1)}, bf16[2048,128]{1,0:T(8,128)(2,1)}, ...) | async-done | bytes 9437200 | tf_op jit(solution)/shard_map/psum | solution.py:270
  2887.9 2.1 convert_element_type.193
  2890.0 2.1 convert_element_type.195
  2892.1 6.8 convert_element_type.191
  2898.8 4.4 convert_element_type.201
  (230 shorter events, 39.8 us)
Async XLA Ops:
  7.2 1202.8 %copy-start = (bf16[2,2048,2,192]{1,3,2,0:T(8,128)(2,1)S(1)}, bf16[2,2048,2,192]{1,3,2,0:T(8,128)(2,1)}, u32[]{:S(2)}) copy-start(bf16[2,2048,2,192]{1,3,2,0:T(8,128)(2,1)} %param.25) | copy-start | bytes 9437188
  19.5 10.2 copy-start.21
  22.0 238.7 %copy-start.50 = (s32[4096,1]{0,1:T(1,128)}, s32[4096,1]{0,1:T(1,128)S(1)}, u32[]{:S(2)}) copy-start(s32[4096,1]{0,1:T(1,128)S(1)} %compare_select_fusion.1) | copy-start | bytes 49156
  88.8 7.5 copy-start.76
  88.8 10.4 copy-start.52
  88.8 551.5 %all-to-all-start.2 = ((bf16[2,8,384,2048]{3,2,0,1:T(8,128)(2,1)}), bf16[2,8,384,2048]{3,2,0,1:T(8,128)(2,1)}, u32[]{:S(2)}, u32[]{:S(2)}) async-start(bf16[2,8,384,2048]{3,2,0,1:T(8,128)(2,1)} %copy.205), calls=%async_computation.2 | async-start | bytes 50331648 | tf_op jit(solution)/shard_map/all_to_all | solution.py:177
  96.2 6.4 copy-start.72
  96.2 123.8 %all-reduce.9.cloned.1.call-start = ((), (), s32[]{:S(2)}) async-start(), calls=%async_computation.4 | async-start | bytes 8388608 | tf_op jit(solution)/shard_map/psum | solution.py:121
  96.5 7.4 copy-start.74
  97.2 6.8 copy-start.62
  99.2 4.7 copy-start.59
  105.0 14.3 copy-start.29
  111.1 4.2 copy-start.65
  111.1 4.3 copy-start.53
  111.1 4.3 copy-start.60
  112.8 5.3 copy-start.69
  115.2 2.9 copy-start.7
  115.2 2.8 copy-start.43
  115.4 7.4 copy-start.23
  115.4 3.8 copy-start.31
  118.1 4.7 copy-start.46
  120.1 2.7 copy-start.17
  120.1 2.7 copy-start.19
  122.8 4.3 copy-start.4
  122.8 4.3 copy-start.67
  122.8 5.3 copy-start.12
  132.6 93.0 %copy-start.48 = (f32[2048]{0:T(1024)S(1)}, f32[2048]{0:T(1024)}, u32[]{:S(2)}) copy-start(f32[2048]{0:T(1024)} %param.24) | copy-start | bytes 24580
  223.6 37.1 %copy-start.57 = (f32[512]{0:T(512)}, f32[512]{0:T(512)S(1)}, u32[]{:S(2)}) copy-start(f32[512]{0:T(512)S(1)} %add_rsqrt_fusion.1) | copy-start | bytes 6148
  640.3 548.7 %all-to-all-start = ((bf16[2,8,384,2048]{3,2,0,1:T(8,128)(2,1)}), bf16[2,8,384,2048]{3,2,0,1:T(8,128)(2,1)}, u32[]{:S(2)}, u32[]{:S(2)}) async-start(bf16[2,8,384,2048]{3,2,0,1:T(8,128)(2,1)} %copy.200), calls=%async_computation | async-start | bytes 50331648 | tf_op jit(solution)/shard_map/all_to_all | solution.py:145
  1210.0 17.3 copy-start.33
  1244.8 19.2 copy-start.78
  1285.2 6.9 copy-start.9
  1285.2 548.4 %all-to-all-start.3 = ((bf16[2,8,384,2048]{3,2,0,1:T(8,128)(2,1)}), bf16[2,8,384,2048]{3,2,0,1:T(8,128)(2,1)}, u32[]{:S(2)}, u32[]{:S(2)}) async-start(bf16[2,8,384,2048]{3,2,0,1:T(8,128)(2,1)} %copy.209), calls=%async_computation.3 | async-start | bytes 50331648 | tf_op jit(solution)/shard_map/all_to_all | solution.py:196
  1326.4 513.7 %copy-start.44 = (f32[512,8]{0,1:T(8,128)S(1)}, f32[512,8]{0,1:T(8,128)}, u32[]{:S(2)}) copy-start(f32[512,8]{0,1:T(8,128)} %copy-done.43) | copy-start | bytes 49156
  1326.4 514.5 %copy-start.68 = (f32[8,512]{1,0:T(8,128)S(1)}, f32[8,512]{1,0:T(8,128)}, u32[]{:S(2)}) copy-start(f32[8,512]{1,0:T(8,128)} %copy-done.67) | copy-start | bytes 49156
  1326.4 514.5 %copy-start.70 = (f32[128]{0:T(128)S(1)}, f32[128]{0:T(128)}, u32[]{:S(2)}) copy-start(f32[128]{0:T(128)} %param.21) | copy-start | bytes 1540
  1326.4 515.1 %copy-start.51 = (s32[4096,1]{0,1:T(1,128)S(1)}, s32[4096,1]{0,1:T(1,128)}, u32[]{:S(2)}) copy-start(s32[4096,1]{0,1:T(1,128)} %copy-done.50) | copy-start | bytes 49156
  1833.6 547.1 %all-to-all-start.1 = ((bf16[2,8,384,2048]{3,2,0,1:T(8,128)(2,1)}), bf16[2,8,384,2048]{3,2,0,1:T(8,128)(2,1)}, u32[]{:S(2)}, u32[]{:S(2)}) async-start(bf16[2,8,384,2048]{3,2,0,1:T(8,128)(2,1)} %copy.202), calls=%async_computation.1 | async-start | bytes 50331648 | tf_op jit(solution)/shard_map/all_to_all | solution.py:164
  1840.0 621.1 %all-reduce.11.cloned.1.call-start = ((), (), s32[]{:S(2)}) async-start(), calls=%async_computation.5 | async-start | bytes 4194304 | tf_op jit(solution)/shard_map/psum | solution.py:201
  1920.2 663.8 %all-reduce.15.cloned.1.call-start = ((), (), s32[]{:S(2)}) async-start(), calls=%async_computation.7 | async-start | bytes 8388608 | tf_op jit(solution)/shard_map/psum | solution.py:169
  2401.7 42.8 %copy-start.22 = (f32[512,8]{1,0:T(8,128)S(1)}, f32[512,8]{1,0:T(8,128)}, u32[]{:S(2)}) copy-start(f32[512,8]{1,0:T(8,128)} %copy-done.21) | copy-start | bytes 49156
  2444.5 16.5 copy-start.49
  2444.5 16.5 copy-start.58
  2461.1 4.2 copy-start.14
  2461.1 4.7 copy-start.3
  2465.7 3.0 copy-start.13
  2465.7 5.5 slice-start
  2468.8 4.0 slice-start.1
  2468.8 4.0 copy-start.24
  2477.3 3.1 copy-start.18
  2477.3 3.1 copy-start.20
  2482.4 2.5 copy-start.26
  2482.4 2.5 copy-start.56
  2482.4 2.5 copy-start.73
  2482.4 2.7 copy-start.30
  2482.5 2.7 copy-start.32
  2486.8 2.9 copy-start.37
  2493.3 3.1 copy-start.35
  2498.5 389.4 %all-reduce.13.cloned.1.call-start = ((), (), s32[]{:S(2)}) async-start(), calls=%async_computation.6 | async-start | bytes 18874368 | tf_op jit(solution)/shard_map/psum | solution.py:270
  2500.0 3.7 copy-start.36
  2503.7 4.5 copy-start.11
  2503.7 4.5 copy-start.28
  2892.0 6.8 copy-start.16
  2898.8 4.5 copy-start.1
  (25 other events, 40.3 us)
Sparse Core Ops, SparseCore 0:
  132.6 87.3 all-reduce.8
  1920.3 51.7 all-reduce.10
  2498.6 85.3 all-reduce.14
  2589.5 298.3 all-reduce.12
where the time goes:
time: 2920 us; the launch traced here: 2910 us
  waiting for transfers between devices  2200 us (75%)
  local copies, waits for them, and re-layouts  385 us (13%)
  matrix products  147 us (5%)
  other arithmetic  107 us (4%)
    all_to_all x1, waiting for transfers between devices, local(): lax.all_to_all(scatter_rows(normed_two[sources], model_width), 'dp', spli...  521 us
    all_to_all x1, waiting for transfers between devices, local(): lax.all_to_all(grad_inputs, 'dp', split_axis=1, concat_axis=1, tiled=True)  507 us
    all_to_all x1, waiting for transfers between devices, local(): lax.all_to_all(expert_out, 'dp', split_axis=1, concat_axis=1, tiled=True)  460 us
    all_to_all x1, waiting for transfers between devices, local(): lax.all_to_all(scatter_rows(grad_routes, model_width), 'dp', split_axis=1...  320 us
    psum x1, waiting for transfers between devices, local(): lax.psum(grad_query_weight.astype(jnp.bfloat16), 'dp').astype(jnp.float32)  268 us
    psum x1, waiting for transfers between devices, local(): lax.psum(jnp.dot(mixed_low, out_weight, preferred_element_type=jnp.float3...  87.5 us
    scatter x2, local copies, waits for them, and re-layouts, scatter_rows(): return buffer.at[slot_index].set(source_rows).reshape(local_experts, data...  76.1 us
  transfers between devices with their start and end apart: 8, of which 7 were waited for; matrix products, arithmetic and copies ran while one was open for 14% of the time, Pallas kernels for 0%

commit v1 on v0

v1 whole, which is shorter than its diff:
```python
import math

import jax
import jax.numpy as jnp
from jax import lax
from jax.sharding import PartitionSpec as P

EPSILON = 1e-06
ROPE_BASE = 1000000.0


def rms_parts(values):
    inverse = lax.rsqrt(jnp.mean(values * values, axis=-1, keepdims=True) + EPSILON)
    return (values * inverse, inverse)


def rms_back(grad_hat, normal_hat, inverse):
    return inverse * (
        grad_hat - normal_hat * jnp.mean(grad_hat * normal_hat, axis=-1, keepdims=True)
    )


def rotary_tables(positions, head_dim):
    halves = jnp.arange(head_dim // 2, dtype=jnp.float32)
    inverse = jnp.exp(halves * (-2.0 * math.log(ROPE_BASE) / head_dim))
    angles = positions.astype(jnp.float32)[:, None] * inverse[None, :]
    return (jnp.cos(angles), jnp.sin(angles))


def rotate(values, cosine_table, sine_table):
    middle_index = values.shape[-1] // 2
    first_half = values[..., :middle_index]
    second = values[..., middle_index:]
    return jnp.concatenate(
        [
            first_half * cosine_table - second * sine_table,
            second * cosine_table + first_half * sine_table,
        ],
        axis=-1,
    )


def rotate_back(gradient, cosine_table, sine_table):
    middle_index = gradient.shape[-1] // 2
    first_half = gradient[..., :middle_index]
    second = gradient[..., middle_index:]
    return jnp.concatenate(
        [
            first_half * cosine_table + second * sine_table,
            second * cosine_table - first_half * sine_table,
        ],
        axis=-1,
    )


def sequence_layout(lengths, token_count):
    endings = jnp.cumsum(lengths)
    places = jnp.arange(token_count, dtype=jnp.int32)
    starts = jnp.sum(jnp.where(endings[None, :] <= places[:, None], lengths[None, :], 0), axis=1)
    return (places, starts)


def local(
    hidden_in,
    seq_lens,
    norm1_gain,
    query_weight,
    key_weight,
    value_weight,
    query_gain,
    key_gain,
    out_weight,
    norm2_gain,
    w_gate_up,
    w_down,
    routes,
    route_weights,
    out_grad,
):
    bf = jnp.bfloat16
    f32 = jnp.float32
    tokens, model_width = hidden_in.shape
    local_experts = w_gate_up.shape[0]
    hidden_part = w_gate_up.shape[3]
    head_dim = query_gain.shape[0]
    local_heads = query_weight.shape[1] // head_dim
    data_size = lax.axis_size("dp")
    tensor_size = lax.axis_size("tensor")
    quarter = tokens // tensor_size
    experts = local_experts * data_size
    score_scale = head_dim ** (-0.5)
    row0 = lax.axis_index("tensor") * quarter

    def mine(array):
        return lax.dynamic_slice_in_dim(array, row0, quarter, 0)

    expert_ids = jnp.arange(experts, dtype=jnp.int32)
    dense = jnp.sum(
        jnp.where(mine(routes)[:, :, None] == expert_ids[None, None, :], mine(route_weights)[:, :, None], 0.0),
        axis=1,
    )
    dense_high = dense.astype(bf)
    dense_low = (dense - dense_high.astype(f32)).astype(bf)
    packed = jnp.concatenate([mine(out_grad), dense_high, dense_low], axis=1)
    gathered = lax.all_gather(packed, "dp", tiled=True)
    grads_all = gathered[:, :model_width]
    dense_all = gathered[:, model_width : model_width + experts].astype(f32) + gathered[
        :, model_width + experts :
    ].astype(f32)
    weight_all = lax.dynamic_slice_in_dim(
        dense_all, lax.axis_index("dp") * local_experts, local_experts, 1
    )
    rows = data_size * quarter
    units = local_experts * hidden_part
    own_weights = jnp.concatenate(
        [
            jnp.transpose(w_gate_up, (2, 0, 3, 1)).reshape(2, units, model_width),
            w_down.reshape(1, units, model_width),
        ],
        axis=0,
    )
    all_weights = lax.all_gather(own_weights, "tensor")
    weight_cols = jnp.broadcast_to(
        weight_all[:, None, :, None], (rows, tensor_size, local_experts, hidden_part)
    ).reshape(rows, tensor_size, units)

    hidden = hidden_in.astype(f32)
    hat_one, inv_one = rms_parts(hidden)
    normed = (hat_one * norm1_gain).astype(bf)
    query_proj = jnp.dot(normed, query_weight, preferred_element_type=f32).reshape(
        tokens, local_heads, head_dim
    )
    key_proj = jnp.dot(normed, key_weight, preferred_element_type=f32)
    value_low = jnp.dot(normed, value_weight, preferred_element_type=f32).astype(bf)
    places, starts = sequence_layout(seq_lens[0], tokens)
    cosine_table, sine_table = rotary_tables(places - starts, head_dim)
    query_hat, query_inv = rms_parts(query_proj)
    query_low = rotate(
        query_hat * query_gain, cosine_table[:, None, :], sine_table[:, None, :]
    ).astype(bf)
    key_hat, key_inv = rms_parts(key_proj)
    key_low = rotate(key_hat * key_gain, cosine_table, sine_table).astype(bf)
    visible = (places[None, :] <= places[:, None]) & (places[None, :] >= starts[:, None])
    scores = jnp.einsum("thd,sd->hts", query_low, key_low, preferred_element_type=f32) * score_scale
    exponent = jnp.where(visible[None], jnp.exp(scores), 0.0)
    totals = jnp.sum(exponent, axis=-1, keepdims=True)
    log_totals = jnp.log(totals)
    soft_low = (exponent / totals).astype(bf)
    mixed_low = (
        jnp.einsum("hts,sd->thd", soft_low, value_low, preferred_element_type=f32)
        .reshape(tokens, local_heads * head_dim)
        .astype(bf)
    )
    attention = lax.psum_scatter(
        jnp.dot(mixed_low, out_weight, preferred_element_type=f32).astype(bf), "tensor", tiled=True
    ).astype(f32)
    hidden_q = mine(hidden_in).astype(f32)
    hat_one_q, inv_one_q = rms_parts(hidden_q)
    middle = hidden_q + attention
    hat_two, inv_two = rms_parts(middle)
    normed_two = (hat_two * norm2_gain).astype(bf)
    inputs = lax.all_gather(normed_two, "dp", tiled=True)

    def project(left, which):
        return jnp.einsum("td,rud->tru", left, all_weights[:, which], preferred_element_type=f32)

    gate_act = project(inputs, 0)
    upward = project(inputs, 1)
    sigmoid_gate = jax.nn.sigmoid(gate_act)
    active = gate_act * sigmoid_gate * upward
    weighted_low = (weight_cols * active).astype(bf)
    mixture_part = jnp.einsum(
        "tru,rud->td", weighted_low, all_weights[:, 2], preferred_element_type=f32
    ).astype(bf)
    mixture = lax.psum_scatter(mixture_part, "dp", tiled=True).astype(f32)
    hidden_out = (middle + mixture).astype(bf)
    grad_active = weight_cols * project(grads_all, 2)
    grad_gate = (
        grad_active * upward * sigmoid_gate * (1.0 + gate_act * (1.0 - sigmoid_gate))
    ).astype(bf)
    grad_up = (grad_active * gate_act * sigmoid_gate).astype(bf)
    grad_normed_part = jnp.einsum(
        "tru,rud->td", grad_gate, all_weights[:, 0], preferred_element_type=f32
    ) + jnp.einsum("tru,rud->td", grad_up, all_weights[:, 1], preferred_element_type=f32)
    grad_normed_two = lax.psum_scatter(grad_normed_part.astype(bf), "dp", tiled=True).astype(f32)
    weight_grads = jnp.stack(
        [
            jnp.einsum("tru,td->rud", grad_gate, inputs, preferred_element_type=f32).astype(bf),
            jnp.einsum("tru,td->rud", grad_up, inputs, preferred_element_type=f32).astype(bf),
            jnp.einsum("tru,td->rud", weighted_low, grads_all, preferred_element_type=f32).astype(bf),
        ],
        axis=1,
    )
    own_grads = (
        lax.psum_scatter(weight_grads.reshape(-1, model_width), "tensor", tiled=True)
        .astype(f32)
        .reshape(3, units, model_width)
    )
    grad_w_gate_up = jnp.transpose(
        own_grads[:2].reshape(2, local_experts, hidden_part, model_width), (1, 3, 0, 2)
    )
    grad_w_down = own_grads[2].reshape(local_experts, hidden_part, model_width)

    grad_out = mine(out_grad).astype(f32)
    grad_gain_two = jnp.sum(grad_normed_two * hat_two, axis=0)
    grad_middle = grad_out + rms_back(grad_normed_two * norm2_gain, hat_two, inv_two)
    grad_mid_low = lax.all_gather(grad_middle.astype(bf), "tensor", tiled=True)
    grad_out_weight = jnp.einsum("ti,td->id", mixed_low, grad_mid_low, preferred_element_type=f32)
    grad_mixed = (
        jnp.einsum("td,id->ti", grad_mid_low, out_weight, preferred_element_type=f32)
        .astype(bf)
        .reshape(tokens, local_heads, head_dim)
    )
    scores_again = (
        jnp.einsum("thd,sd->hts", query_low, key_low, preferred_element_type=f32) * score_scale
    )
    soft_again = jnp.where(visible[None], jnp.exp(scores_again - log_totals), 0.0)
    grad_soft = jnp.einsum("thd,sd->hts", grad_mixed, value_low, preferred_element_type=f32)
    grad_scores = (
        soft_again * (grad_soft - jnp.sum(soft_again * grad_soft, axis=-1, keepdims=True))
    ).astype(bf)
    grad_values = jnp.einsum(
        "hts,thd->sd", soft_again.astype(bf), grad_mixed, preferred_element_type=f32
    ).astype(bf)
    grad_query_rot = score_scale * jnp.einsum(
        "hts,sd->thd", grad_scores, key_low, preferred_element_type=f32
    )
    grad_key_rot = score_scale * jnp.einsum(
        "hts,thd->sd", grad_scores, query_low, preferred_element_type=f32
    )
    grad_query_norm = rotate_back(grad_query_rot, cosine_table[:, None, :], sine_table[:, None, :])
    grad_query_gain = jnp.sum(grad_query_norm * query_hat, axis=(0, 1))
    grad_query_low = (
        rms_back(grad_query_norm * query_gain, query_hat, query_inv)
        .reshape(tokens, local_heads * head_dim)
        .astype(bf)
    )
    grad_key_norm = rotate_back(grad_key_rot, cosine_table, sine_table)
    grad_key_gain = jnp.sum(grad_key_norm * key_hat, axis=0)
    grad_key_low = rms_back(grad_key_norm * key_gain, key_hat, key_inv).astype(bf)
    grad_query_weight = jnp.einsum("ti,tj->ij", normed, grad_query_low, preferred_element_type=f32)
    grad_key_weight = jnp.einsum("ti,tj->ij", normed, grad_key_low, preferred_element_type=f32)
    grad_value_weight = jnp.einsum("ti,tj->ij", normed, grad_values, preferred_element_type=f32)
    grad_normed_one = jnp.einsum("tj,ij->ti", grad_query_low, query_weight, preferred_element_type=f32)
    grad_normed_one = grad_normed_one + jnp.einsum(
        "tj,ij->ti", grad_key_low, key_weight, preferred_element_type=f32
    )
    grad_normed_one = grad_normed_one + jnp.einsum(
        "tj,ij->ti", grad_values, value_weight, preferred_element_type=f32
    )
    grad_normed_one = lax.psum_scatter(grad_normed_one.astype(bf), "tensor", tiled=True).astype(f32)
    grad_gain_one = jnp.sum(grad_normed_one * hat_one_q, axis=0)
    grad_hidden = grad_middle + rms_back(grad_normed_one * norm1_gain, hat_one_q, inv_one_q)
    both = lax.all_gather(
        jnp.stack([hidden_out, grad_hidden.astype(bf)], axis=0), "tensor", axis=1, tiled=True
    )
    grad_out_sum = lax.psum(grad_out_weight.astype(bf), "dp").astype(f32)
    summed = (
        lax.psum(grad_query_weight.astype(bf), "dp").astype(f32),
        lax.psum(grad_key_weight.astype(bf), "dp").astype(f32),
        lax.psum(grad_value_weight.astype(bf), "dp").astype(f32),
    )
    gains = lax.psum(
        jnp.concatenate([grad_gain_one, grad_gain_two, grad_query_gain, grad_key_gain]),
        ("dp", "tensor"),
    )
    return (
        both[0],
        both[1],
        gains[:model_width],
        summed[0],
        summed[1],
        summed[2],
        gains[2 * model_width : 2 * model_width + head_dim],
        gains[2 * model_width + head_dim :],
        grad_out_sum,
        gains[model_width : 2 * model_width],
        grad_w_gate_up,
        grad_w_down,
    )


def solution(mesh):
    in_specs = (
        P("dp", None),
        P("dp", None),
        P(),
        P(None, "tensor"),
        P(None, "tensor"),
        P(None, "tensor"),
        P(),
        P(),
        P("tensor", None),
        P(),
        P("dp", None, None, "tensor"),
        P("dp", "tensor", None),
        P("dp", None),
        P("dp", None),
        P("dp", None),
    )
    out_specs = (
        P("dp", None),
        P("dp", None),
        P(),
        P(None, "tensor"),
        P(None, "tensor"),
        P(None, "tensor"),
        P(),
        P(),
        P("tensor", None),
        P(),
        P("dp", None, None, "tensor"),
        P("dp", "tensor", None),
    )
    return jax.shard_map(local, mesh=mesh, in_specs=in_specs, out_specs=out_specs, check_vma=False)
```

time: 2920 us -> 1140 us (0.39)
  waiting for transfers between devices: 2200 us -> 828 us
  local copies, waits for them, and re-layouts: 385 us -> 50.5 us
  other arithmetic: 107 us -> 50 us
    all_to_all x4 -> x0, waiting for transfers between devices: 1810 us -> none  [the longest x1 521 us: local(): lax.all_to_all(scatter_rows(normed_two[sources], model_width), 'dp', spli...]
    reduce_scatter x0 -> x5, waiting for transfers between devices: none -> 342 us  [the longest x1 136 us: local(): lax.psum_scatter(weight_grads.reshape(-1, model_width), 'tensor', tiled=T...]
    all_gather x0 -> x5, waiting for transfers between devices: none -> 264 us  [the longest x1 113 us: local(): all_weights = lax.all_gather(own_weights, 'tensor')]
    psum x4 -> x1, waiting for transfers between devices: 390 us -> 222 us  [local(): lax.psum(grad_query_weight.astype(bf), 'dp').astype(f32)]
    gather x3 -> x0, local copies, waits for them, and re-layouts: 119 us -> none  [the longest x1 42.8 us: local(): lax.all_to_all(expert_out, 'dp', split_axis=1, concat_axis=1, tiled=True)]
    reshape x5 -> x0, local copies, waits for them, and re-layouts: 84.4 us -> none  [the longest x2 42.1 us: scatter_rows(): return buffer.at[slot_index].set(source_rows).reshape(local_experts, data...]
    all_to_all x4 -> x0, local copies, waits for them, and re-layouts: 84.1 us -> none  [the longest x1 21 us: local(): lax.all_to_all(grad_inputs, 'dp', split_axis=1, concat_axis=1, tiled=True)]
    scatter x2 -> x0, local copies, waits for them, and re-layouts: 76.1 us -> none  [scatter_rows(): return buffer.at[slot_index].set(source_rows).reshape(local_experts, data...]
  transfers between devices with their start and end apart: 8 -> 11, of which waited for: 7 -> 11; matrix products, arithmetic and copies ran while one was open for 14% -> 10% of each run, Pallas kernels for 0% -> 0%
where the time goes in v1:
time: 1140 us
  waiting for transfers between devices  828 us (73%)
  matrix products  146 us (13%)
  local copies, waits for them, and re-layouts  50.5 us (4%)
  other arithmetic  50 us (4%)
  blocking collectives  43.3 us (4%)
  between operations  17 us (1%)
    psum x1, waiting for transfers between devices, local(): lax.psum(grad_query_weight.astype(bf), 'dp').astype(f32)  222 us
    reduce_scatter x1, waiting for transfers between devices, local(): lax.psum_scatter(weight_grads.reshape(-1, model_width), 'tensor', tiled=T...  136 us
    all_gather x1, waiting for transfers between devices, local(): all_weights = lax.all_gather(own_weights, 'tensor')  113 us
    reduce_scatter x1, waiting for transfers between devices, local(): mixture = lax.psum_scatter(mixture_part, 'dp', tiled=True).astype(f32)  90.9 us
    reduce_scatter x1, waiting for transfers between devices, local(): lax.psum_scatter(grad_normed_part.astype(bf), 'dp', tiled=True).astype(f32)  86.9 us
    all_gather x1, waiting for transfers between devices, local(): inputs = lax.all_gather(normed_two, 'dp', tiled=True)  63.2 us
    all_gather x1, waiting for transfers between devices, local(): gathered = lax.all_gather(packed, 'dp', tiled=True)  46.5 us
    psum x1, blocking collectives, local(): lax.psum(jnp.concatenate([grad_gain_one, grad_gain_two, grad_query_gain,...  43.3 us
  transfers between devices with their start and end apart: 11, of which 11 were waited for; matrix products, arithmetic and copies ran while one was open for 10% of the time, Pallas kernels for 0%

profile of v1, /device:TPU:0, one launch (start us, length us, event | category | flops | bytes accessed | tf_op | source)
XLA Modules:
  0.0 1135.7 jit_solution(16545600781011678941)
XLA Ops:
  10.0 2.6 fusion.15
  12.6 3.1 fusion.46
  15.7 2.4 fusion.93
  19.3 2.5 multiply_reduce_fusion.5
  24.2 1.9 fusion.30
  27.0 2.6 fusion.7
  29.6 2.4 fusion.31
  32.0 1.8 copy-done.2
  34.9 3.7 convolution_convert_fusion.2
  42.6 1.6 concatenate.27
  44.4 2.2 copy.174
  46.7 2.6 pad_maximum_fusion.1
  49.4 23.3 %reduce-scatter.6.cloned.1.call-done = bf16[128,2048]{1,0:T(8,128)(2,1)} async-done(((bf16[512,2048]{1,0:T(8,128)(2,1)}), bf16[128,2048]{1,0:T(8,128)(2,1)}) %reduce-scatter.6.cloned.1.call-update) | async-done | bytes 524304 | tf_op jit(solution)/shard_map/reduce_scatter | solution.py:154
  72.7 1.5 multiply_reduce_fusion.2
  74.2 2.2 multiply_convert_fusion.3
  76.5 46.5 %all-gather.7.cloned.1.call-done = bf16[1024,2080]{1,0:T(8,128)(2,1)} async-done(((bf16[128,2080]{1,0:T(8,128)(2,1)}), bf16[1024,2080]{1,0:T(8,128)(2,1)}) %all-gather.7.cloned.1.call-update) | async-done | bytes 4259856 | tf_op jit(solution)/shard_map/all_gather | solution.py:105
  125.3 2.0 broadcast_in_dim.55
  127.3 3.0 copy.173
  130.3 113.1 %all-gather.15.cloned.1.call-done = bf16[12,384,2048]{2,1,0:T(8,128)(2,1)} async-done(((bf16[3,384,2048]{2,1,0:T(8,128)(2,1)}), bf16[12,384,2048]{2,1,0:T(8,128)(2,1)}) %all-gather.15.cloned.1.call-update) | async-done | bytes 18874384 | tf_op jit(solution)/shard_map/all_gather | solution.py:122
  243.4 12.0 %fusion.12 = f32[1024,4,384]{2,0,1:T(8,128)} fusion(bf16[4,3,384,2048]{3,2,1,0:T(8,128)(2,1)} %bitcast.231, bf16[1024,2080]{1,0:T(8,128)(2,1)} %all-gather.7.cloned.1.call-done), kind=kOutput, calls=%fused_computation.30 | convolution fusion | flops 6442450944 | bytes 16777216 | tf_op jit(solution)/shard_map/td,rud->tru/dot_general | solution.py:165
  255.3 63.2 %all-gather.9.cloned.1.call-done = bf16[1024,2048]{1,0:T(8,128)(2,1)} async-done(((bf16[128,2048]{1,0:T(8,128)(2,1)}), bf16[1024,2048]{1,0:T(8,128)(2,1)}) %all-gather.9.cloned.1.call-update) | async-done | bytes 4194320 | tf_op jit(solution)/shard_map/all_gather | solution.py:162
  318.5 11.8 %fusion.9 = f32[1024,4,384]{2,0,1:T(8,128)} fusion(bf16[4,3,384,2048]{3,2,1,0:T(8,128)(2,1)} %bitcast.232, bf16[1024,2048]{1,0:T(8,128)(2,1)} %all-gather.9.cloned.1.call-done), kind=kOutput, calls=%fused_computation.27 | convolution fusion | flops 6442450944 | bytes 16777216 | tf_op jit(solution)/shard_map/td,rud->tru/dot_general | solution.py:165
  330.3 15.8 %multiply_convert_fusion.2 = (bf16[1024,4,384]{2,0,1:T(8,128)(2,1)}, bf16[1024,4,384]{2,0,1:T(8,128)(2,1)S(1)}, bf16[1024,4,384]{2,0,1:T(8,128)(2,1)}) fusion(f32[1024,4,384]{2,0,1:T(8,128)} %fusion.9, f32[1024,384]{1,0:T(8,128)S(1)} %copy-done.21, f32[1024,4,384]{2,0,1:T(8,128)} %fusion.12, bf16[4,3,384,2048]{3,2,1,0:T(8,128)(2,1)} %bitcast.233, ...), kind=kOutput, calls=%fused_computation.24 | convolution fusion | flops 6470762496 | bytes 34078720 | tf_op jit(solution)/shard_map/td,rud->tru/dot_general | solution.py:165
  346.1 10.0 fusion.8
  356.1 10.3 fusion.3
  366.5 86.9 %reduce-scatter.10.cloned.1.call-done = bf16[128,2048]{1,0:T(8,128)(2,1)} async-done(((bf16[1024,2048]{1,0:T(8,128)(2,1)}), bf16[128,2048]{1,0:T(8,128)(2,1)}) %reduce-scatter.10.cloned.1.call-update) | async-done | bytes 524304 | tf_op jit(solution)/shard_map/reduce_scatter | solution.py:185
  453.4 2.3 fusion.53
  456.3 2.6 fusion.89
  462.4 18.8 %all-gather.11.cloned.1.call-done = bf16[512,2048]{1,0:T(8,128)(2,1)} async-done(((bf16[128,2048]{1,0:T(8,128)(2,1)}), bf16[512,2048]{1,0:T(8,128)(2,1)}) %all-gather.11.cloned.1.call-update) | async-done | bytes 2097168 | tf_op jit(solution)/shard_map/all_gather | solution.py:207
  481.2 5.3 fusion.35
  486.6 5.1 fusion
  491.7 2.7 fusion.2
  494.4 1.8 multiply_bitcast_fusion
  496.2 2.6 fusion.39
  498.9 1.6 fusion.43
  501.5 3.2 fusion.64
  506.2 1.6 mul.456
  507.8 1.5 fusion.29
  510.0 2.4 fusion.101
  514.0 2.0 add_convert_fusion
  516.2 11.0 bitcast_convert_fusion
  528.8 1.8 convolution_convert_fusion.4
  530.6 1.8 convolution_convert_fusion.3
  532.4 4.4 convolution_convert_fusion
  536.8 4.5 convolution_convert_fusion.1
  542.0 5.4 reduce-scatter.12.cloned.1.call-done
  547.4 1.5 fusion.55
  548.9 90.9 %reduce-scatter.8.cloned.1.call-done = bf16[128,2048]{1,0:T(8,128)(2,1)} async-done(((bf16[1024,2048]{1,0:T(8,128)(2,1)}), bf16[128,2048]{1,0:T(8,128)(2,1)}) %reduce-scatter.8.cloned.1.call-update) | async-done | bytes 524304 | tf_op jit(solution)/shard_map/reduce_scatter | solution.py:175
  639.8 2.2 fusion.65
  643.4 9.8 convert_bitcast_fusion
  653.2 7.4 convert_bitcast_fusion.1
  660.6 7.4 convert_bitcast_fusion.2
  668.1 2.2 pad_maximum_fusion
  670.3 6.7 copy.190
  677.6 43.3 %psum.35 = f32[4352]{0:T(1024)S(1)} all-reduce(f32[4352]{0:T(1024)S(1)} %pad_maximum_fusion.8), channel_id=1, replica_groups=mesh['dp'=8,'tensor'=4] {'dp','tensor'}, use_global_device_ids=true, to_apply=%region_23.24 | all-reduce | flops 4352 | bytes 34816 | tf_op jit(solution)/shard_map/psum | solution.py:263
  722.1 221.7 %all-reduce.3.cloned.1.call-done = (bf16[2048,1024]{1,0:T(8,128)(2,1)}, bf16[2048,128]{1,0:T(8,128)(2,1)}, bf16[2048,128]{1,0:T(8,128)(2,1)}, bf16[1024,2048]{1,0:T(8,128)(2,1)}) async-done(((bf16[2048,1024]{1,0:T(8,128)(2,1)}, bf16[2048,128]{1,0:T(8,128)(2,1)}, bf16[2048,128]{1,0:T(8,128)(2,1)}, bf16[1024,2048]{1,0:T(8,128)(2,1)}), (bf16[2048,1024]{1,0:T(8,128)(2,1)}, bf16[2048,128]{1,0:T(8,128)(2,1)}, ...) | async-done | bytes 9437200 | tf_op jit(solution)/shard_map/psum | solution.py:259
  943.8 6.8 convert_element_type.187
  952.7 4.4 convert_element_type.193
  957.1 22.2 %all-gather.13.cloned.1.call-done = bf16[2,512,2048]{2,1,0:T(8,128)(2,1)} async-done(((bf16[2,128,2048]{2,1,0:T(8,128)(2,1)}), bf16[2,512,2048]{2,1,0:T(8,128)(2,1)}) %all-gather.13.cloned.1.call-update) | async-done | bytes 4194320 | tf_op jit(solution)/shard_map/all_gather | solution.py:254
  979.3 4.8 slice_bitcast_fusion.16
  984.1 135.6 %reduce-scatter.14.cloned.1.call-done = bf16[1152,2048]{1,0:T(8,128)(2,1)} async-done(((bf16[4608,2048]{1,0:T(8,128)(2,1)}), bf16[1152,2048]{1,0:T(8,128)(2,1)}) %reduce-scatter.14.cloned.1.call-update) | async-done | bytes 4718608 | tf_op jit(solution)/shard_map/reduce_scatter | solution.py:195
  1119.7 2.9 slice.113
  1122.7 3.1 copy.191
  1125.8 2.0 slice.114
  (214 shorter events, 30.3 us)
Async XLA Ops:
  8.0 11.3 copy-start
  8.0 7.7 copy-start.35
  8.0 64.6 %reduce-scatter.6.cloned.1.call-start = ((), (), s32[]{:S(2)}) async-start(), calls=%async_computation.5 | async-start | bytes 2621440 | tf_op jit(solution)/shard_map/reduce_scatter | solution.py:154
  8.1 14.6 %copy-start.51 = (f32[64]{0:T(128)}, f32[64]{0:T(128)S(1)}, u32[]{:S(2)}) copy-start(f32[64]{0:T(128)S(1)} %multiply_exponential_fusion) | copy-start | bytes 772
  8.9 6.8 copy-start.3
  8.9 6.8 copy-start.57
  10.0 12.7 %copy-start.40 = (f32[512]{0:T(512)}, f32[512]{0:T(512)S(1)}, u32[]{:S(2)}) copy-start(f32[512]{0:T(512)S(1)} %subtract_convert_fusion.2) | copy-start | bytes 6148
  12.6 6.7 copy-start.49
  18.6 4.0 copy-start.47
  24.0 2.9 copy-start.15
  24.2 2.7 copy-start.17
  26.9 2.7 copy-start.9
  26.9 2.7 copy-start.11
  27.0 2.7 copy-start.31
  29.6 4.3 copy-start.2
  29.6 4.3 copy-start.43
  29.6 5.3 copy-start.56
  38.6 84.3 %all-gather.7.cloned.1.call-start = ((), (), s32[]{:S(2)}) async-start(), calls=%async_computation.6 | async-start | bytes 5013504 | tf_op jit(solution)/shard_map/all_gather | solution.py:105
  44.3 199.1 %all-gather.15.cloned.1.call-start = ((), (), s32[]{:S(2)}) async-start(), calls=%async_computation.14 | async-start | bytes 23592960 | tf_op jit(solution)/shard_map/all_gather | solution.py:122
  44.3 2.4 copy-start.20
  49.3 24.8 %copy-start.33 = (f32[2048]{0:T(1024)S(1)}, f32[2048]{0:T(1024)}, u32[]{:S(2)}) copy-start(f32[2048]{0:T(1024)} %param.24) | copy-start | bytes 24580
  49.3 269.2 %all-gather.9.cloned.1.call-start = ((), (), s32[]{:S(2)}) async-start(), calls=%async_computation.7 | async-start | bytes 4718592 | tf_op jit(solution)/shard_map/all_gather | solution.py:162
  74.2 50.1 %copy-start.44 = (f32[128]{0:T(128)}, f32[128]{0:T(128)S(1)}, u32[]{:S(2)}) copy-start(f32[128]{0:T(128)S(1)} %add_rsqrt_fusion.4) | copy-start | bytes 1540
  76.4 377.0 %reduce-scatter.10.cloned.1.call-start = ((), (), s32[]{:S(2)}) async-start(), calls=%async_computation.9 | async-start | bytes 4718592 | tf_op jit(solution)/shard_map/reduce_scatter | solution.py:185
  318.5 11.8 %copy-start.21 = (f32[1024,384]{1,0:T(8,128)S(1)}, f32[1024,384]{1,0:T(8,128)}, u32[]{:S(2)}) copy-start(f32[1024,384]{1,0:T(8,128)} %copy.173) | copy-start | bytes 4718596
  346.1 10.0 copy-start.63
  346.1 10.0 copy-start.65
  366.4 87.0 %copy-start.5 = (bf16[128,2048]{1,0:T(8,128)(2,1)S(1)}, bf16[128,2048]{1,0:T(8,128)(2,1)}, u32[]{:S(2)}) copy-start(bf16[128,2048]{1,0:T(8,128)(2,1)} %reduce-scatter.6.cloned.1.call-done) | copy-start | bytes 1572868
  366.5 114.8 %all-gather.11.cloned.1.call-start = ((), (), s32[]{:S(2)}) async-start(), calls=%async_computation.10 | async-start | bytes 2621440 | tf_op jit(solution)/shard_map/all_gather | solution.py:207
  458.9 88.5 %reduce-scatter.12.cloned.1.call-start = ((), (), s32[]{:S(2)}) async-start(), calls=%async_computation.11 | async-start | bytes 2621440 | tf_op jit(solution)/shard_map/reduce_scatter | solution.py:251
  481.2 5.3 copy-start.30
  481.2 5.4 copy-start.32
  481.2 10.4 slice-start
  486.6 5.1 slice-start.1
  501.5 4.1 copy-start.22
  505.6 2.2 copy-start.6
  505.6 2.2 copy-start.42
  509.3 3.1 copy-start.23
  510.0 2.4 copy-start.19
  510.0 2.4 copy-start.41
  510.0 2.4 copy-start.52
  510.0 3.0 copy-start.14
  510.0 3.0 copy-start.38
  510.0 3.0 copy-start.48
  516.1 123.7 %reduce-scatter.8.cloned.1.call-start = ((), (), s32[]{:S(2)}) async-start(), calls=%async_computation.8 | async-start | bytes 4718592 | tf_op jit(solution)/shard_map/reduce_scatter | solution.py:175
  527.2 416.6 %all-reduce.3.cloned.1.call-start = ((), (), s32[]{:S(2)}) async-start(), calls=%async_computation.15 | async-start | bytes 18874368 | tf_op jit(solution)/shard_map/psum | solution.py:259
  528.8 3.7 copy-start.60
  528.8 3.7 copy-start.62
  532.4 4.4 copy-start.24
  541.3 98.5 %copy-start.7 = (bf16[128,2048]{1,0:T(8,128)(2,1)S(1)}, bf16[128,2048]{1,0:T(8,128)(2,1)}, u32[]{:S(2)}) copy-start(bf16[128,2048]{1,0:T(8,128)(2,1)} %reduce-scatter.10.cloned.1.call-done) | copy-start | bytes 1572868
  541.3 98.5 %copy-start.34 = (f32[2048]{0:T(1024)S(1)}, f32[2048]{0:T(1024)}, u32[]{:S(2)}) copy-start(f32[2048]{0:T(1024)} %param.24) | copy-start | bytes 24580
  541.3 98.5 %copy-start.45 = (f32[128]{0:T(128)S(1)}, f32[128]{0:T(128)}, u32[]{:S(2)}) copy-start(f32[128]{0:T(128)} %copy-done.44) | copy-start | bytes 1540
  541.3 98.5 %copy-start.54 = (f32[128]{0:T(128)S(1)}, f32[128]{0:T(128)}, u32[]{:S(2)}) copy-start(f32[128]{0:T(128)} %copy-done.53) | copy-start | bytes 1540
  541.3 438.0 %all-gather.13.cloned.1.call-start = ((), (), s32[]{:S(2)}) async-start(), calls=%async_computation.12 | async-start | bytes 5242880 | tf_op jit(solution)/shard_map/all_gather | solution.py:254
  643.1 476.6 %reduce-scatter.14.cloned.1.call-start = ((), (), s32[]{:S(2)}) async-start(), calls=%async_computation.13 | async-start | bytes 23592960 | tf_op jit(solution)/shard_map/reduce_scatter | solution.py:195
  643.4 9.8 copy-start.59
  643.4 9.8 copy-start.66
  653.2 7.4 copy-start.64
  943.8 6.8 copy-start.27
  943.8 7.8 copy-start.26
  943.8 8.9 copy-start.8
  1119.7 6.0 slice-start.2
  1122.6 3.2 slice-start.3
  1122.6 5.2 copy-start.1
  (18 other events, 22.5 us)
Sparse Core Ops, SparseCore 0:
  38.8 33.8 reduce-scatter.5
  459.1 22.1 all-gather.10
  516.2 31.1 reduce-scatter.11
  551.5 88.2 reduce-scatter.7
  645.2 298.5 all-reduce.2
  945.8 33.4 all-gather.12
  981.9 137.8 reduce-scatter.13
Sparse Core Ops, SparseCore 1:
  44.4 78.5 all-gather.6
  125.0 118.3 all-gather.14
  245.9 72.5 all-gather.8
  366.6 86.8 reduce-scatter.9

commit v2 on v1

--- a/solution.py
+++ b/solution.py
@@ -1,8 +1,11 @@
+import functools
 import math
 
 import jax
 import jax.numpy as jnp
 from jax import lax
+from jax.experimental import pallas as pl
+from jax.experimental.pallas import tpu as pltpu
 from jax.sharding import PartitionSpec as P
 
 EPSILON = 1e-06
@@ -58,6 +61,532 @@
     places = jnp.arange(token_count, dtype=jnp.int32)
     starts = jnp.sum(jnp.where(endings[None, :] <= places[:, None], lengths[None, :], 0), axis=1)
     return (places, starts)
+
+
+LANES = 128
+MESH = pl.DeviceIdType.MESH
+VMEM_LIMIT = 60 * 1024 * 1024
+
+
+def ring_place(index, size):
+    return jnp.where(index % 2 == 0, index // 2, size - (index + 1) // 2)
+
+
+def ring_index(place, size):
+    place = place % size
+    return jnp.where(place < size // 2, 2 * place, 2 * size - 1 - 2 * place)
+
+
+def tensor_peers():
+    own = lax.axis_index("tensor")
+    partner = own + 1 - 2 * (own % 2)
+    across = (own + 2) % 4
+    return own, partner, across
+
+
+def greet(devices):
+    barrier = pltpu.get_barrier_semaphore()
+    for device in devices:
+        pl.semaphore_signal(barrier, inc=1, device_id=device, device_id_type=MESH)
+    pl.semaphore_wait(barrier, len(devices))
+
+
+def push(source, target, sems, device):
+    return pltpu.make_async_remote_copy(
+        src_ref=source,
+        dst_ref=target,
+        send_sem=sems[0],
+        recv_sem=sems[1],
+        device_id=device,
+        device_id_type=MESH,
+    )
+
+
+class GatherRing:
+    def __init__(self, size, blocks, sems, key, parts=2):
+        self.size, self.blocks, self.sems, self.key, self.parts = size, blocks, sems, key, parts
+        self.place = ring_place(lax.axis_index("dp"), size)
+        self.sent = []
+        self.live = {}
+
+    def send(self, step):
+        size, half = self.size, self.blocks.shape[1] // 2
+        piece = half // self.parts
+        for part in range(self.parts):
+            for way in (0, 1):
+                sign = 1 - 2 * way
+                block = self.key(ring_index(self.place + size * 2 - sign * step, size))
+                rows = pl.ds(way * half + part * piece, piece)
+                ref = self.blocks.at[block, rows]
+                device = (ring_index(self.place + size + sign, size), lax.axis_index("tensor"))
+                copy = push(
+                    ref,
+                    ref,
+                    (self.sems.at[0, way, step, part], self.sems.at[1, way, step, part]),
+                    device,
+                )
+                if step > 0:
+                    self.live[step - 1, part, way].wait_recv()
+                copy.start()
+                self.live[step, part, way] = copy
+                self.sent.append(copy)
+
+    def step(self, step):
+        if step + 1 < self.size - 1:
+            self.send(step + 1)
+        else:
+            for part in range(self.parts):
+                for way in (0, 1):
+                    self.live[step, part, way].wait_recv()
+
+    def finish(self):
+        for copy in self.sent:
+            copy.wait_send()
+
+
+def row_loop(total, rows, body):
+    def run(index, carry):
+        body(pl.ds(pl.multiple_of(index * rows, rows), rows))
+        return carry
+
+    lax.fori_loop(0, total // rows, run, 0)
+
+
+def exchange_tokens_body(
+    size,
+    part_ref,
+    token_ref,
+    pack_ref,
+    gain_ref,
+    middle_ref,
+    inputs_ref,
+    packs_ref,
+    from_partner,
+    from_across,
+    joined,
+    ring_sems,
+    pack_sems,
+    side_sems,
+    local_sem,
+):
+    f32 = jnp.float32
+    dp = lax.axis_index("dp")
+    own, partner, across = tensor_peers()
+    far_partner = (partner + 2) % 4
+    quarter = token_ref.shape[0]
+    place = ring_place(dp, size)
+    neighbours = [(ring_index(place + 1, size), own), (ring_index(place + size - 1, size), own)]
+    greet(neighbours + [(dp, partner), (dp, across)])
+
+    def part_rows(index):
+        return pl.ds(pl.multiple_of(index * quarter, quarter), quarter)
+
+    def side(index):
+        return (side_sems.at[0, index], side_sems.at[1, index])
+
+    first = push(part_ref.at[part_rows(far_partner)], from_partner.at[1], side(0), (dp, partner))
+    second = push(part_ref.at[part_rows(partner)], from_partner.at[0], side(1), (dp, partner))
+    first.start()
+    second.start()
+    keep = pltpu.make_async_copy(pack_ref, packs_ref.at[dp], local_sem)
+    keep.start()
+    keep.wait()
+    packs = GatherRing(size, packs_ref, pack_sems, lambda index: index)
+    packs.send(0)
+    first.wait_recv()
+    base = across * quarter
+
+    def join(rows):
+        there = pl.ds(pl.multiple_of(base + rows.start, 16), rows.size)
+        joined[rows, :] = (
+            part_ref[there, :].astype(f32) + from_partner[1, rows, :].astype(f32)
+        ).astype(jnp.bfloat16)
+
+    row_loop(quarter, 16, join)
+    third = push(joined, from_across, side(2), (dp, across))
+    third.start()
+    packs.step(0)
+    second.wait_recv()
+    third.wait_recv()
+    mine = own * quarter
+
+    def norm(rows):
+        there = pl.ds(pl.multiple_of(mine + rows.start, 16), rows.size)
+        middle = (
+            token_ref[rows, :].astype(f32)
+            + part_ref[there, :].astype(f32)
+            + from_partner[0, rows, :].astype(f32)
+            + from_across[rows, :].astype(f32)
+        )
+        middle_ref[rows, :] = middle
+        inverse = lax.rsqrt(jnp.mean(middle * middle, axis=-1, keepdims=True) + EPSILON)
+        inputs_ref[dp, rows, :] = (middle * inverse * gain_ref[...]).astype(jnp.bfloat16)
+
+    row_loop(quarter, 16, norm)
+    tokens = GatherRing(size, inputs_ref, ring_sems, lambda index: index)
+    tokens.send(0)
+    for step in range(1, size - 1):
+        packs.step(step)
+        tokens.step(step - 1)
+    tokens.step(size - 2)
+    packs.finish()
+    tokens.finish()
+    first.wait_send()
+    second.wait_send()
+    third.wait_send()
+
+
+def exchange_tokens(size, partial, token_rows, packed, gain):
+    quarter, width = token_rows.shape
+    columns = packed.shape[1]
+    bf = jnp.bfloat16
+    vmem = pl.BlockSpec(memory_space=pltpu.VMEM)
+    dma = pltpu.SemaphoreType.DMA
+    return pl.pallas_call(
+        functools.partial(exchange_tokens_body, size),
+        out_shape=(
+            jax.ShapeDtypeStruct((quarter, width), jnp.float32),
+            jax.ShapeDtypeStruct((size, quarter, width), bf),
+            jax.ShapeDtypeStruct((size, quarter, columns), bf),
+        ),
+        in_specs=[vmem] * 4,
+        out_specs=(vmem,) * 3,
+        scratch_shapes=[
+            pltpu.VMEM((2, quarter, width), bf),
+            pltpu.VMEM((quarter, width), bf),
+            pltpu.VMEM((quarter, width), bf),
+            dma((2, 2, size - 1, 2)),
+            dma((2, 2, size - 1, 2)),
+            dma((2, 3)),
+            dma(()),
+        ],
+        compiler_params=pltpu.CompilerParams(
+            collective_id=0, has_side_effects=True, vmem_limit_bytes=VMEM_LIMIT
+        ),
+        name="exchange_tokens",
+    )(partial, token_rows, packed, gain.reshape(1, -1))
+
+
+def finish_sums_body(
+    size,
+    lead,
+    qkv_ref,
+    out_ref,
+    normed_ref,
+    middle_ref,
+    token_ref,
+    hidden_ref,
+    gain_ref,
+    gains_ref,
+    hidden_all,
+    grad_all,
+    query_out,
+    key_out,
+    value_out,
+    outer_out,
+    gains_out,
+    slots_a,
+    slots_b,
+    gather_a,
+    gather_b,
+    wide_a,
+    wide_b,
+    from_partner,
+    from_across,
+    joined,
+    totals,
+    pair_gains,
+    ring_gains,
+    sems_a,
+    sems_b,
+    ring_sems,
+    side_sems,
+    store_sems,
+    local_sems,
+):
+    f32, bf = jnp.float32, jnp.bfloat16
+    dp = lax.axis_index("dp")
+    own, partner, across = tensor_peers()
+    far_partner = (partner + 2) % 4
+    quarter, width = token_ref.shape
+    place = ring_place(dp, size)
+    forward = (ring_index(place + 1, size), own)
+    backward = (ring_index(place + size - 1, size), own)
+    ways = ((forward, 1), (backward, -1))
+    greet([forward, backward, (dp, partner), (dp, across)])
+    waits = []
+
+    def start(copy):
+        copy.start()
+        waits.append(copy)
+        return copy
+
+    sets = (
+        (qkv_ref, slots_a, gather_a, wide_a, sems_a),
+        (out_ref, slots_b, gather_b, wide_b, sems_b),
+    )
+
+    def block_of(ref, block, way):
+        rows = ref.shape[0] // size
+        cut = ref.shape[1] // 2
+        return (pl.ds(pl.multiple_of(block * rows, rows), rows), pl.ds(way * cut, cut))
+
+    def wrap(value):
+        return (value + 2 * size) % size
+
+    live = {}
+
+    def reduce_send(step):
+        for which, (ref, slots, _, _, sems) in enumerate(sets):
+            for way, (device, sign) in enumerate(ways):
+                if step == 0:
+                    source = ref.at[block_of(ref, wrap(place - sign), way)]
+                else:
+                    add_own(which, way, step - 1)
+                    source = slots.at[way, step - 1]
+                live[which, way, step] = start(
+                    push(
+                        source,
+                        slots.at[way, step],
+                        (sems.at[0, way, step], sems.at[1, way, step]),
+                        device,
+                    )
+                )
+
+    def add_own(which, way, step):
+        ref, slots, _, _, _ = sets[which]
+        live[which, way, step].wait_recv()
+        sign = ways[way][1]
+        rows, columns = block_of(ref, wrap(place - sign * (2 + step)), way)
+        base = rows.start
+
+        def add(inner):
+            there = pl.ds(pl.multiple_of(base + inner.start, 16), inner.size)
+            slots[way, step, inner, :] = (
+                slots[way, step, inner, :].astype(f32) + ref[there, columns].astype(f32)
+            ).astype(bf)
+
+        row_loop(ref.shape[0] // size, 16, add)
+
+    gather = {}
+
+    def gather_send(step):
+        for which, (ref, slots, blocks, _, sems) in enumerate(sets):
+            cut = ref.shape[1] // 2
+            for way, (device, sign) in enumerate(ways):
+                columns = pl.ds(way * cut, cut)
+                block = wrap(place - sign * step)
+                if step == 0:
+                    add_own(which, way, size - 2)
+                    source = slots.at[way, size - 2]
+                else:
+                    gather[which, way, step - 1].wait_recv()
+                    source = blocks.at[block, :, columns]
+                gather[which, way, step] = start(
+                    push(
+                        source,
+                        blocks.at[block, :, columns],
+                        (sems.at[0, way, size - 1 + step], sems.at[1, way, size - 1 + step]),
+                        device,
+                    )
+                )
+                store(which, way, block, source)
+
+    pending = {}
+
+    def store(which, way, block, source):
+        ref, _, _, wide, _ = sets[which]
+        rows_total = ref.shape[0] // size
+        cut = ref.shape[1] // 2
+        for copy in pending.pop((which, way), []):
+            copy.wait()
+
+        def widen(inner):
+            wide[way, inner, :] = source[inner, :].astype(f32)
+
+        row_loop(rows_total, 16, widen)
+        rows = pl.ds(pl.multiple_of(block * rows_total, rows_total), rows_total)
+        if which == 1:
+            targets = [(outer_out.at[rows, pl.ds(way * cut, cut)], 0, cut)]
+        elif way == 0:
+            targets = [(query_out.at[rows, pl.ds(0, cut)], 0, cut)]
+        else:
+            rest = lead - cut
+            tail = key_out.shape[1]
+            targets = [
+                (query_out.at[rows, pl.ds(cut, rest)], 0, rest),
+                (key_out.at[rows], rest, tail),
+                (value_out.at[rows], rest + tail, tail),
+            ]
+        copies = []
+        for index, (target, first, count) in enumerate(targets):
+            copy = pltpu.make_async_copy(
+                wide.at[way, :, pl.ds(first, count)], target, store_sems.at[which, way, index]
+            )
+            copy.start()
+            copies.append(copy)
+        pending[which, way] = copies
+
+    def part_rows(index):
+        return pl.ds(pl.multiple_of(index * quarter, quarter), quarter)
+
+    def side(index):
+        return (side_sems.at[0, index], side_sems.at[1, index])
+
+    reduce_send(0)
+    first = start(
+        push(normed_ref.at[part_rows(far_partner)], from_partner.at[1], side(0), (dp, partner))
+    )
+    second = start(
+        push(normed_ref.at[part_rows(partner)], from_partner.at[0], side(1), (dp, partner))
+    )
+    mine = part_rows(own)
+    spread = []
+    spread.append(start(push(hidden_ref, hidden_all.at[mine], side(3), (dp, across))))
+    spread.append(start(push(hidden_ref, hidden_all.at[mine], side(4), (dp, partner))))
+    keep = pltpu.make_async_copy(hidden_ref, hidden_all.at[mine], local_sems.at[0])
+    keep.start()
+    reduce_send(1)
+    first.wait_recv()
+    away = across * quarter
+
+    def join(rows):
+        there = pl.ds(pl.multiple_of(away + rows.start, 16), rows.size)
+        joined[rows, :] = (
+            normed_ref[there, :].astype(f32) + from_partner[1, rows, :].astype(f32)
+        ).astype(bf)
+
+    row_loop(quarter, 16, join)
+    third = start(push(joined, from_across, side(2), (dp, across)))
+    reduce_send(2)
+    second.wait_recv()
+    third.wait_recv()
+    home = own * quarter
+    totals[...] = jnp.zeros_like(totals)
+
+    def finish(rows):
+        there = pl.ds(pl.multiple_of(home + rows.start, 16), rows.size)
+        grads = (
+            normed_ref[there, :].astype(f32)
+            + from_partner[0, rows, :].astype(f32)
+            + from_across[rows, :].astype(f32)
+        )
+        hidden = token_ref[rows, :].astype(f32)
+        inverse = lax.rsqrt(jnp.mean(hidden * hidden, axis=-1, keepdims=True) + EPSILON)
+        hat = hidden * inverse
+        product = grads * hat
+        totals[:, :width] += jnp.sum(product.reshape(-1, 8, width), axis=0)
+        scaled = grads * gain_ref[...]
+        back = inverse * (scaled - hat * jnp.mean(scaled * hat, axis=-1, keepdims=True))
+        joined_grad = (middle_ref[rows, :] + back).astype(bf)
+        grad_all[there, :] = joined_grad
+
+    row_loop(quarter, 16, finish)
+    spread.append(start(push(grad_all.at[mine], grad_all.at[mine], side(5), (dp, across))))
+    spread.append(start(push(grad_all.at[mine], grad_all.at[mine], side(6), (dp, partner))))
+    pair_gains[0, :, :width] = jnp.sum(totals[:, :width], axis=0, keepdims=True)
+    pair_gains[0, :, width:] = gains_ref[...]
+    swap = start(push(pair_gains.at[0], pair_gains.at[1], side(7), (dp, partner)))
+    reduce_send(3)
+    far = part_rows(across)
+    spread[0].wait_recv()
+    spread.append(start(push(hidden_all.at[far], hidden_all.at[far], side(8), (dp, partner))))
+    spread[2].wait_recv()
+    spread.append(start(push(grad_all.at[far], grad_all.at[far], side(9), (dp, partner))))
+    swap.wait_recv()
+    pair_gains[2] = pair_gains[0] + pair_gains[1]
+    swap = start(push(pair_gains.at[2], pair_gains.at[3], side(10), (dp, across)))
+    for step in range(4, size - 1):
+        reduce_send(step)
+    swap.wait_recv()
+    ring_gains[place] = pair_gains[2] + pair_gains[3]
+    gather_send(0)
+    small = None
+    for step in range(size - 1):
+        if small is not None:
+            small.wait_recv()
+        ref = ring_gains.at[wrap(place - step)]
+        small = start(push(ref, ref, (ring_sems.at[0, step], ring_sems.at[1, step]), forward))
+        if step > 0:
+            gather_send(step)
+    small.wait_recv()
+    for which, (ref, _, blocks, _, _) in enumerate(sets):
+        cut = ref.shape[1] // 2
+        for way, (_, sign) in enumerate(ways):
+            gather[which, way, size - 2].wait_recv()
+            block = wrap(place - sign * (size - 1))
+            store(which, way, block, blocks.at[block, :, pl.ds(way * cut, cut)])
+    gains_out[...] = jnp.sum(ring_gains[...], axis=0)
+    for copies in pending.values():
+        for copy in copies:
+            copy.wait()
+    keep.wait()
+    for index in (1, 3, 4, 5):
+        spread[index].wait_recv()
+    for copy in waits:
+        copy.wait_send()
+
+
+def finish_sums(
+    size, grad_in, grad_out, grad_normed, grad_middle, token_rows, hidden_rows, gain, gains, head_dim
+):
+    bf, f32 = jnp.bfloat16, jnp.float32
+    quarter, width = token_rows.shape
+    tokens = grad_normed.shape[0]
+    lead = grad_in.shape[1] - 2 * head_dim
+    vmem = pl.BlockSpec(memory_space=pltpu.VMEM)
+    anywhere = pl.BlockSpec(memory_space=pl.ANY)
+    dma = pltpu.SemaphoreType.DMA
+    rows_a, rows_b = grad_in.shape[0] // size, grad_out.shape[0] // size
+    cut_a, cut_b = grad_in.shape[1] // 2, grad_out.shape[1] // 2
+    count = width + gains.shape[1]
+    return pl.pallas_call(
+        functools.partial(finish_sums_body, size, lead),
+        out_shape=(
+            jax.ShapeDtypeStruct((tokens, width), bf),
+            jax.ShapeDtypeStruct((tokens, width), bf),
+            jax.ShapeDtypeStruct((width, lead), f32),
+            jax.ShapeDtypeStruct((width, head_dim), f32),
+            jax.ShapeDtypeStruct((width, head_dim), f32),
+            jax.ShapeDtypeStruct(grad_out.shape, f32),
+            jax.ShapeDtypeStruct((1, count), f32),
+        ),
+        in_specs=[vmem] * 8,
+        out_specs=(vmem, vmem, anywhere, anywhere, anywhere, anywhere, vmem),
+        scratch_shapes=[
+            pltpu.VMEM((2, size - 1, rows_a, cut_a), bf),
+            pltpu.VMEM((2, size - 1, rows_b, cut_b), bf),
+            pltpu.VMEM((size, rows_a, 2 * cut_a), bf),
+            pltpu.VMEM((size, rows_b, 2 * cut_b), bf),
+            pltpu.VMEM((2, rows_a, cut_a), f32),
+            pltpu.VMEM((2, rows_b, cut_b), f32),
+            pltpu.VMEM((2, quarter, width), bf),
+            pltpu.VMEM((quarter, width), bf),
+            pltpu.VMEM((quarter, width), bf),
+            pltpu.VMEM((8, width), f32),
+            pltpu.VMEM((4, 1, count), f32),
+            pltpu.VMEM((size, 1, count), f32),
+            dma((2, 2, 2 * size - 2)),
+            dma((2, 2, 2 * size - 2)),
+            dma((2, size - 1)),
+            dma((2, 11)),
+            dma((2, 2, 3)),
+            dma((1,)),
+        ],
+        compiler_params=pltpu.CompilerParams(
+            collective_id=1, has_side_effects=True, vmem_limit_bytes=VMEM_LIMIT
+        ),
+        name="finish_sums",
+    )(
+        grad_in,
+        grad_out,
+        grad_normed,
+        grad_middle,
+        token_rows,
+        hidden_rows,
+        gain.reshape(1, -1),
+        gains,
+    )
 
 
 def local(
@@ -101,14 +630,9 @@
     )
     dense_high = dense.astype(bf)
     dense_low = (dense - dense_high.astype(f32)).astype(bf)
-    packed = jnp.concatenate([mine(out_grad), dense_high, dense_low], axis=1)
-    gathered = lax.all_gather(packed, "dp", tiled=True)
-    grads_all = gathered[:, :model_width]
-    dense_all = gathered[:, model_width : model_width + experts].astype(f32) + gathered[
-        :, model_width + experts :
-    ].astype(f32)
-    weight_all = lax.dynamic_slice_in_dim(
-        dense_all, lax.axis_index("dp") * local_experts, local_experts, 1
+    spare = -2 * experts % LANES
+    packed = jnp.concatenate(
+        [mine(out_grad), dense_high, dense_low, jnp.zeros((quarter, spare), bf)], axis=1
     )
     rows = data_size * quarter
     units = local_experts * hidden_part
@@ -120,10 +644,6 @@
         axis=0,
     )
     all_weights = lax.all_gather(own_weights, "tensor")
-    weight_cols = jnp.broadcast_to(
-        weight_all[:, None, :, None], (rows, tensor_size, local_experts, hidden_part)
-    ).reshape(rows, tensor_size, units)
-
     hidden = hidden_in.astype(f32)
     hat_one, inv_one = rms_parts(hidden)
     normed = (hat_one * norm1_gain).astype(bf)
@@ -151,15 +671,25 @@
         .reshape(tokens, local_heads * head_dim)
         .astype(bf)
     )
-    attention = lax.psum_scatter(
-        jnp.dot(mixed_low, out_weight, preferred_element_type=f32).astype(bf), "tensor", tiled=True
-    ).astype(f32)
-    hidden_q = mine(hidden_in).astype(f32)
-    hat_one_q, inv_one_q = rms_parts(hidden_q)
-    middle = hidden_q + attention
+    hidden_q = mine(hidden_in)
+    hat_one_q, inv_one_q = rms_parts(hidden_q.astype(f32))
+    partial = jnp.dot(mixed_low, out_weight, preferred_element_type=f32).astype(bf)
+    middle, inputs, gathered = exchange_tokens(
+        data_size, partial, hidden_q, packed, norm2_gain
+    )
+    inputs = inputs.reshape(rows, model_width)
+    gathered = gathered.reshape(rows, -1)
+    grads_all = gathered[:, :model_width]
+    dense_all = gathered[:, model_width : model_width + experts].astype(f32) + gathered[
+        :, model_width + experts : model_width + 2 * experts
+    ].astype(f32)
+    weight_all = lax.dynamic_slice_in_dim(
+        dense_all, lax.axis_index("dp") * local_experts, local_experts, 1
+    )
+    weight_cols = jnp.broadcast_to(
+        weight_all[:, None, :, None], (rows, tensor_size, local_experts, hidden_part)
+    ).reshape(rows, tensor_size, units)
     hat_two, inv_two = rms_parts(middle)
-    normed_two = (hat_two * norm2_gain).astype(bf)
-    inputs = lax.all_gather(normed_two, "dp", tiled=True)
 
     def project(left, which):
         return jnp.einsum("td,rud->tru", left, all_weights[:, which], preferred_element_type=f32)
@@ -238,9 +768,10 @@
     grad_key_norm = rotate_back(grad_key_rot, cosine_table, sine_table)
     grad_key_gain = jnp.sum(grad_key_norm * key_hat, axis=0)
     grad_key_low = rms_back(grad_key_norm * key_gain, key_hat, key_inv).astype(bf)
-    grad_query_weight = jnp.einsum("ti,tj->ij", normed, grad_query_low, preferred_element_type=f32)
-    grad_key_weight = jnp.einsum("ti,tj->ij", normed, grad_key_low, preferred_element_type=f32)
-    grad_value_weight = jnp.einsum("ti,tj->ij", normed, grad_values, preferred_element_type=f32)
+    grad_all_low = jnp.concatenate([grad_query_low, grad_key_low, grad_values], axis=1)
+    grad_in_weights = jnp.einsum(
+        "ti,tj->ij", normed, grad_all_low, preferred_element_type=f32
+    ).astype(bf)
     grad_normed_one = jnp.einsum("tj,ij->ti", grad_query_low, query_weight, preferred_element_type=f32)
     grad_normed_one = grad_normed_one + jnp.einsum(
         "tj,ij->ti", grad_key_low, key_weight, preferred_element_type=f32
@@ -248,32 +779,30 @@
     grad_normed_one = grad_normed_one + jnp.einsum(
         "tj,ij->ti", grad_values, value_weight, preferred_element_type=f32
     )
-    grad_normed_one = lax.psum_scatter(grad_normed_one.astype(bf), "tensor", tiled=True).astype(f32)
-    grad_gain_one = jnp.sum(grad_normed_one * hat_one_q, axis=0)
-    grad_hidden = grad_middle + rms_back(grad_normed_one * norm1_gain, hat_one_q, inv_one_q)
-    both = lax.all_gather(
-        jnp.stack([hidden_out, grad_hidden.astype(bf)], axis=0), "tensor", axis=1, tiled=True
-    )
-    grad_out_sum = lax.psum(grad_out_weight.astype(bf), "dp").astype(f32)
-    summed = (
-        lax.psum(grad_query_weight.astype(bf), "dp").astype(f32),
-        lax.psum(grad_key_weight.astype(bf), "dp").astype(f32),
-        lax.psum(grad_value_weight.astype(bf), "dp").astype(f32),
-    )
-    gains = lax.psum(
-        jnp.concatenate([grad_gain_one, grad_gain_two, grad_query_gain, grad_key_gain]),
-        ("dp", "tensor"),
-    )
+    gains = jnp.concatenate([grad_gain_two, grad_query_gain, grad_key_gain]).reshape(1, -1)
+    final = finish_sums(
+        data_size,
+        grad_in_weights,
+        grad_out_weight.astype(bf),
+        grad_normed_one.astype(bf),
+        grad_middle,
+        hidden_q,
+        hidden_out,
+        norm1_gain,
+        gains,
+        head_dim,
+    )
+    gains = final[6].reshape(-1)
     return (
-        both[0],
-        both[1],
+        final[0],
+        final[1],
         gains[:model_width],
-        summed[0],
-        summed[1],
-        summed[2],
+        final[2],
+        final[3],
+        final[4],
         gains[2 * model_width : 2 * model_width + head_dim],
         gains[2 * model_width + head_dim :],
-        grad_out_sum,
+        final[5],
         gains[model_width : 2 * model_width],
         grad_w_gate_up,
         grad_w_down,

time: 1140 us -> 734 us (0.64)
  waiting for transfers between devices: 828 us -> 155 us
  Pallas kernels: 0 us -> 324 us
  blocking collectives: 43.3 us -> 0 us
  other arithmetic: 50 us -> 24.7 us
    pallas_call x0 -> x2, Pallas kernels: none -> 324 us  [the longest x1 215 us: finish_sums(): pl.pallas_call(functools.partial(finish_sums_body, size, lead), out_shape...]
    psum x1 -> x0, waiting for transfers between devices: 222 us -> none  [local(): lax.psum(grad_query_weight.astype(bf), 'dp').astype(f32)]
    reduce_scatter x1, waiting for transfers between devices: 136 us -> 0.01 us  [local(): lax.psum_scatter(weight_grads.reshape(-1, model_width), 'tensor', tiled=T...]
    all_gather x3 -> x0, waiting for transfers between devices: 132 us -> none  [the longest x1 63.2 us: local(): inputs = lax.all_gather(normed_two, 'dp', tiled=True)]
    all_gather x1, waiting for transfers between devices: 113 us -> 0.01 us  [local(): all_weights = lax.all_gather(own_weights, 'tensor')]
    psum x1 -> x0, blocking collectives: 43.3 us -> none  [local(): lax.psum(jnp.concatenate([grad_gain_one, grad_gain_two, grad_query_gain,...]
    reduce_scatter x2 -> x0, waiting for transfers between devices: 28.8 us -> none  [the longest x1 23.3 us: local(): lax.psum_scatter(jnp.dot(mixed_low, out_weight, preferred_element_type=f3...]
    reduce_scatter x1, waiting for transfers between devices: 86.9 us -> 63.7 us  [local(): lax.psum_scatter(grad_normed_part.astype(bf), 'dp', tiled=True).astype(f32)]
  transfers between devices with their start and end apart: 11 -> 5, of which waited for: 11 -> 2; matrix products, arithmetic and copies ran while one was open for 10% -> 18% of each run, Pallas kernels for 0% -> 44%
where the time goes in v2:
time: 734 us; the launch traced here: 729 us
  Pallas kernels  324 us (44%)
  waiting for transfers between devices  155 us (21%)
  matrix products  151 us (21%)
  local copies, waits for them, and re-layouts  57.8 us (8%)
  other arithmetic  24.7 us (3%)
  between operations  15.4 us (2%)
    pallas_call x1, Pallas kernels, finish_sums(): pl.pallas_call(functools.partial(finish_sums_body, size, lead), out_shape...  215 us
    pallas_call x1, Pallas kernels, exchange_tokens(): pl.pallas_call(functools.partial(exchange_tokens_body, size), out_shape=(...  109 us
    reduce_scatter x1, waiting for transfers between devices, local(): mixture = lax.psum_scatter(mixture_part, 'dp', tiled=True).astype(f32)  91.6 us
    reduce_scatter x1, waiting for transfers between devices, local(): lax.psum_scatter(grad_normed_part.astype(bf), 'dp', tiled=True).astype(f32)  63.7 us
    dot_general x3, matrix products, project(): jnp.einsum('td,rud->tru', left, all_weights[:, which], preferred_element_...  38.9 us
    unnamed x166, local copies, waits for them, and re-layouts  32.3 us
  transfers between devices with their start and end apart: 5, of which 2 were waited for; matrix products, arithmetic and copies ran while one was open for 18% of the time, Pallas kernels for 44%

profile of v2, /device:TPU:0, one launch (start us, length us, event | category | flops | bytes accessed | tf_op | source)
XLA Modules:
  0.0 729.1 jit_solution(6518605092131058974)
XLA Ops:
  7.3 2.2 copy.184
  9.6 2.6 pad_maximum_fusion.1
  12.3 0.8 constant_dynamic-slice_fusion
  14.9 5.2 fusion.76
  21.3 2.9 multiply_reduce_fusion.5
  24.3 2.4 constant_dynamic-slice_fusion.2
  26.8 1.2 concatenate.30.pack_ref
  28.4 1.2 fusion.58
  29.7 3.4 fusion.42
  33.9 0.8 subtract_convert_fusion
  34.7 2.7 fusion.7
  37.5 2.4 fusion.27
  39.9 1.8 copy-done.3
  41.7 1.0 copy-done.57
  42.8 3.7 convolution_convert_fusion.2.part_ref
  46.5 109.4 %exchange_tokens.1 = (f32[128,2048]{1,0:T(8,128)}, bf16[8,128,2048]{2,1,0:T(8,128)(2,1)}, bf16[8,128,2176]{2,1,0:T(8,128)(2,1)}) custom-call(bf16[512,2048]{1,0:T(8,128)(2,1)} %convolution_convert_fusion.2.part_ref, bf16[128,2048]{1,0:T(8,128)(2,1)} %get-tuple-element.128.token_ref, bf16[128,2176]{1,0:T(8,128)(2,1)} %concatenate.30.pack_ref, f32[1,2048]{1,0:T(1,128)} %bitcast.226), custom_call_target="tpu_custom_call" | custom-call | tf_op jit(solution)/shard_map/exchange_tokens/pallas_call | solution.py:245
  155.8 1.3 fusion.80
  157.7 1.6 copy.183
  159.4 12.1 %fusion.9 = f32[1024,4,384]{2,0,1:T(8,128)} fusion(bf16[4,3,384,2048]{3,2,1,0:T(8,128)(2,1)} %bitcast.236, bf16[1024,2176]{1,0:T(8,128)(2,1)} %bitcast.228), kind=kOutput, calls=%fused_computation.28 | convolution fusion | flops 6442450944 | bytes 16777216 | tf_op jit(solution)/shard_map/td,rud->tru/dot_general | solution.py:695
  171.5 10.6 %fusion.13 = f32[1024,4,384]{2,0,1:T(8,128)} fusion(bf16[1024,2048,1]{1,0,2:T(8,128)(2,1)S(1)} %bitcast.243, bf16[4,3,384,2048]{3,2,1,0:T(8,128)(2,1)} %bitcast.237), kind=kOutput, calls=%fused_computation.32 | convolution fusion | flops 6442450944 | bytes 16777216 | tf_op jit(solution)/shard_map/td,rud->tru/dot_general | solution.py:695
  182.0 16.2 %multiply_convert_fusion = (bf16[1024,4,384]{2,0,1:T(8,128)(2,1)}, bf16[1024,4,384]{2,0,1:T(8,128)(2,1)}, bf16[1024,4,384]{2,0,1:T(8,128)(2,1)}) fusion(f32[1024,4,384]{2,0,1:T(8,128)} %fusion.13, f32[1024,384]{1,0:T(8,128)S(1)} %copy-done.27, f32[1024,4,384]{2,0,1:T(8,128)} %fusion.9, bf16[1024,2048,1]{1,0,2:T(8,128)(2,1)S(1)} %bitcast.244, ...), kind=kOutput, calls=%fused_computation.23 | convolution fusion | flops 6470762496 | bytes 34078720 | tf_op jit(solution)/shard_map/td,rud->tru/dot_general | solution.py:695
  198.2 9.9 %fusion.10 = f32[1024,2048,1]{1,0,2:T(8,128)S(1)} fusion(bf16[1024,4,384]{2,0,1:T(8,128)(2,1)} %get-tuple-element.100, bf16[4,3,384,2048]{3,2,1,0:T(8,128)(2,1)} %bitcast.239), kind=kOutput, calls=%fused_computation.29 | convolution fusion | flops 6442450944 | bytes 17825792 | tf_op jit(solution)/shard_map/tru,rud->td/dot_general | solution.py:714
  208.1 10.6 %fusion.3 = bf16[1024,2048]{1,0:T(8,128)(2,1)} fusion(f32[1024,2048,1]{1,0,2:T(8,128)S(1)} %fusion.10, bf16[1024,4,384]{2,0,1:T(8,128)(2,1)S(1)} %copy-done.64, bf16[4,3,384,2048]{3,2,1,0:T(8,128)(2,1)} %bitcast.240), kind=kOutput, calls=%fused_computation.8 | convolution fusion | flops 6446645248 | bytes 22020096 | tf_op jit(solution)/shard_map/tru,rud->td/dot_general | solution.py:712
  218.7 11.1 %bitcast_convert_fusion = bf16[1024,2048]{1,0:T(8,128)(2,1)} fusion(bf16[1024,4,384]{2,0,1:T(8,128)(2,1)} %get-tuple-element.98, bf16[4,3,384,2048]{3,2,1,0:T(8,128)(2,1)} %bitcast.241), kind=kOutput, calls=%fused_computation.1 | convolution fusion | flops 6444548096 | bytes 13631488 | tf_op jit(solution)/shard_map/tru,rud->td/dot_general | solution.py:702
  229.9 1.1 copy-done.6
  231.2 11.3 %convert_bitcast_fusion = bf16[4,1,384,2048]{3,2,0,1:T(8,128)(2,1)} fusion(bf16[1024,4,384]{2,0,1:T(8,128)(2,1)} %get-tuple-element.98, bf16[1024,2176]{1,0:T(8,128)(2,1)} %bitcast.229), kind=kOutput, calls=%fused_computation.20 | convolution fusion | flops 6445596672 | bytes 13631488 | tf_op jit(solution)/shard_map/tru,td->rud/dot_general | solution.py:720
  242.5 63.7 %reduce-scatter.4.cloned.1.call-done = bf16[128,2048]{1,0:T(8,128)(2,1)} async-done(((bf16[1024,2048]{1,0:T(8,128)(2,1)}), bf16[128,2048]{1,0:T(8,128)(2,1)}) %reduce-scatter.4.cloned.1.call-update) | async-done | bytes 524304 | tf_op jit(solution)/shard_map/reduce_scatter | solution.py:715
  306.2 91.6 %reduce-scatter.6.cloned.1.call-done = bf16[128,2048]{1,0:T(8,128)(2,1)} async-done(((bf16[1024,2048]{1,0:T(8,128)(2,1)}), bf16[128,2048]{1,0:T(8,128)(2,1)}) %reduce-scatter.6.cloned.1.call-update) | async-done | bytes 524304 | tf_op jit(solution)/shard_map/reduce_scatter | solution.py:705
  397.8 2.4 fusion.46
  400.2 2.5 fusion.78
  402.8 10.2 %convert_bitcast_fusion.1 = bf16[4,1,384,2048]{3,2,0,1:T(8,128)(2,1)S(1)} fusion(bf16[1024,4,384]{2,0,1:T(8,128)(2,1)} %get-tuple-element.100, bf16[1024,2048,1]{1,0,2:T(8,128)(2,1)} %bitcast.242), kind=kOutput, calls=%fused_computation.21 | convolution fusion | flops 6445596672 | bytes 13631488 | tf_op jit(solution)/shard_map/tru,td->rud/dot_general | solution.py:719
  413.0 7.4 %convert_bitcast_fusion.2 = bf16[4,1,384,2048]{3,2,0,1:T(8,128)(2,1)S(1)} fusion(bf16[1024,4,384]{2,0,1:T(8,128)(2,1)S(1)} %copy-done.65, bf16[1024,2048,1]{1,0,2:T(8,128)(2,1)S(1)} %bitcast.245), kind=kOutput, calls=%fused_computation.22 | convolution fusion | flops 6445596672 | bytes 13631488 | tf_op jit(solution)/shard_map/tru,td->rud/dot_general | solution.py:718
  420.5 2.2 pad_maximum_fusion
  422.6 6.7 copy.203
  430.2 5.2 convolution_convert_fusion.3
  436.1 7.7 %fusion = (f32[8,512]{1,0:T(8,128)S(1)}, f32[512,512,8]{1,0,2:T(8,128)S(1)}) fusion(f32[512,512,8]{1,0,2:T(8,128)} %copy-done.3, f32[8,512]{1,0:T(8,128)S(1)} %log.8, pred[512,512]{0,1:T(8,128)(4,1)S(1)} %copy-done.19, bf16[512,128,1]{1,0,2:T(8,128)(2,1)S(1)} %copy-done.38, bf16[512,8,128]{0,2,1:T(8,128)(2,1)S(1)} %bitcast.222), kind=kOutput, calls=%fused_computation.4 | convolution fusion | flops 547352576 | bytes 18251776 | tf_op jit(solution)/shard_map/thd,sd->hts/dot_general | solution.py:748
  443.8 1.0 slice-done
  444.8 2.5 slice-done.1
  447.2 2.9 fusion.2
  450.1 1.9 multiply_bitcast_fusion
  452.1 1.0 multiply_add_fusion
  453.1 1.2 copy-done.5
  454.3 2.8 fusion.48
  458.8 1.5 fusion.25
  461.6 1.3 fusion.35
  463.0 1.5 fusion.61
  466.5 4.4 convolution_convert_fusion.1.out_ref
  470.8 2.4 fusion.82
  473.6 1.5 fusion.39
  475.1 2.0 add_convert_fusion.normed_ref
  477.2 4.9 convolution_convert_fusion.qkv_ref
  482.1 214.8 %finish_sums.1 = (bf16[512,2048]{1,0:T(8,128)(2,1)}, bf16[512,2048]{1,0:T(8,128)(2,1)}, f32[2048,1024]{1,0:T(8,128)}, f32[2048,128]{1,0:T(8,128)}, f32[2048,128]...) custom-call(bf16[2048,1280]{1,0:T(8,128)(2,1)} %convolution_convert_fusion.qkv_ref, ...), custom_call_target="tpu_custom_call" | custom-call | tf_op jit(solution)/shard_map/finish_sums/pallas_call | solution.py:543
  696.9 1.2 slice_bitcast_fusion.16
  698.1 1.3 fusion.81
  699.4 2.9 slice.115
  702.3 3.6 copy.204
  706.0 2.0 slice.116
  708.0 1.3 copy.248
  709.9 1.3 copy.249
  711.2 0.9 slice-done.9
  712.1 4.3 copy.250
  716.4 1.0 copy.251
  717.4 1.0 copy.252
  718.7 3.4 copy.253
  (212 shorter events, 13.1 us)
Async XLA Ops:
  7.2 14.1 %copy-start = (bf16[2048,128]{1,0:T(8,128)(2,1)S(1)}, bf16[2048,128]{1,0:T(8,128)(2,1)}, u32[]{:S(2)}) copy-start(bf16[2048,128]{1,0:T(8,128)(2,1)} %param.19) | copy-start | bytes 1572868
  7.2 152.1 %all-gather.6.cloned.1.call-start = ((), (), s32[]{:S(2)}) async-start(), calls=%async_computation.7 | async-start | bytes 23592960 | tf_op jit(solution)/shard_map/all_gather | solution.py:646
  12.2 2.6 copy-start.46
  12.2 294.0 %reduce-scatter.4.cloned.1.call-start = ((), (), s32[]{:S(2)}) async-start(), calls=%async_computation.3 | async-start | bytes 4718592 | tf_op jit(solution)/shard_map/reduce_scatter | solution.py:715
  14.9 14.8 %copy-start.54 = (f32[512]{0:T(512)}, f32[512]{0:T(512)S(1)}, u32[]{:S(2)}) copy-start(f32[512]{0:T(512)S(1)} %add_rsqrt_fusion.2) | copy-start | bytes 6148
  20.1 13.0 %copy-start.4 = (f32[512,1024]{1,0:T(8,128)}, f32[512,1024]{1,0:T(8,128)S(1)}, u32[]{:S(2)}) copy-start(f32[512,1024]{1,0:T(8,128)S(1)} %fusion.76) | copy-start | bytes 6291460
  21.3 7.0 copy-start.48
  24.3 8.8 %copy-start.10 = (f32[512,128]{1,0:T(8,128)}, f32[512,128]{1,0:T(8,128)S(1)}, u32[]{:S(2)}) copy-start(f32[512,128]{1,0:T(8,128)S(1)} %copy.175) | copy-start | bytes 786436
  26.7 6.4 copy-start.50
  27.9 5.9 copy-start.52
  28.0 5.8 copy-start.40
  28.1 5.8 copy-start.42
  28.1 5.8 copy-start.35
  28.2 9.2 %copy-start.18 = (pred[512,512]{0,1:T(8,128)(4,1)}, pred[512,512]{0,1:T(8,128)(4,1)S(1)}, u32[]{:S(2)}) copy-start(pred[512,512]{0,1:T(8,128)(4,1)S(1)} %fusion.47) | copy-start | bytes 786436
  29.6 4.3 copy-start.20
  29.6 4.3 copy-start.22
  29.7 5.1 copy-start.31
  29.7 5.1 copy-start.33
  33.1 4.3 copy-start.37
  34.7 2.7 copy-start.12
  34.7 2.7 copy-start.14
  37.4 4.3 copy-start.3
  37.4 4.3 copy-start.44
  37.5 5.3 copy-start.57
  41.7 4.7 copy-start.62
  159.4 12.1 %copy-start.59 = (bf16[8,128,2048]{2,1,0:T(8,128)(2,1)S(1)}, bf16[8,128,2048]{2,1,0:T(8,128)(2,1)}, u32[]{:S(2)}) copy-start(bf16[8,128,2048]{2,1,0:T(8,128)(2,1)} %get-tuple-element.24) | copy-start | bytes 12582916
  171.5 10.6 %copy-start.27 = (f32[1024,384]{1,0:T(8,128)S(1)}, f32[1024,384]{1,0:T(8,128)}, u32[]{:S(2)}) copy-start(f32[1024,384]{1,0:T(8,128)} %copy.183) | copy-start | bytes 4718596
  198.2 9.9 %copy-start.64 = (bf16[1024,4,384]{2,0,1:T(8,128)(2,1)S(1)}, bf16[1024,4,384]{2,0,1:T(8,128)(2,1)}, u32[]{:S(2)}) copy-start(bf16[1024,4,384]{2,0,1:T(8,128)(2,1)} %get-tuple-element.99) | copy-start | bytes 9437188
  218.7 179.1 %reduce-scatter.6.cloned.1.call-start = ((), (), s32[]{:S(2)}) async-start(), calls=%async_computation.5 | async-start | bytes 4718592 | tf_op jit(solution)/shard_map/reduce_scatter | solution.py:705
  229.8 200.4 %all-gather.4.cloned.1.call-start = ((), (), s32[]{:S(2)}) async-start(), calls=%async_computation.4 | async-start | bytes 2621440 | tf_op jit(solution)/shard_map/all_gather | solution.py:737
  231.2 166.6 %copy-start.39 = (f32[2048]{0:T(1024)S(1)}, f32[2048]{0:T(1024)}, u32[]{:S(2)}) copy-start(f32[2048]{0:T(1024)} %param.24) | copy-start | bytes 24580
  402.7 296.7 %reduce-scatter.8.cloned.1.call-start = ((), (), s32[]{:S(2)}) async-start(), calls=%async_computation.6 | async-start | bytes 23592960 | tf_op jit(solution)/shard_map/reduce_scatter | solution.py:725
  402.8 10.2 %copy-start.60 = (bf16[8,128,2048]{2,1,0:T(8,128)(2,1)S(1)}, bf16[8,128,2048]{2,1,0:T(8,128)(2,1)}, u32[]{:S(2)}) copy-start(bf16[8,128,2048]{2,1,0:T(8,128)(2,1)} %get-tuple-element.24) | copy-start | bytes 12582916
  402.8 10.2 %copy-start.65 = (bf16[1024,4,384]{2,0,1:T(8,128)(2,1)S(1)}, bf16[1024,4,384]{2,0,1:T(8,128)(2,1)}, u32[]{:S(2)}) copy-start(bf16[1024,4,384]{2,0,1:T(8,128)(2,1)} %get-tuple-element.99) | copy-start | bytes 9437188
  402.8 17.6 %slice-start.10 = ((s8[6291456]{0:T(1024)(128)(4,1)}), s8[4194304]{0:T(1024)(128)(4,1)S(1)}, s32[]{:S(2)}) async-start(s8[6291456]{0:T(1024)(128)(4,1)} %bitcast.219), calls=%async_computation.18 | async-start | bytes 8388608
  413.0 7.4 %slice-start.11 = ((s8[6291456]{0:T(1024)(128)(4,1)}), s8[2097152]{0:T(1024)(128)(4,1)S(1)}, s32[]{:S(2)}) async-start(s8[6291456]{0:T(1024)(128)(4,1)} %bitcast.219), calls=%async_computation.19 | async-start | bytes 4194304
  430.2 5.9 copy-start.19
  430.2 5.9 copy-start.38
  436.0 7.7 %copy-start.8 = (bf16[512,1024]{0,1:T(8,128)(2,1)}, bf16[512,1024]{0,1:T(8,128)(2,1)S(1)}, u32[]{:S(2)}) copy-start(bf16[512,1024]{0,1:T(8,128)(2,1)S(1)} %copy.226) | copy-start | bytes 3145732
  436.0 8.7 %slice-start = ((s8[8388608]{0:T(1024)(128)(4,1)}), s8[4194304]{0:T(1024)(128)(4,1)S(1)}, s32[]{:S(2)}) async-start(s8[8388608]{0:T(1024)(128)(4,1)} %bitcast.203), calls=%async_computation.8 | async-start | bytes 8388608
  436.1 11.2 %slice-start.1 = ((s8[8388608]{0:T(1024)(128)(4,1)}), s8[4194304]{0:T(1024)(128)(4,1)S(1)}, s32[]{:S(2)}) async-start(s8[8388608]{0:T(1024)(128)(4,1)} %bitcast.203), calls=%async_computation.9 | async-start | bytes 8388608
  447.2 2.9 copy-start.32
  447.2 2.9 copy-start.34
  450.1 3.0 copy-start.1
  458.8 2.8 copy-start.15
  460.3 2.6 copy-start.43
  460.3 4.1 copy-start.11
  460.4 4.1 copy-start.41
  460.4 4.1 copy-start.49
  463.0 3.4 copy-start.61
  463.0 3.4 copy-start.63
  466.4 4.4 copy-start.58
  466.5 6.7 slice-start.2
  470.8 2.7 copy-start.9
  699.4 6.5 slice-start.4
  702.3 3.7 slice-start.5
  702.3 5.7 copy-start.25
  702.3 8.9 %slice-start.8 = ((s8[8388608]{0:T(1024)(128)(4,1)}), s8[4194304]{0:T(1024)(128)(4,1)S(1)}, s32[]{:S(2)}) async-start(s8[8388608]{0:T(1024)(128)(4,1)} %bitcast.214), calls=%async_computation.16 | async-start | bytes 8388608
  706.0 3.9 copy-start.24
  706.0 6.2 slice-start.9
  709.9 8.5 %slice-start.6 = ((s8[8388608]{0:T(1024)(128)(4,1)}), s8[4194304]{0:T(1024)(128)(4,1)S(1)}, s32[]{:S(2)}) async-start(s8[8388608]{0:T(1024)(128)(4,1)} %bitcast.212), calls=%async_computation.14 | async-start | bytes 8388608
  712.1 4.3 copy-start.29
  712.1 5.2 copy-start.28
  712.1 6.6 slice-start.7
  (19 other events, 35.2 us)
Sparse Core Ops, SparseCore 0:
  12.3 133.9 all-gather.5
  218.8 87.3 reduce-scatter.3
  309.8 87.9 reduce-scatter.5
  402.9 22.1 all-gather.3
  429.5 171.5 reduce-scatter.7

commit v3 on v2

--- a/solution.py
+++ b/solution.py
@@ -102,9 +102,18 @@
     )
 
 
+def slot_of(delta, size):
+    delta = (delta + size // 2 - 1) % size - (size // 2 - 1)
+    if delta == 0:
+        return size - 1
+    if delta == size // 2:
+        return size - 2
+    return 2 * delta - 1 if delta > 0 else -2 * delta - 2
+
+
 class GatherRing:
-    def __init__(self, size, blocks, sems, key, parts=2):
-        self.size, self.blocks, self.sems, self.key, self.parts = size, blocks, sems, key, parts
+    def __init__(self, size, blocks, sems, parts=2):
+        self.size, self.blocks, self.sems, self.parts = size, blocks, sems, parts
         self.place = ring_place(lax.axis_index("dp"), size)
         self.sent = []
         self.live = {}
@@ -115,13 +124,13 @@
         for part in range(self.parts):
             for way in (0, 1):
                 sign = 1 - 2 * way
-                block = self.key(ring_index(self.place + size * 2 - sign * step, size))
                 rows = pl.ds(way * half + part * piece, piece)
-                ref = self.blocks.at[block, rows]
+                source = self.blocks.at[slot_of(-sign * step, size), rows]
+                target = self.blocks.at[slot_of(-sign * (step + 1), size), rows]
                 device = (ring_index(self.place + size + sign, size), lax.axis_index("tensor"))
                 copy = push(
-                    ref,
-                    ref,
+                    source,
+                    target,
                     (self.sems.at[0, way, step, part], self.sems.at[1, way, step, part]),
                     device,
                 )
@@ -188,10 +197,10 @@
     second = push(part_ref.at[part_rows(partner)], from_partner.at[0], side(1), (dp, partner))
     first.start()
     second.start()
-    keep = pltpu.make_async_copy(pack_ref, packs_ref.at[dp], local_sem)
+    keep = pltpu.make_async_copy(pack_ref, packs_ref.at[size - 1], local_sem)
     keep.start()
     keep.wait()
-    packs = GatherRing(size, packs_ref, pack_sems, lambda index: index)
+    packs = GatherRing(size, packs_ref, pack_sems)
     packs.send(0)
     first.wait_recv()
     base = across * quarter
@@ -220,10 +229,10 @@
         )
         middle_ref[rows, :] = middle
         inverse = lax.rsqrt(jnp.mean(middle * middle, axis=-1, keepdims=True) + EPSILON)
-        inputs_ref[dp, rows, :] = (middle * inverse * gain_ref[...]).astype(jnp.bfloat16)
+        inputs_ref[size - 1, rows, :] = (middle * inverse * gain_ref[...]).astype(jnp.bfloat16)
 
     row_loop(quarter, 16, norm)
-    tokens = GatherRing(size, inputs_ref, ring_sems, lambda index: index)
+    tokens = GatherRing(size, inputs_ref, ring_sems)
     tokens.send(0)
     for step in range(1, size - 1):
         packs.step(step)
@@ -267,30 +276,334 @@
     )(partial, token_rows, packed, gain.reshape(1, -1))
 
 
+def matmul_nt(left, right):
+    return lax.dot_general(left, right, (((1,), (1,)), ((), ())), preferred_element_type=jnp.float32)
+
+
+def matmul(left, right):
+    return lax.dot_general(left, right, (((1,), (0,)), ((), ())), preferred_element_type=jnp.float32)
+
+
+def run_experts_body(
+    size,
+    local_experts,
+    experts,
+    inputs_ref,
+    packs_ref,
+    weights_ref,
+    member_ref,
+    middle_ref,
+    gain_ref,
+    mix_ref,
+    wgrad_ref,
+    gmid_ref,
+    gmid_all,
+    gain_out,
+    weights,
+    hidden,
+    parts,
+    slots,
+    turned,
+    stage,
+    totals,
+    load_sems,
+    ring_sems,
+    side_sems,
+    store_sems,
+):
+    f32, bf = jnp.float32, jnp.bfloat16
+    dp = lax.axis_index("dp")
+    own, partner, across = tensor_peers()
+    width = inputs_ref.shape[1]
+    quarter = inputs_ref.shape[0] // size
+    pair = 2 * quarter
+    half = size // 2
+    units = weights.shape[1]
+    members = weights_ref.shape[0]
+    span = units // members
+    cut = width // 2
+    wide = 512
+    place = ring_place(dp, size)
+    forward = (ring_index(place + 1, size), own)
+    backward = (ring_index(place + size - 1, size), own)
+    greet([forward, backward, (dp, partner), (dp, across)])
+    pieces = units // LANES
+    each = pieces // members
+
+    def load(piece):
+        source = weights_ref.at[piece // each, :, pl.ds((piece % each) * LANES, LANES), :]
+        target = weights.at[:, pl.ds(piece * LANES, LANES), :]
+        return pltpu.make_async_copy(source, target, load_sems.at[piece])
+
+    for piece in range(pieces):
+        load(piece).start()
+
+    def ring_copy(way, step, source):
+        device = forward if way == 0 else backward
+        return push(
+            source, slots.at[way, step], (ring_sems.at[0, way, step], ring_sems.at[1, way, step]), device
+        )
+
+    def columns_of(way):
+        return pl.ds(way * cut, cut)
+
+    def ring_step(step, blocks, first=False):
+        for way in (0, 1):
+            if first:
+                source = parts.at[blocks[way], :, columns_of(way)]
+            else:
+                source = slots.at[way, step - 1]
+                ring_copy(way, step - 1, source).wait_recv()
+
+                def add(rows):
+                    slots[way, step - 1, rows, :] = (
+                        slots[way, step - 1, rows, :].astype(f32)
+                        + parts[blocks[way], rows, columns_of(way)].astype(f32)
+                    ).astype(bf)
+
+                row_loop(quarter, 16, add)
+            ring_copy(way, step, source).start()
+
+    def do_pair(index, carry):
+        rows = pl.ds(pl.multiple_of(index * pair, pair), pair)
+        tail = packs_ref[rows, width:].astype(f32)
+        lane = lax.broadcasted_iota(jnp.int32, tail.shape, 1)
+        shares = []
+        for expert in range(local_experts):
+            name = dp * local_experts + expert
+            picked = (lane == name) | (lane == experts + name)
+            shares.append(jnp.sum(jnp.where(picked, tail, 0.0), axis=1, keepdims=True))
+
+        def do_units(tile, carry):
+            here = pl.ds(pl.multiple_of(tile * wide, wide), wide)
+
+            @pl.when(index == 0)
+            def _():
+                for piece in range(wide // LANES):
+                    load(tile * (wide // LANES) + piece).wait()
+
+            scale = shares[0] * member_ref[0:1, here]
+            for expert in range(1, local_experts):
+                scale = scale + shares[expert] * member_ref[expert : expert + 1, here]
+            tokens = inputs_ref[rows, :]
+            gate = matmul_nt(tokens, weights[0, here, :])
+            upward = matmul_nt(tokens, weights[1, here, :])
+            grads = scale * matmul_nt(packs_ref[rows, :width], weights[2, here, :])
+            share = jax.nn.sigmoid(gate)
+            silu = gate * share
+            hidden[0, rows, here] = (grads * upward * share * (1.0 + gate * (1.0 - share))).astype(bf)
+            hidden[1, rows, here] = (grads * silu).astype(bf)
+            hidden[2, rows, here] = (scale * silu * upward).astype(bf)
+            return carry
+
+        lax.fori_loop(0, units // wide, do_units, 0)
+
+        def do_columns(tile, carry):
+            here = pl.ds(pl.multiple_of(tile * wide, wide), wide)
+            sums = matmul(hidden[0, rows, :], weights[0, :, here]) + matmul(
+                hidden[1, rows, :], weights[1, :, here]
+            )
+            low = sums.astype(bf)
+            parts[2 * index, :, here] = low[:quarter]
+            parts[2 * index + 1, :, here] = low[quarter:]
+            return carry
+
+        lax.fori_loop(0, width // wide, do_columns, 0)
+
+        @pl.when(index == 0)
+        def _():
+            ring_step(0, (0, 1), first=True)
+
+        @pl.when(index > 0)
+        def _():
+            ring_step(index, (2 * index, 2 * index + 1 - index // (half - 1)))
+
+        return carry
+
+    lax.fori_loop(0, half, do_pair, 0)
+
+    def mix_pairs(first, last):
+        def run(index, carry):
+            rows = pl.ds(pl.multiple_of(index * pair, pair), pair)
+            left = ring_index(place + size - 1 - index, size)
+            right = ring_index(place + (index + 1) % half, size)
+
+            def do_columns(tile, carry):
+                here = pl.ds(pl.multiple_of(tile * wide, wide), wide)
+                low = matmul(hidden[2, rows, :], weights[2, :, here]).astype(bf)
+                mix_ref[left, :, here] = low[:quarter]
+                mix_ref[right, :, here] = low[quarter:]
+                return carry
+
+            lax.fori_loop(0, width // wide, do_columns, 0)
+            return carry
+
+        lax.fori_loop(first, last, run, 0)
+
+    def store(kind, member, slot):
+        return pltpu.make_async_copy(stage.at[slot], wgrad_ref.at[member, kind], store_sems.at[slot])
+
+    def weight_grads(first, last):
+        def run(index, carry):
+            kind = index // members
+            member = index % members
+            slot = index % 2
+
+            @pl.when(index >= 2)
+            def _():
+                store(kind, member, slot).wait()
+
+            rows = pl.ds(pl.multiple_of(member * span, span), span)
+            for chunk in range(half):
+                some = pl.ds(chunk * pair, pair)
+                turned[:, some] = hidden[kind, some, rows].T
+
+            def do_columns(tile, carry):
+                here = pl.ds(pl.multiple_of(tile * wide, wide), wide)
+                source = inputs_ref if first < 2 * members else packs_ref
+                stage[slot, :, here] = matmul(turned[...], source[:, here]).astype(bf)
+                return carry
+
+            lax.fori_loop(0, width // wide, do_columns, 0)
+            store(kind, member, slot).start()
+            return carry
+
+        lax.fori_loop(first, last, run, 0)
+
+    def final_sum():
+        totals[...] = jnp.zeros_like(totals)
+        for way in (0, 1):
+            ring_copy(way, size - 2, slots.at[way, size - 2]).wait_recv()
+        base = own * quarter
+
+        def finish(rows):
+            sums = jnp.concatenate(
+                [slots[0, size - 2, rows, :].astype(f32), slots[1, size - 2, rows, :].astype(f32)],
+                axis=-1,
+            ) + parts[size - 1, rows, :].astype(f32)
+            middle = middle_ref[rows, :]
+            inverse = lax.rsqrt(jnp.mean(middle * middle, axis=-1, keepdims=True) + EPSILON)
+            hat = middle * inverse
+            product = sums * hat
+            totals[...] += product[:8] + product[8:]
+            scaled = sums * gain_ref[...]
+            back = inverse * (scaled - hat * jnp.mean(scaled * hat, axis=-1, keepdims=True))
+            above = packs_ref[
+                pl.ds(pl.multiple_of((size - 1) * quarter + rows.start, 16), rows.size), :width
+            ]
+            grad = above.astype(f32) + back
+            gmid_ref[rows, :] = grad
+            gmid_all[pl.ds(pl.multiple_of(base + rows.start, 16), rows.size), :] = grad.astype(bf)
+
+        row_loop(quarter, 16, finish)
+        gain_out[...] = jnp.sum(totals[...], axis=0, keepdims=True)
+
+    def rows_of(index):
+        return pl.ds(pl.multiple_of(index * quarter, quarter), quarter)
+
+    def spread(index, whose, device):
+        ref = gmid_all.at[rows_of(whose)]
+        return push(ref, ref, (side_sems.at[0, index], side_sems.at[1, index]), device)
+
+    def first_spread():
+        spread(0, own, (dp, across)).start()
+        spread(1, own, (dp, partner)).start()
+
+    def second_spread():
+        spread(0, own, (dp, across)).wait_recv()
+        spread(2, across, (dp, partner)).start()
+
+    events = []
+    for step in range(half, size - 1):
+        delta = -(1 + step)
+        blocks = (slot_of(delta, size), slot_of(-delta, size))
+        events.append(functools.partial(ring_step, step, blocks))
+
+    def closing():
+        final_sum()
+        first_spread()
+
+    events.append(closing)
+    events.append(second_spread)
+    work = [functools.partial(mix_pairs, 0, half // 2), functools.partial(mix_pairs, half // 2, half)]
+    for first in range(0, 3 * members, 2):
+        work.append(functools.partial(weight_grads, first, first + 2))
+    done = 0
+    for number, piece in enumerate(work):
+        piece()
+        upto = min(len(events), -(-(number + 1) * len(events) // (len(work) - 2)))
+        while done < upto:
+            events[done]()
+            done += 1
+    for slot in (0, 1):
+        store(0, 0, slot).wait()
+    spread(1, own, (dp, partner)).wait_recv()
+    spread(2, across, (dp, partner)).wait_recv()
+    for index, device in ((0, across), (1, partner), (2, partner)):
+        spread(index, own, (dp, device)).wait_send()
+    for way in (0, 1):
+        for step in range(size - 1):
+            ring_copy(way, step, slots.at[way, step]).wait_send()
+
+
+def run_experts(size, inputs, packs, weights, middle, gain, experts):
+    bf, f32 = jnp.bfloat16, jnp.float32
+    members, _, span, width = weights.shape
+    local_experts = experts // size
+    rows = inputs.shape[0]
+    quarter = rows // size
+    units = members * span
+    expert_of = (jnp.arange(units, dtype=jnp.int32) // (span // local_experts)) % local_experts
+    member = (expert_of[None, :] == jnp.arange(local_experts, dtype=jnp.int32)[:, None]).astype(f32)
+    vmem = pl.BlockSpec(memory_space=pltpu.VMEM)
+    anywhere = pl.BlockSpec(memory_space=pl.ANY)
+    dma = pltpu.SemaphoreType.DMA
+    return pl.pallas_call(
+        functools.partial(run_experts_body, size, local_experts, experts),
+        out_shape=(
+            jax.ShapeDtypeStruct((size, quarter, width), bf),
+            jax.ShapeDtypeStruct((members, 3, span, width), bf),
+            jax.ShapeDtypeStruct((quarter, width), f32),
+            jax.ShapeDtypeStruct((members * quarter, width), bf),
+            jax.ShapeDtypeStruct((1, width), f32),
+        ),
+        in_specs=[vmem, vmem, anywhere, vmem, vmem, vmem],
+        out_specs=(vmem, anywhere, vmem, vmem, vmem),
+        scratch_shapes=[
+            pltpu.VMEM((3, units, width), bf),
+            pltpu.VMEM((3, rows, units), bf),
+            pltpu.VMEM((size, quarter, width), bf),
+            pltpu.VMEM((2, size - 1, quarter, width // 2), bf),
+            pltpu.VMEM((span, rows), bf),
+            pltpu.VMEM((2, span, width), bf),
+            pltpu.VMEM((8, width), f32),
+            dma((units // LANES,)),
+            dma((2, 2, size - 1)),
+            dma((2, 3)),
+            dma((2,)),
+        ],
+        compiler_params=pltpu.CompilerParams(
+            collective_id=2, has_side_effects=True, vmem_limit_bytes=VMEM_LIMIT
+        ),
+        name="run_experts",
+    )(inputs, packs, weights, member, middle, gain.reshape(1, -1))
+
+
 def finish_sums_body(
     size,
-    lead,
     qkv_ref,
     out_ref,
     normed_ref,
     middle_ref,
     token_ref,
-    hidden_ref,
     gain_ref,
     gains_ref,
-    hidden_all,
     grad_all,
-    query_out,
-    key_out,
-    value_out,
-    outer_out,
+    gather_a,
+    gather_b,
     gains_out,
     slots_a,
     slots_b,
-    gather_a,
-    gather_b,
-    wide_a,
-    wide_b,
     from_partner,
     from_across,
     joined,
@@ -301,8 +614,6 @@
     sems_b,
     ring_sems,
     side_sems,
-    store_sems,
-    local_sems,
 ):
     f32, bf = jnp.float32, jnp.bfloat16
     dp = lax.axis_index("dp")
@@ -322,8 +633,8 @@
         return copy
 
     sets = (
-        (qkv_ref, slots_a, gather_a, wide_a, sems_a),
-        (out_ref, slots_b, gather_b, wide_b, sems_b),
+        (qkv_ref, slots_a, gather_a, sems_a),
+        (out_ref, slots_b, gather_b, sems_b),
     )
 
     def block_of(ref, block, way):
@@ -337,7 +648,7 @@
     live = {}
 
     def reduce_send(step):
-        for which, (ref, slots, _, _, sems) in enumerate(sets):
+        for which, (ref, slots, _, sems) in enumerate(sets):
             for way, (device, sign) in enumerate(ways):
                 if step == 0:
                     source = ref.at[block_of(ref, wrap(place - sign), way)]
@@ -354,7 +665,7 @@
                 )
 
     def add_own(which, way, step):
-        ref, slots, _, _, _ = sets[which]
+        ref, slots, blocks, _ = sets[which]
         live[which, way, step].wait_recv()
         sign = ways[way][1]
         rows, columns = block_of(ref, wrap(place - sign * (2 + step)), way)
@@ -362,70 +673,33 @@
 
         def add(inner):
             there = pl.ds(pl.multiple_of(base + inner.start, 16), inner.size)
-            slots[way, step, inner, :] = (
-                slots[way, step, inner, :].astype(f32) + ref[there, columns].astype(f32)
-            ).astype(bf)
+            sums = (slots[way, step, inner, :].astype(f32) + ref[there, columns].astype(f32)).astype(bf)
+            if step == size - 2:
+                blocks[place, inner, columns] = sums
+            else:
+                slots[way, step, inner, :] = sums
 
         row_loop(ref.shape[0] // size, 16, add)
 
     gather = {}
 
     def gather_send(step):
-        for which, (ref, slots, blocks, _, sems) in enumerate(sets):
+        for which, (ref, _, blocks, sems) in enumerate(sets):
             cut = ref.shape[1] // 2
             for way, (device, sign) in enumerate(ways):
-                columns = pl.ds(way * cut, cut)
-                block = wrap(place - sign * step)
                 if step == 0:
                     add_own(which, way, size - 2)
-                    source = slots.at[way, size - 2]
                 else:
                     gather[which, way, step - 1].wait_recv()
-                    source = blocks.at[block, :, columns]
+                source = blocks.at[wrap(place - sign * step), :, pl.ds(way * cut, cut)]
                 gather[which, way, step] = start(
                     push(
                         source,
-                        blocks.at[block, :, columns],
+                        source,
                         (sems.at[0, way, size - 1 + step], sems.at[1, way, size - 1 + step]),
                         device,
                     )
                 )
-                store(which, way, block, source)
-
-    pending = {}
-
-    def store(which, way, block, source):
-        ref, _, _, wide, _ = sets[which]
-        rows_total = ref.shape[0] // size
-        cut = ref.shape[1] // 2
-        for copy in pending.pop((which, way), []):
-            copy.wait()
-
-        def widen(inner):
-            wide[way, inner, :] = source[inner, :].astype(f32)
-
-        row_loop(rows_total, 16, widen)
-        rows = pl.ds(pl.multiple_of(block * rows_total, rows_total), rows_total)
-        if which == 1:
-            targets = [(outer_out.at[rows, pl.ds(way * cut, cut)], 0, cut)]
-        elif way == 0:
-            targets = [(query_out.at[rows, pl.ds(0, cut)], 0, cut)]
-        else:
-            rest = lead - cut
-            tail = key_out.shape[1]
-            targets = [
-                (query_out.at[rows, pl.ds(cut, rest)], 0, rest),
-                (key_out.at[rows], rest, tail),
-                (value_out.at[rows], rest + tail, tail),
-            ]
-        copies = []
-        for index, (target, first, count) in enumerate(targets):
-            copy = pltpu.make_async_copy(
-                wide.at[way, :, pl.ds(first, count)], target, store_sems.at[which, way, index]
-            )
-            copy.start()
-            copies.append(copy)
-        pending[which, way] = copies
 
     def part_rows(index):
         return pl.ds(pl.multiple_of(index * quarter, quarter), quarter)
@@ -442,10 +716,6 @@
     )
     mine = part_rows(own)
     spread = []
-    spread.append(start(push(hidden_ref, hidden_all.at[mine], side(3), (dp, across))))
-    spread.append(start(push(hidden_ref, hidden_all.at[mine], side(4), (dp, partner))))
-    keep = pltpu.make_async_copy(hidden_ref, hidden_all.at[mine], local_sems.at[0])
-    keep.start()
     reduce_send(1)
     first.wait_recv()
     away = across * quarter
@@ -482,20 +752,18 @@
         grad_all[there, :] = joined_grad
 
     row_loop(quarter, 16, finish)
-    spread.append(start(push(grad_all.at[mine], grad_all.at[mine], side(5), (dp, across))))
-    spread.append(start(push(grad_all.at[mine], grad_all.at[mine], side(6), (dp, partner))))
+    spread.append(start(push(grad_all.at[mine], grad_all.at[mine], side(3), (dp, across))))
+    spread.append(start(push(grad_all.at[mine], grad_all.at[mine], side(4), (dp, partner))))
     pair_gains[0, :, :width] = jnp.sum(totals[:, :width], axis=0, keepdims=True)
     pair_gains[0, :, width:] = gains_ref[...]
-    swap = start(push(pair_gains.at[0], pair_gains.at[1], side(7), (dp, partner)))
+    swap = start(push(pair_gains.at[0], pair_gains.at[1], side(5), (dp, partner)))
     reduce_send(3)
     far = part_rows(across)
     spread[0].wait_recv()
-    spread.append(start(push(hidden_all.at[far], hidden_all.at[far], side(8), (dp, partner))))
-    spread[2].wait_recv()
-    spread.append(start(push(grad_all.at[far], grad_all.at[far], side(9), (dp, partner))))
+    spread.append(start(push(grad_all.at[far], grad_all.at[far], side(6), (dp, partner))))
     swap.wait_recv()
     pair_gains[2] = pair_gains[0] + pair_gains[1]
-    swap = start(push(pair_gains.at[2], pair_gains.at[3], side(10), (dp, across)))
+    swap = start(push(pair_gains.at[2], pair_gains.at[3], side(7), (dp, across)))
     for step in range(4, size - 1):
         reduce_send(step)
     swap.wait_recv()
@@ -510,56 +778,37 @@
         if step > 0:
             gather_send(step)
     small.wait_recv()
-    for which, (ref, _, blocks, _, _) in enumerate(sets):
-        cut = ref.shape[1] // 2
-        for way, (_, sign) in enumerate(ways):
-            gather[which, way, size - 2].wait_recv()
-            block = wrap(place - sign * (size - 1))
-            store(which, way, block, blocks.at[block, :, pl.ds(way * cut, cut)])
+    for copy in (gather[which, way, size - 2] for which in (0, 1) for way in (0, 1)):
+        copy.wait_recv()
     gains_out[...] = jnp.sum(ring_gains[...], axis=0)
-    for copies in pending.values():
-        for copy in copies:
-            copy.wait()
-    keep.wait()
-    for index in (1, 3, 4, 5):
-        spread[index].wait_recv()
+    spread[1].wait_recv()
+    spread[2].wait_recv()
     for copy in waits:
         copy.wait_send()
 
 
-def finish_sums(
-    size, grad_in, grad_out, grad_normed, grad_middle, token_rows, hidden_rows, gain, gains, head_dim
-):
+def finish_sums(size, grad_in, grad_out, grad_normed, grad_middle, token_rows, gain, gains):
     bf, f32 = jnp.bfloat16, jnp.float32
     quarter, width = token_rows.shape
     tokens = grad_normed.shape[0]
-    lead = grad_in.shape[1] - 2 * head_dim
     vmem = pl.BlockSpec(memory_space=pltpu.VMEM)
-    anywhere = pl.BlockSpec(memory_space=pl.ANY)
     dma = pltpu.SemaphoreType.DMA
     rows_a, rows_b = grad_in.shape[0] // size, grad_out.shape[0] // size
     cut_a, cut_b = grad_in.shape[1] // 2, grad_out.shape[1] // 2
     count = width + gains.shape[1]
     return pl.pallas_call(
-        functools.partial(finish_sums_body, size, lead),
+        functools.partial(finish_sums_body, size),
         out_shape=(
             jax.ShapeDtypeStruct((tokens, width), bf),
-            jax.ShapeDtypeStruct((tokens, width), bf),
-            jax.ShapeDtypeStruct((width, lead), f32),
-            jax.ShapeDtypeStruct((width, head_dim), f32),
-            jax.ShapeDtypeStruct((width, head_dim), f32),
-            jax.ShapeDtypeStruct(grad_out.shape, f32),
+            jax.ShapeDtypeStruct((size, rows_a, 2 * cut_a), bf),
+            jax.ShapeDtypeStruct((size, rows_b, 2 * cut_b), bf),
             jax.ShapeDtypeStruct((1, count), f32),
         ),
-        in_specs=[vmem] * 8,
-        out_specs=(vmem, vmem, anywhere, anywhere, anywhere, anywhere, vmem),
+        in_specs=[vmem] * 7,
+        out_specs=(vmem,) * 4,
         scratch_shapes=[
             pltpu.VMEM((2, size - 1, rows_a, cut_a), bf),
             pltpu.VMEM((2, size - 1, rows_b, cut_b), bf),
-            pltpu.VMEM((size, rows_a, 2 * cut_a), bf),
-            pltpu.VMEM((size, rows_b, 2 * cut_b), bf),
-            pltpu.VMEM((2, rows_a, cut_a), f32),
-            pltpu.VMEM((2, rows_b, cut_b), f32),
             pltpu.VMEM((2, quarter, width), bf),
             pltpu.VMEM((quarter, width), bf),
             pltpu.VMEM((quarter, width), bf),
@@ -569,9 +818,7 @@
             dma((2, 2, 2 * size - 2)),
             dma((2, 2, 2 * size - 2)),
             dma((2, size - 1)),
-            dma((2, 11)),
-            dma((2, 2, 3)),
-            dma((1,)),
+            dma((2, 8)),
         ],
         compiler_params=pltpu.CompilerParams(
             collective_id=1, has_side_effects=True, vmem_limit_bytes=VMEM_LIMIT
@@ -583,10 +830,66 @@
         grad_normed,
         grad_middle,
         token_rows,
-        hidden_rows,
         gain.reshape(1, -1),
         gains,
     )
+
+
+def large_experts(size, inputs, packs, all_weights, middle, gain, experts, out_rows):
+    f32, bf = jnp.float32, jnp.bfloat16
+    members, _, units, model_width = all_weights.shape
+    local_experts = experts // size
+    indices = jnp.arange(size, dtype=jnp.int32)
+    half = size // 2
+    delta = (ring_place(indices, size) - ring_place(lax.axis_index("dp"), size)) % size
+    ahead = jnp.where(delta == half, size - 2, jnp.where(delta == 0, size - 1, 2 * delta - 1))
+    slots = jnp.where(delta > half, 2 * (size - delta) - 2, ahead)
+    inputs = inputs[slots].reshape(-1, model_width)
+    packs = packs[slots].reshape(inputs.shape[0], -1)
+    grads_all = packs[:, :model_width]
+    shares = packs[:, model_width : model_width + 2 * experts].astype(f32)
+    shares = shares[:, :experts] + shares[:, experts:]
+    shares = lax.dynamic_slice_in_dim(
+        shares, lax.axis_index("dp") * local_experts, local_experts, 1
+    )
+    weight_cols = jnp.broadcast_to(
+        shares[:, None, :, None],
+        (shares.shape[0], members, local_experts, units // local_experts),
+    ).reshape(-1, members, units)
+
+    def project(left, which):
+        return jnp.einsum("td,rud->tru", left, all_weights[:, which], preferred_element_type=f32)
+
+    gate_act = project(inputs, 0)
+    upward = project(inputs, 1)
+    sigmoid_gate = jax.nn.sigmoid(gate_act)
+    active = gate_act * sigmoid_gate * upward
+    weighted_low = (weight_cols * active).astype(bf)
+    mixture_part = jnp.einsum(
+        "tru,rud->td", weighted_low, all_weights[:, 2], preferred_element_type=f32
+    ).astype(bf)
+    grad_active = weight_cols * project(grads_all, 2)
+    grad_gate = (
+        grad_active * upward * sigmoid_gate * (1.0 + gate_act * (1.0 - sigmoid_gate))
+    ).astype(bf)
+    grad_up = (grad_active * gate_act * sigmoid_gate).astype(bf)
+    grad_normed_part = jnp.einsum(
+        "tru,rud->td", grad_gate, all_weights[:, 0], preferred_element_type=f32
+    ) + jnp.einsum("tru,rud->td", grad_up, all_weights[:, 1], preferred_element_type=f32)
+    grad_normed_two = lax.psum_scatter(grad_normed_part.astype(bf), "dp", tiled=True).astype(f32)
+    weight_grads = jnp.stack(
+        [
+            jnp.einsum("tru,td->rud", grad_gate, inputs, preferred_element_type=f32).astype(bf),
+            jnp.einsum("tru,td->rud", grad_up, inputs, preferred_element_type=f32).astype(bf),
+            jnp.einsum("tru,td->rud", weighted_low, grads_all, preferred_element_type=f32).astype(bf),
+        ],
+        axis=1,
+    )
+    hat_two, inv_two = rms_parts(middle)
+    grad_gain_two = jnp.sum(grad_normed_two * hat_two, axis=0)
+    grad_middle = out_rows.astype(f32) + rms_back(grad_normed_two * gain, hat_two, inv_two)
+    grad_mid_low = lax.all_gather(grad_middle.astype(bf), "tensor", tiled=True)
+    return (mixture_part, weight_grads, grad_middle, grad_mid_low, grad_gain_two)
 
 
 def local(
@@ -672,55 +975,26 @@
         .astype(bf)
     )
     hidden_q = mine(hidden_in)
-    hat_one_q, inv_one_q = rms_parts(hidden_q.astype(f32))
     partial = jnp.dot(mixed_low, out_weight, preferred_element_type=f32).astype(bf)
-    middle, inputs, gathered = exchange_tokens(
-        data_size, partial, hidden_q, packed, norm2_gain
-    )
-    inputs = inputs.reshape(rows, model_width)
-    gathered = gathered.reshape(rows, -1)
-    grads_all = gathered[:, :model_width]
-    dense_all = gathered[:, model_width : model_width + experts].astype(f32) + gathered[
-        :, model_width + experts : model_width + 2 * experts
-    ].astype(f32)
-    weight_all = lax.dynamic_slice_in_dim(
-        dense_all, lax.axis_index("dp") * local_experts, local_experts, 1
-    )
-    weight_cols = jnp.broadcast_to(
-        weight_all[:, None, :, None], (rows, tensor_size, local_experts, hidden_part)
-    ).reshape(rows, tensor_size, units)
-    hat_two, inv_two = rms_parts(middle)
-
-    def project(left, which):
-        return jnp.einsum("td,rud->tru", left, all_weights[:, which], preferred_element_type=f32)
-
-    gate_act = project(inputs, 0)
-    upward = project(inputs, 1)
-    sigmoid_gate = jax.nn.sigmoid(gate_act)
-    active = gate_act * sigmoid_gate * upward
-    weighted_low = (weight_cols * active).astype(bf)
-    mixture_part = jnp.einsum(
-        "tru,rud->td", weighted_low, all_weights[:, 2], preferred_element_type=f32
-    ).astype(bf)
+    middle, inputs, gathered = exchange_tokens(data_size, partial, hidden_q, packed, norm2_gain)
+    if data_size <= 8:
+        mixture_part, weight_grads, grad_middle, grad_mid_low, grad_gain_two = run_experts(
+            data_size,
+            inputs.reshape(rows, model_width),
+            gathered.reshape(rows, -1),
+            all_weights,
+            middle,
+            norm2_gain,
+            experts,
+        )
+        grad_gain_two = grad_gain_two.reshape(-1)
+        mixture_part = mixture_part.reshape(rows, model_width)
+    else:
+        mixture_part, weight_grads, grad_middle, grad_mid_low, grad_gain_two = large_experts(
+            data_size, inputs, gathered, all_weights, middle, norm2_gain, experts, mine(out_grad)
+        )
     mixture = lax.psum_scatter(mixture_part, "dp", tiled=True).astype(f32)
-    hidden_out = (middle + mixture).astype(bf)
-    grad_active = weight_cols * project(grads_all, 2)
-    grad_gate = (
-        grad_active * upward * sigmoid_gate * (1.0 + gate_act * (1.0 - sigmoid_gate))
-    ).astype(bf)
-    grad_up = (grad_active * gate_act * sigmoid_gate).astype(bf)
-    grad_normed_part = jnp.einsum(
-        "tru,rud->td", grad_gate, all_weights[:, 0], preferred_element_type=f32
-    ) + jnp.einsum("tru,rud->td", grad_up, all_weights[:, 1], preferred_element_type=f32)
-    grad_normed_two = lax.psum_scatter(grad_normed_part.astype(bf), "dp", tiled=True).astype(f32)
-    weight_grads = jnp.stack(
-        [
-            jnp.einsum("tru,td->rud", grad_gate, inputs, preferred_element_type=f32).astype(bf),
-            jnp.einsum("tru,td->rud", grad_up, inputs, preferred_element_type=f32).astype(bf),
-            jnp.einsum("tru,td->rud", weighted_low, grads_all, preferred_element_type=f32).astype(bf),
-        ],
-        axis=1,
-    )
+    hidden_out = lax.all_gather((middle + mixture).astype(bf), "tensor", tiled=True)
     own_grads = (
         lax.psum_scatter(weight_grads.reshape(-1, model_width), "tensor", tiled=True)
         .astype(f32)
@@ -730,11 +1004,6 @@
         own_grads[:2].reshape(2, local_experts, hidden_part, model_width), (1, 3, 0, 2)
     )
     grad_w_down = own_grads[2].reshape(local_experts, hidden_part, model_width)
-
-    grad_out = mine(out_grad).astype(f32)
-    grad_gain_two = jnp.sum(grad_normed_two * hat_two, axis=0)
-    grad_middle = grad_out + rms_back(grad_normed_two * norm2_gain, hat_two, inv_two)
-    grad_mid_low = lax.all_gather(grad_middle.astype(bf), "tensor", tiled=True)
     grad_out_weight = jnp.einsum("ti,td->id", mixed_low, grad_mid_low, preferred_element_type=f32)
     grad_mixed = (
         jnp.einsum("td,id->ti", grad_mid_low, out_weight, preferred_element_type=f32)
@@ -780,29 +1049,29 @@
         "tj,ij->ti", grad_values, value_weight, preferred_element_type=f32
     )
     gains = jnp.concatenate([grad_gain_two, grad_query_gain, grad_key_gain]).reshape(1, -1)
-    final = finish_sums(
+    grad_hidden, in_low, out_low, gains = finish_sums(
         data_size,
         grad_in_weights,
         grad_out_weight.astype(bf),
         grad_normed_one.astype(bf),
         grad_middle,
         hidden_q,
-        hidden_out,
         norm1_gain,
         gains,
-        head_dim,
-    )
-    gains = final[6].reshape(-1)
+    )
+    in_low = in_low.reshape(model_width, -1)
+    lead = local_heads * head_dim
+    gains = gains.reshape(-1)
     return (
-        final[0],
-        final[1],
+        hidden_out,
+        grad_hidden,
         gains[:model_width],
-        final[2],
-        final[3],
-        final[4],
+        in_low[:, :lead].astype(f32),
+        in_low[:, lead : lead + head_dim].astype(f32),
+        in_low[:, lead + head_dim :].astype(f32),
         gains[2 * model_width : 2 * model_width + head_dim],
         gains[2 * model_width + head_dim :],
-        final[5],
+        out_low.reshape(-1, model_width).astype(f32),
         gains[model_width : 2 * model_width],
         grad_w_gate_up,
         grad_w_down,

time: 734 us -> 664 us (0.905)
  Pallas kernels: 324 us -> 423 us
  matrix products: 151 us -> 54.2 us
  waiting for transfers between devices: 155 us -> 87.2 us
  local copies, waits for them, and re-layouts: 57.8 us -> 43.3 us
  other arithmetic: 24.7 us -> 35.7 us
    dot_general x9 -> x0, matrix products: 99.2 us -> none  [the longest x3 38.9 us: project(): jnp.einsum('td,rud->tru', left, all_weights[:, which], preferred_element_...]
    pallas_call x1 -> x2, Pallas kernels: 215 us -> 314 us  [the longest x1 205 us: finish_sums(): pl.pallas_call(functools.partial(finish_sums_body, size), out_shape=(jax....]
    reduce_scatter x1 -> x0, waiting for transfers between devices: 63.7 us -> none  [local(): lax.psum_scatter(grad_normed_part.astype(bf), 'dp', tiled=True).astype(f32)]
    unnamed x166 -> x112, local copies, waits for them, and re-layouts: 32.3 us -> 17.2 us
    convert_element_type x1 -> x5, other arithmetic: 2.52 us -> 17.1 us  [the longest x1 6.79 us: local(): in_low[:, :lead].astype(f32)]
  transfers between devices with their start and end apart: 5 -> 4, of which waited for: 2 -> 1; matrix products, arithmetic and copies ran while one was open for 18% -> 16% of each run, Pallas kernels for 44% -> 48%
where the time goes in v3:
time: 664 us; the launch traced here: 658 us
  Pallas kernels  423 us (64%)
  waiting for transfers between devices  87.2 us (13%)
  matrix products  54.2 us (8%)
  local copies, waits for them, and re-layouts  43.3 us (7%)
  other arithmetic  35.7 us (5%)
  between operations  14.8 us (2%)
    pallas_call x1, Pallas kernels, finish_sums(): pl.pallas_call(functools.partial(finish_sums_body, size), out_shape=(jax....  205 us
    pallas_call x1, Pallas kernels, exchange_tokens(): pl.pallas_call(functools.partial(exchange_tokens_body, size), out_shape=(...  110 us
    pallas_call x1, Pallas kernels, run_experts(): pl.pallas_call(functools.partial(run_experts_body, size, local_experts, e...  108 us
    reduce_scatter x1, waiting for transfers between devices, local(): mixture = lax.psum_scatter(mixture_part, 'dp', tiled=True).astype(f32)  86.6 us
    unnamed x112, local copies, waits for them, and re-layouts  17.2 us
  transfers between devices with their start and end apart: 4, of which 1 were waited for; matrix products, arithmetic and copies ran while one was open for 16% of the time, Pallas kernels for 48%

profile of v3, /device:TPU:0, one launch (start us, length us, event | category | flops | bytes accessed | tf_op | source)
XLA Modules:
  0.0 658.5 jit_solution(3349388044728514892)
XLA Ops:
  7.2 2.2 copy.149
  9.6 2.6 pad_maximum_fusion
  12.3 0.8 constant_dynamic-slice_fusion
  13.1 0.7 constant_dynamic-slice_fusion.1
  13.8 0.7 copy.146
  14.6 0.7 copy.147
  15.3 0.7 copy.148
  16.9 0.9 multiply_reduce_fusion.4
  18.7 0.8 copy.142
  19.5 6.0 fusion.64
  26.0 0.6 multiply_reduce_fusion.1
  26.6 0.7 copy.139
  27.3 0.9 subtract_convert_fusion.1
  28.3 2.3 constant_dynamic-slice_fusion.2
  30.6 2.2 concatenate.30.pack_ref
  32.9 0.8 fusion.34
  33.7 2.7 fusion.33
  36.4 1.4 fusion.19
  37.9 0.8 subtract_convert_fusion
  38.7 2.6 fusion.6
  41.4 2.4 fusion.20
  43.8 1.8 copy-done.3
  45.6 1.1 copy-done.43
  46.7 3.7 convolution_convert_fusion.2.part_ref
  50.4 109.6 %exchange_tokens.1 = (f32[128,2048]{1,0:T(8,128)}, bf16[8,128,2048]{2,1,0:T(8,128)(2,1)}, bf16[8,128,2176]{2,1,0:T(8,128)(2,1)}) custom-call(bf16[512,2048]{1,0:T(8,128)(2,1)} %convolution_convert_fusion.2.part_ref, bf16[128,2048]{1,0:T(8,128)(2,1)} %get-tuple-element.125.token_ref, bf16[128,2176]{1,0:T(8,128)(2,1)} %concatenate.30.pack_ref, f32[1,2048]{1,0:T(1,128)} %bitcast.176), custom_call_target="tpu_custom_call" | custom-call | tf_op jit(solution)/shard_map/exchange_tokens/pallas_call | solution.py:254
  160.6 108.1 %run_experts.1 = (bf16[8,128,2048]{2,1,0:T(8,128)(2,1)}, bf16[4,3,384,2048]{3,2,1,0:T(8,128)(2,1)}, f32[128,2048]{1,0:T(8,128)}, bf16[512,2048]{1,0:T(8,128)(2,1)}, f32[1,2048]{1,0:T(1,128)}) custom-call(bf16[1024,2048]{1,0:T(8,128)(2,1)} %bitcast.170, bf16[1024,2176]{1,0:T(8,128)(2,1)} %bitcast.169, bf16[4,3,384,2048]{3,2,1,0:T(8,128)(2,1)} %bitcast.162, ...), custom_call_target="tpu_custom_call" | custom-call | tf_op jit(solution)/shard_map/run_experts/pallas_call | solution.py:561
  268.8 86.6 %reduce-scatter.3.cloned.1.call-done = bf16[128,2048]{1,0:T(8,128)(2,1)} async-done(((bf16[1024,2048]{1,0:T(8,128)(2,1)}), bf16[128,2048]{1,0:T(8,128)(2,1)}) %reduce-scatter.3.cloned.1.call-update) | async-done | bytes 524304 | tf_op jit(solution)/shard_map/reduce_scatter | solution.py:996
  355.4 2.3 add_convert_fusion.2
  358.3 1.3 log.8
  359.6 0.8 copy.175
  360.5 1.2 broadcast_bitcast_fusion
  361.7 6.4 convolution_convert_fusion.3
  368.1 2.3 copy.176
  370.4 6.8 %fusion = (f32[8,512]{1,0:T(8,128)S(1)}, f32[512,512,8]{1,0,2:T(8,128)S(1)}) fusion(f32[512,512,8]{1,0,2:T(8,128)} %copy-done.3, f32[8,512]{1,0:T(8,128)} %log.8, pred[512,512]{0,1:T(8,128)(4,1)S(1)} %fusion.34, bf16[512,128,1]{1,0,2:T(8,128)(2,1)} %copy-done.23, bf16[512,8,128]{0,2,1:T(8,128)(2,1)} %bitcast.171), kind=kOutput, calls=%fused_computation.2 | convolution fusion | flops 547352576 | bytes 18251776 | tf_op jit(solution)/shard_map/thd,sd->hts/dot_general | solution.py:1017
  377.3 2.7 fusion.2
  380.0 1.8 multiply_bitcast_fusion
  382.0 1.0 multiply_add_fusion
  383.0 3.0 fusion.35
  386.0 0.8 copy.155
  386.9 1.8 mul.316
  389.3 2.4 fusion.18
  391.8 0.8 copy-done.2
  392.6 0.6 copy-done.8
  393.2 0.6 copy-done.10
  393.9 1.9 fusion.26
  397.4 0.7 fusion.71
  398.2 7.2 %convolution_convert_fusion.1.out_ref = bf16[1024,2048]{1,0:T(8,128)(2,1)} fusion(bf16[512,1024]{0,1:T(8,128)(2,1)S(1)} %bitcast.186, bf16[512,2048]{1,0:T(8,128)(2,1)} %get-tuple-element.28), kind=kOutput, calls=%fused_computation.26 | convolution fusion | flops 2149580800 | bytes 7340032 | tf_op jit(solution)/shard_map/ti,td->id/dot_general | solution.py:1007
  405.4 2.4 fusion.70
  407.8 1.0 slice-done.3
  409.0 1.5 fusion.30
  410.6 2.0 add_convert_fusion.normed_ref
  412.7 5.1 convolution_convert_fusion.qkv_ref
  417.8 205.5 %finish_sums.1 = (bf16[512,2048]{1,0:T(8,128)(2,1)}, bf16[8,256,1280]{2,1,0:T(8,128)(2,1)}, bf16[8,128,2048]{2,1,0:T(8,128)(2,1)}, f32[1,4352]{1,0:T(1,128)}) custom-call(bf16[2048,1280]{1,0:T(8,128)(2,1)} %convolution_convert_fusion.qkv_ref, bf16[1024,2048]{1,0:T(8,128)(2,1)} %convolution_convert_fusion.1.out_ref, ...), custom_call_target="tpu_custom_call" | custom-call | tf_op jit(solution)/shard_map/finish_sums/pallas_call | solution.py:799
  623.2 1.2 slice_bitcast_fusion
  624.4 1.3 fusion.69
  625.7 2.7 slice_convert_fusion.1
  628.4 6.8 %slice_convert_fusion = f32[2048,1024]{1,0:T(8,128)} fusion(bf16[2048,1280]{1,0:T(8,128)(2,1)} %bitcast.168), kind=kLoop, calls=%fused_computation.20 | loop fusion | flops 2097152 | bytes 12582912 | tf_op jit(solution)/shard_map/convert_element_type | solution.py:1069
  635.2 4.7 bitcast_convert_fusion
  640.0 2.9 slice.97
  642.9 3.1 copy.162
  646.0 2.0 slice.98
  648.2 1.3 copy.194
  649.5 0.9 copy-done.16
  650.4 1.3 copy.195
  (140 shorter events, 6.5 us)
Async XLA Ops:
  7.2 9.7 %copy-start = (bf16[2048,128]{1,0:T(8,128)(2,1)S(1)}, bf16[2048,128]{1,0:T(8,128)(2,1)}, u32[]{:S(2)}) copy-start(bf16[2048,128]{1,0:T(8,128)(2,1)} %param.19) | copy-start | bytes 1572868
  7.2 2.4 copy-start.17
  7.2 153.4 %all-gather.6.cloned.1.call-start = ((), (), s32[]{:S(2)}) async-start(), calls=%async_computation.5 | async-start | bytes 23592960 | tf_op jit(solution)/shard_map/all_gather | solution.py:949
  12.2 3.8 copy-start.42
  12.2 4.1 copy-start.11
  12.2 4.6 copy-start.33
  12.2 343.2 %reduce-scatter.3.cloned.1.call-start = ((), (), s32[]{:S(2)}) async-start(), calls=%async_computation.2 | async-start | bytes 4718592 | tf_op jit(solution)/shard_map/reduce_scatter | solution.py:996
  16.2 1.7 copy-start.40
  16.3 1.5 copy-start.29
  16.3 1.5 copy-start.36
  16.9 8.7 %copy-start.38 = (f32[512]{0:T(512)}, f32[512]{0:T(512)S(1)}, u32[]{:S(2)}) copy-start(f32[512]{0:T(512)S(1)} %add_rsqrt_fusion.2) | copy-start | bytes 6148
  17.8 0.7 copy-start.25
  17.8 0.7 copy-start.27
  27.3 5.5 copy-start.24
  36.4 4.9 copy-start.23
  36.4 1.5 copy-start.13
  38.7 2.6 copy-start.7
  38.7 2.6 copy-start.9
  41.3 4.3 copy-start.3
  41.3 4.3 copy-start.31
  41.4 5.4 copy-start.43
  45.6 4.8 copy-start.45
  268.8 371.2 %all-gather.4.cloned.1.call-start = ((), (), s32[]{:S(2)}) async-start(), calls=%async_computation.3 | async-start | bytes 2621440 | tf_op jit(solution)/shard_map/all_gather | solution.py:997
  357.7 282.2 %reduce-scatter.5.cloned.1.call-start = ((), (), s32[]{:S(2)}) async-start(), calls=%async_computation.4 | async-start | bytes 23592960 | tf_op jit(solution)/shard_map/reduce_scatter | solution.py:999
  370.4 6.9 %slice-start = ((s8[8388608]{0:T(1024)(128)(4,1)}), s8[4194304]{0:T(1024)(128)(4,1)S(1)}, s32[]{:S(2)}) async-start(s8[8388608]{0:T(1024)(128)(4,1)} %bitcast.153), calls=%async_computation.6 | async-start | bytes 8388608
  370.4 6.9 %slice-start.1 = ((s8[8388608]{0:T(1024)(128)(4,1)}), s8[4194304]{0:T(1024)(128)(4,1)S(1)}, s32[]{:S(2)}) async-start(s8[8388608]{0:T(1024)(128)(4,1)} %bitcast.153), calls=%async_computation.7 | async-start | bytes 8388608
  370.4 6.9 %copy-start.21 = (f32[8,512]{1,0:T(8,128)S(1)}, f32[8,512]{1,0:T(8,128)}, u32[]{:S(2)}) copy-start(f32[8,512]{1,0:T(8,128)} %log.8) | copy-start | bytes 49156
  380.0 2.0 copy-start.1
  380.0 2.0 copy-start.14
  382.0 1.0 copy-start.35
  383.0 5.6 copy-start.18
  386.0 3.2 copy-start.30
  386.9 2.4 copy-start.4
  389.3 3.3 copy-start.2
  389.3 4.0 copy-start.8
  389.3 4.6 copy-start.10
  393.9 1.9 copy-start.28
  393.9 1.9 copy-start.41
  393.9 2.5 copy-start.26
  393.9 2.5 copy-start.37
  393.9 2.7 copy-start.32
  396.4 1.8 copy-start.46
  398.2 7.2 %copy-start.19 = (bf16[512,1024]{1,0:T(8,128)(2,1)S(1)}, bf16[512,1024]{1,0:T(8,128)(2,1)}, u32[]{:S(2)}) copy-start(bf16[512,1024]{1,0:T(8,128)(2,1)} %get-tuple-element.99) | copy-start | bytes 3145732
  398.2 7.2 %copy-start.44 = (bf16[2048,1024]{1,0:T(8,128)(2,1)S(1)}, bf16[2048,1024]{1,0:T(8,128)(2,1)}, u32[]{:S(2)}) copy-start(bf16[2048,1024]{1,0:T(8,128)(2,1)} %param.18) | copy-start | bytes 12582916
  398.2 9.6 %slice-start.2 = ((s8[8388608]{0:T(1024)(128)(4,1)}), s8[4194304]{0:T(1024)(128)(4,1)S(1)}, s32[]{:S(2)}) async-start(s8[8388608]{0:T(1024)(128)(4,1)} %bitcast.155), calls=%async_computation.8 | async-start | bytes 8388608
  405.4 3.4 slice-start.3
  405.4 3.6 copy-start.6
  405.4 3.6 copy-start.22
  409.0 1.5 copy-start.20
  410.6 2.1 copy-start.12
  410.6 2.1 copy-start.34
  410.6 2.1 copy-start.39
  628.4 6.8 %copy-start.5 = (bf16[8,128,2048]{2,1,0:T(8,128)(2,1)S(1)}, bf16[8,128,2048]{2,1,0:T(8,128)(2,1)}, u32[]{:S(2)}) copy-start(bf16[8,128,2048]{2,1,0:T(8,128)(2,1)} %get-tuple-element.34) | copy-start | bytes 12582916
  640.0 6.0 slice-start.4
  642.8 3.2 slice-start.5
  646.0 2.2 copy-start.15
  648.0 2.4 copy-start.16
Sparse Core Ops, SparseCore 0:
  12.3 133.9 all-gather.5
  268.9 86.5 reduce-scatter.2
  357.9 22.1 all-gather.3
  382.6 160.6 reduce-scatter.4

commit v4 on v3

--- a/solution.py
+++ b/solution.py
@@ -65,7 +65,7 @@
 
 LANES = 128
 MESH = pl.DeviceIdType.MESH
-VMEM_LIMIT = 60 * 1024 * 1024
+VMEM_LIMIT = 127 * 512 * 1024
 
 
 def ring_place(index, size):
@@ -294,22 +294,27 @@
     member_ref,
     middle_ref,
     gain_ref,
-    mix_ref,
-    wgrad_ref,
+    hidden_out,
+    kept_ref,
+    given_ref,
     gmid_ref,
     gmid_all,
     gain_out,
     weights,
     hidden,
-    parts,
-    slots,
+    grad_parts,
+    mix_parts,
+    grad_slots,
+    mix_slots,
     turned,
     stage,
     totals,
     load_sems,
-    ring_sems,
+    grad_sems,
+    mix_sems,
     side_sems,
     store_sems,
+    give_sems,
 ):
     f32, bf = jnp.float32, jnp.bfloat16
     dp = lax.axis_index("dp")
@@ -338,22 +343,27 @@
     for piece in range(pieces):
         load(piece).start()
 
-    def ring_copy(way, step, source):
+    grad_ring = (grad_parts, grad_slots, grad_sems)
+    mix_ring = (mix_parts, mix_slots, mix_sems)
+
+    def ring_copy(ring, way, step, source):
         device = forward if way == 0 else backward
+        _, slots, sems = ring
         return push(
-            source, slots.at[way, step], (ring_sems.at[0, way, step], ring_sems.at[1, way, step]), device
+            source, slots.at[way, step], (sems.at[0, way, step], sems.at[1, way, step]), device
         )
 
     def columns_of(way):
         return pl.ds(way * cut, cut)
 
-    def ring_step(step, blocks, first=False):
+    def ring_step(ring, step, blocks, first=False):
+        parts, slots, _ = ring
         for way in (0, 1):
             if first:
                 source = parts.at[blocks[way], :, columns_of(way)]
             else:
                 source = slots.at[way, step - 1]
-                ring_copy(way, step - 1, source).wait_recv()
+                ring_copy(ring, way, step - 1, source).wait_recv()
 
                 def add(rows):
                     slots[way, step - 1, rows, :] = (
@@ -362,7 +372,7 @@
                     ).astype(bf)
 
                 row_loop(quarter, 16, add)
-            ring_copy(way, step, source).start()
+            ring_copy(ring, way, step, source).start()
 
     def do_pair(index, carry):
         rows = pl.ds(pl.multiple_of(index * pair, pair), pair)
@@ -404,54 +414,61 @@
                 hidden[1, rows, :], weights[1, :, here]
             )
             low = sums.astype(bf)
-            parts[2 * index, :, here] = low[:quarter]
-            parts[2 * index + 1, :, here] = low[quarter:]
+            grad_parts[2 * index, :, here] = low[:quarter]
+            grad_parts[2 * index + 1, :, here] = low[quarter:]
             return carry
 
+        def do_mix(tile, carry):
+            here = pl.ds(pl.multiple_of(tile * wide, wide), wide)
+            low = matmul(hidden[2, rows, :], weights[2, :, here]).astype(bf)
+            mix_parts[2 * index, :, here] = low[:quarter]
+            mix_parts[2 * index + 1, :, here] = low[quarter:]
+            return carry
+
         lax.fori_loop(0, width // wide, do_columns, 0)
 
-        @pl.when(index == 0)
-        def _():
-            ring_step(0, (0, 1), first=True)
-
-        @pl.when(index > 0)
-        def _():
-            ring_step(index, (2 * index, 2 * index + 1 - index // (half - 1)))
-
+        def go_on(ring):
+            @pl.when(index == 0)
+            def _():
+                ring_step(ring, 0, (0, 1), first=True)
+
+            @pl.when(index > 0)
+            def _():
+                ring_step(ring, index, (2 * index, 2 * index + 1 - index // (half - 1)))
+
+        go_on(grad_ring)
+        lax.fori_loop(0, width // wide, do_mix, 0)
+        go_on(mix_ring)
         return carry
 
     lax.fori_loop(0, half, do_pair, 0)
-
-    def mix_pairs(first, last):
-        def run(index, carry):
-            rows = pl.ds(pl.multiple_of(index * pair, pair), pair)
-            left = ring_index(place + size - 1 - index, size)
-            right = ring_index(place + (index + 1) % half, size)
-
-            def do_columns(tile, carry):
-                here = pl.ds(pl.multiple_of(tile * wide, wide), wide)
-                low = matmul(hidden[2, rows, :], weights[2, :, here]).astype(bf)
-                mix_ref[left, :, here] = low[:quarter]
-                mix_ref[right, :, here] = low[quarter:]
-                return carry
-
-            lax.fori_loop(0, width // wide, do_columns, 0)
-            return carry
-
-        lax.fori_loop(first, last, run, 0)
-
-    def store(kind, member, slot):
-        return pltpu.make_async_copy(stage.at[slot], wgrad_ref.at[member, kind], store_sems.at[slot])
+    far_partner = (partner + 2) % 4
+
+    def keep(index, slot):
+        target = kept_ref.at[index % members - 2, index // members]
+        return pltpu.make_async_copy(stage.at[slot], target, store_sems.at[slot])
+
+    def give(index, slot):
+        target = given_ref.at[index % members, index // members]
+        number = 2 * (index // members) + index % members
+        return push(
+            stage.at[slot], target, (give_sems.at[0, number], give_sems.at[1, number]), (dp, partner)
+        )
 
     def weight_grads(first, last):
         def run(index, carry):
             kind = index // members
-            member = index % members
+            whose = index % members
             slot = index % 2
-
-            @pl.when(index >= 2)
+            member = jnp.where(whose < 2, partner + 2 * whose, own + 2 * (3 - whose)) % members
+
+            @pl.when((index >= 2) & (whose < 2))
             def _():
-                store(kind, member, slot).wait()
+                keep(index - 2, slot).wait()
+
+            @pl.when(whose >= 2)
+            def _():
+                give(index - 2, slot).wait_send()
 
             rows = pl.ds(pl.multiple_of(member * span, span), span)
             for chunk in range(half):
@@ -465,7 +482,15 @@
                 return carry
 
             lax.fori_loop(0, width // wide, do_columns, 0)
-            store(kind, member, slot).start()
+
+            @pl.when(whose < 2)
+            def _():
+                give(index, slot).start()
+
+            @pl.when(whose >= 2)
+            def _():
+                keep(index, slot).start()
+
             return carry
 
         lax.fori_loop(first, last, run, 0)
@@ -473,14 +498,17 @@
     def final_sum():
         totals[...] = jnp.zeros_like(totals)
         for way in (0, 1):
-            ring_copy(way, size - 2, slots.at[way, size - 2]).wait_recv()
+            ring_copy(grad_ring, way, size - 2, grad_slots.at[way, size - 2]).wait_recv()
         base = own * quarter
 
         def finish(rows):
             sums = jnp.concatenate(
-                [slots[0, size - 2, rows, :].astype(f32), slots[1, size - 2, rows, :].astype(f32)],
+                [
+                    grad_slots[0, size - 2, rows, :].astype(f32),
+                    grad_slots[1, size - 2, rows, :].astype(f32),
+                ],
                 axis=-1,
-            ) + parts[size - 1, rows, :].astype(f32)
+            ) + grad_parts[size - 1, rows, :].astype(f32)
             middle = middle_ref[rows, :]
             inverse = lax.rsqrt(jnp.mean(middle * middle, axis=-1, keepdims=True) + EPSILON)
             hat = middle * inverse
@@ -513,37 +541,55 @@
         spread(0, own, (dp, across)).wait_recv()
         spread(2, across, (dp, partner)).start()
 
-    events = []
+    def final_mix():
+        for way in (0, 1):
+            ring_copy(mix_ring, way, size - 2, mix_slots.at[way, size - 2]).wait_recv()
+
+        def finish(rows):
+            for way in (0, 1):
+                columns = columns_of(way)
+                hidden_out[rows, columns] = (
+                    middle_ref[rows, columns]
+                    + mix_slots[way, size - 2, rows, :].astype(f32)
+                    + mix_parts[size - 1, rows, columns].astype(f32)
+                ).astype(bf)
+
+        row_loop(quarter, 16, finish)
+
+    def closing():
+        final_sum()
+        first_spread()
+
+    grad_events, mix_events = [], []
     for step in range(half, size - 1):
         delta = -(1 + step)
         blocks = (slot_of(delta, size), slot_of(-delta, size))
-        events.append(functools.partial(ring_step, step, blocks))
-
-    def closing():
-        final_sum()
-        first_spread()
-
-    events.append(closing)
-    events.append(second_spread)
-    work = [functools.partial(mix_pairs, 0, half // 2), functools.partial(mix_pairs, half // 2, half)]
-    for first in range(0, 3 * members, 2):
-        work.append(functools.partial(weight_grads, first, first + 2))
+        grad_events.append(functools.partial(ring_step, grad_ring, step, blocks))
+        mix_events.append(functools.partial(ring_step, mix_ring, step, blocks))
+    events = grad_events[:-1]
+    events += [grad_events[-1], mix_events[0], closing] + mix_events[1:2] + [second_spread]
+    events += mix_events[2:] + [final_mix]
+    work = [functools.partial(weight_grads, first, first + 2) for first in range(0, 3 * members, 2)]
     done = 0
     for number, piece in enumerate(work):
         piece()
-        upto = min(len(events), -(-(number + 1) * len(events) // (len(work) - 2)))
+        upto = -(-(number + 1) * len(events) // len(work))
         while done < upto:
             events[done]()
             done += 1
     for slot in (0, 1):
-        store(0, 0, slot).wait()
+        keep(3 * members - 2 + slot, slot).wait()
+    for kind in range(3):
+        for whose in (0, 1):
+            give(kind * members + whose, 0).wait_recv()
     spread(1, own, (dp, partner)).wait_recv()
     spread(2, across, (dp, partner)).wait_recv()
     for index, device in ((0, across), (1, partner), (2, partner)):
         spread(index, own, (dp, device)).wait_send()
-    for way in (0, 1):
-        for step in range(size - 1):
-            ring_copy(way, step, slots.at[way, step]).wait_send()
+    for ring in (grad_ring, mix_ring):
+        for way in (0, 1):
+            for step in range(size - 1):
+                ring_copy(ring, way, step, ring[1].at[way, step]).wait_send()
 
 
 def run_experts(size, inputs, packs, weights, middle, gain, experts):
@@ -561,26 +607,31 @@
     return pl.pallas_call(
         functools.partial(run_experts_body, size, local_experts, experts),
         out_shape=(
-            jax.ShapeDtypeStruct((size, quarter, width), bf),
-            jax.ShapeDtypeStruct((members, 3, span, width), bf),
+            jax.ShapeDtypeStruct((quarter, width), bf),
+            jax.ShapeDtypeStruct((2, 3, span, width), bf),
+            jax.ShapeDtypeStruct((2, 3, span, width), bf),
             jax.ShapeDtypeStruct((quarter, width), f32),
             jax.ShapeDtypeStruct((members * quarter, width), bf),
             jax.ShapeDtypeStruct((1, width), f32),
         ),
         in_specs=[vmem, vmem, anywhere, vmem, vmem, vmem],
-        out_specs=(vmem, anywhere, vmem, vmem, vmem),
+        out_specs=(vmem, anywhere, anywhere, vmem, vmem, vmem),
         scratch_shapes=[
             pltpu.VMEM((3, units, width), bf),
             pltpu.VMEM((3, rows, units), bf),
             pltpu.VMEM((size, quarter, width), bf),
+            pltpu.VMEM((size, quarter, width), bf),
+            pltpu.VMEM((2, size - 1, quarter, width // 2), bf),
             pltpu.VMEM((2, size - 1, quarter, width // 2), bf),
             pltpu.VMEM((span, rows), bf),
             pltpu.VMEM((2, span, width), bf),
             pltpu.VMEM((8, width), f32),
             dma((units // LANES,)),
             dma((2, 2, size - 1)),
+            dma((2, 2, size - 1)),
             dma((2, 3)),
             dma((2,)),
+            dma((2, 6)),
         ],
         compiler_params=pltpu.CompilerParams(
             collective_id=2, has_side_effects=True, vmem_limit_bytes=VMEM_LIMIT
@@ -596,8 +647,12 @@
     normed_ref,
     middle_ref,
     token_ref,
+    hidden_ref,
+    cross_ref,
     gain_ref,
     gains_ref,
+    hidden_all,
+    crossed_ref,
     grad_all,
     gather_a,
     gather_b,
@@ -715,7 +770,16 @@
         push(normed_ref.at[part_rows(partner)], from_partner.at[0], side(1), (dp, partner))
     )
     mine = part_rows(own)
+    crossing = start(push(cross_ref, crossed_ref, side(8), (dp, across)))
+    home = own * quarter
+
+    def keep(rows):
+        hidden_all[pl.ds(pl.multiple_of(home + rows.start, 16), rows.size), :] = hidden_ref[rows, :]
+
+    row_loop(quarter, 16, keep)
     spread = []
+    shown = [start(push(hidden_ref, hidden_all.at[mine], side(9), (dp, across)))]
+    shown.append(start(push(hidden_ref, hidden_all.at[mine], side(10), (dp, partner))))
     reduce_send(1)
     first.wait_recv()
     away = across * quarter
@@ -731,7 +795,6 @@
     reduce_send(2)
     second.wait_recv()
     third.wait_recv()
-    home = own * quarter
     totals[...] = jnp.zeros_like(totals)
 
     def finish(rows):
@@ -759,6 +822,8 @@
     swap = start(push(pair_gains.at[0], pair_gains.at[1], side(5), (dp, partner)))
     reduce_send(3)
     far = part_rows(across)
+    shown[0].wait_recv()
+    shown.append(start(push(hidden_all.at[far], hidden_all.at[far], side(11), (dp, partner))))
     spread[0].wait_recv()
     spread.append(start(push(grad_all.at[far], grad_all.at[far], side(6), (dp, partner))))
     swap.wait_recv()
@@ -781,17 +846,20 @@
     for copy in (gather[which, way, size - 2] for which in (0, 1) for way in (0, 1)):
         copy.wait_recv()
     gains_out[...] = jnp.sum(ring_gains[...], axis=0)
-    spread[1].wait_recv()
-    spread[2].wait_recv()
+    for copy in (spread[1], spread[2], shown[1], shown[2], crossing):
+        copy.wait_recv()
     for copy in waits:
         copy.wait_send()
 
 
-def finish_sums(size, grad_in, grad_out, grad_normed, grad_middle, token_rows, gain, gains):
+def finish_sums(
+    size, grad_in, grad_out, grad_normed, grad_middle, token_rows, hidden_rows, cross, gain, gains
+):
     bf, f32 = jnp.bfloat16, jnp.float32
     quarter, width = token_rows.shape
     tokens = grad_normed.shape[0]
     vmem = pl.BlockSpec(memory_space=pltpu.VMEM)
+    anywhere = pl.BlockSpec(memory_space=pl.ANY)
     dma = pltpu.SemaphoreType.DMA
     rows_a, rows_b = grad_in.shape[0] // size, grad_out.shape[0] // size
     cut_a, cut_b = grad_in.shape[1] // 2, grad_out.shape[1] // 2
@@ -800,12 +868,14 @@
         functools.partial(finish_sums_body, size),
         out_shape=(
             jax.ShapeDtypeStruct((tokens, width), bf),
+            jax.ShapeDtypeStruct(cross.shape, bf),
+            jax.ShapeDtypeStruct((tokens, width), bf),
             jax.ShapeDtypeStruct((size, rows_a, 2 * cut_a), bf),
             jax.ShapeDtypeStruct((size, rows_b, 2 * cut_b), bf),
             jax.ShapeDtypeStruct((1, count), f32),
         ),
-        in_specs=[vmem] * 7,
-        out_specs=(vmem,) * 4,
+        in_specs=[vmem] * 6 + [anywhere, vmem, vmem],
+        out_specs=(vmem, anywhere) + (vmem,) * 4,
         scratch_shapes=[
             pltpu.VMEM((2, size - 1, rows_a, cut_a), bf),
             pltpu.VMEM((2, size - 1, rows_b, cut_b), bf),
@@ -818,7 +888,7 @@
             dma((2, 2, 2 * size - 2)),
             dma((2, 2, 2 * size - 2)),
             dma((2, size - 1)),
-            dma((2, 8)),
+            dma((2, 12)),
         ],
         compiler_params=pltpu.CompilerParams(
             collective_id=1, has_side_effects=True, vmem_limit_bytes=VMEM_LIMIT
@@ -830,12 +900,14 @@
         grad_normed,
         grad_middle,
         token_rows,
+        hidden_rows,
+        cross,
         gain.reshape(1, -1),
         gains,
     )
 
 
-def large_experts(size, inputs, packs, all_weights, middle, gain, experts, out_rows):
+def large_experts(size, inputs, packs, all_weights, middle, gain, experts):
     f32, bf = jnp.float32, jnp.bfloat16
     members, _, units, model_width = all_weights.shape
     local_experts = experts // size
@@ -844,8 +916,10 @@
     delta = (ring_place(indices, size) - ring_place(lax.axis_index("dp"), size)) % size
     ahead = jnp.where(delta == half, size - 2, jnp.where(delta == 0, size - 1, 2 * delta - 1))
     slots = jnp.where(delta > half, 2 * (size - delta) - 2, ahead)
-    inputs = inputs[slots].reshape(-1, model_width)
-    packs = packs[slots].reshape(inputs.shape[0], -1)
+    quarter = middle.shape[0]
+    out_rows = packs[-quarter:, :model_width]
+    inputs = inputs.reshape(size, quarter, -1)[slots].reshape(-1, model_width)
+    packs = packs.reshape(size, quarter, -1)[slots].reshape(inputs.shape[0], -1)
     grads_all = packs[:, :model_width]
     shares = packs[:, model_width : model_width + 2 * experts].astype(f32)
     shares = shares[:, :experts] + shares[:, experts:]
@@ -889,7 +963,13 @@
     grad_gain_two = jnp.sum(grad_normed_two * hat_two, axis=0)
     grad_middle = out_rows.astype(f32) + rms_back(grad_normed_two * gain, hat_two, inv_two)
     grad_mid_low = lax.all_gather(grad_middle.astype(bf), "tensor", tiled=True)
-    return (mixture_part, weight_grads, grad_middle, grad_mid_low, grad_gain_two)
+    mixture = lax.psum_scatter(mixture_part, "dp", tiled=True).astype(f32)
+    hidden_out = (middle + mixture).astype(bf)
+    zero = jnp.zeros(weight_grads.shape[1:], bf)
+    sums = lax.psum_scatter(weight_grads.reshape(-1, model_width), "tensor", tiled=True)
+    kept = jnp.stack([zero, sums.reshape(zero.shape)])
+    given = jnp.stack([zero, zero])
+    return (hidden_out, kept, given, grad_middle, grad_mid_low, grad_gain_two)
 
 
 def local(
@@ -977,33 +1057,18 @@
     hidden_q = mine(hidden_in)
     partial = jnp.dot(mixed_low, out_weight, preferred_element_type=f32).astype(bf)
     middle, inputs, gathered = exchange_tokens(data_size, partial, hidden_q, packed, norm2_gain)
-    if data_size <= 8:
-        mixture_part, weight_grads, grad_middle, grad_mid_low, grad_gain_two = run_experts(
-            data_size,
-            inputs.reshape(rows, model_width),
-            gathered.reshape(rows, -1),
-            all_weights,
-            middle,
-            norm2_gain,
-            experts,
-        )
-        grad_gain_two = grad_gain_two.reshape(-1)
-        mixture_part = mixture_part.reshape(rows, model_width)
-    else:
-        mixture_part, weight_grads, grad_middle, grad_mid_low, grad_gain_two = large_experts(
-            data_size, inputs, gathered, all_weights, middle, norm2_gain, experts, mine(out_grad)
-        )
-    mixture = lax.psum_scatter(mixture_part, "dp", tiled=True).astype(f32)
-    hidden_out = lax.all_gather((middle + mixture).astype(bf), "tensor", tiled=True)
-    own_grads = (
-        lax.psum_scatter(weight_grads.reshape(-1, model_width), "tensor", tiled=True)
-        .astype(f32)
-        .reshape(3, units, model_width)
-    )
-    grad_w_gate_up = jnp.transpose(
-        own_grads[:2].reshape(2, local_experts, hidden_part, model_width), (1, 3, 0, 2)
-    )
-    grad_w_down = own_grads[2].reshape(local_experts, hidden_part, model_width)
+    stage = run_experts if data_size <= 8 else large_experts
+    hidden_out, kept, given, grad_middle, grad_mid_low, grad_gain_two = stage(
+        data_size,
+        inputs.reshape(rows, model_width),
+        gathered.reshape(rows, -1),
+        all_weights,
+        middle,
+        norm2_gain,
+        experts,
+    )
+    grad_gain_two = grad_gain_two.reshape(-1)
+    joined = (kept[0].astype(f32) + given[1].astype(f32)).astype(bf)
     grad_out_weight = jnp.einsum("ti,td->id", mixed_low, grad_mid_low, preferred_element_type=f32)
     grad_mixed = (
         jnp.einsum("td,id->ti", grad_mid_low, out_weight, preferred_element_type=f32)
@@ -1049,16 +1114,23 @@
         "tj,ij->ti", grad_values, value_weight, preferred_element_type=f32
     )
     gains = jnp.concatenate([grad_gain_two, grad_query_gain, grad_key_gain]).reshape(1, -1)
-    grad_hidden, in_low, out_low, gains = finish_sums(
+    hidden_out, crossed, grad_hidden, in_low, out_low, gains = finish_sums(
         data_size,
         grad_in_weights,
         grad_out_weight.astype(bf),
         grad_normed_one.astype(bf),
         grad_middle,
         hidden_q,
+        hidden_out,
+        joined,
         norm1_gain,
         gains,
     )
+    own_grads = kept[1].astype(f32) + given[0].astype(f32) + crossed.astype(f32)
+    grad_w_gate_up = jnp.transpose(
+        own_grads[:2].reshape(2, local_experts, hidden_part, model_width), (1, 3, 0, 2)
+    )
+    grad_w_down = own_grads[2].reshape(local_experts, hidden_part, model_width)
     in_low = in_low.reshape(model_width, -1)
     lead = local_heads * head_dim
     gains = gains.reshape(-1)

time: 664 us -> 650 us (0.979)
  waiting for transfers between devices: 87.2 us -> 0.02 us
  Pallas kernels: 423 us -> 502 us
  local copies, waits for them, and re-layouts: 43.3 us -> 30.3 us
  other arithmetic: 35.7 us -> 44.5 us
    reduce_scatter x2 -> x0, waiting for transfers between devices: 86.6 us -> none  [the longest x1 86.6 us: local(): mixture = lax.psum_scatter(mixture_part, 'dp', tiled=True).astype(f32)]
    pallas_call x1, Pallas kernels: 205 us -> 283 us  [finish_sums(): pl.pallas_call(functools.partial(finish_sums_body, size), out_shape=(jax....]
    add x0 -> x1, other arithmetic: none -> 8.42 us  [local(): own_grads = kept[1].astype(f32) + given[0].astype(f32) + crossed.astype(f32)]
    unnamed x112 -> x125, local copies, waits for them, and re-layouts: 17.2 us -> 16.1 us
  transfers between devices with their start and end apart: 4 -> 1, of which waited for: 1 -> 0; matrix products, arithmetic and copies ran while one was open for 16% -> 6% of each run, Pallas kernels for 48% -> 17%
where the time goes in v4:
time: 650 us; the launch traced here: 645 us
  Pallas kernels  502 us (77%)
  matrix products  53.1 us (8%)
  other arithmetic  44.5 us (7%)
  local copies, waits for them, and re-layouts  30.3 us (5%)
  between operations  15.5 us (2%)
    pallas_call x1, Pallas kernels, finish_sums(): pl.pallas_call(functools.partial(finish_sums_body, size), out_shape=(jax....  283 us
    pallas_call x1, Pallas kernels, run_experts(): pl.pallas_call(functools.partial(run_experts_body, size, local_experts, e...  110 us
    pallas_call x1, Pallas kernels, exchange_tokens(): pl.pallas_call(functools.partial(exchange_tokens_body, size), out_shape=(...  109 us
    unnamed x125, local copies, waits for them, and re-layouts  16.1 us
  transfers between devices with their start and end apart: 1, of which 0 were waited for; matrix products, arithmetic and copies ran while one was open for 6% of the time, Pallas kernels for 17%

profile of v4, /device:TPU:0, one launch (start us, length us, event | category | flops | bytes accessed | tf_op | source)
XLA Modules:
  0.0 645.4 jit_solution(11825762712269829023)
XLA Ops:
  7.3 2.2 copy.144
  9.6 2.6 pad_maximum_fusion
  12.2 0.8 constant_dynamic-slice_fusion.1
  13.2 0.7 copy.142
  14.1 0.5 fusion.9
  14.6 0.9 multiply_reduce_fusion.4
  15.8 5.2 fusion.68
  21.1 0.5 copy.176
  21.6 0.6 multiply_reduce_fusion.1
  22.3 0.8 copy.172
  23.6 1.7 fusion.46
  25.4 0.7 fusion.20
  26.1 0.8 subtract_convert_fusion
  27.0 6.3 fusion.6
  33.3 2.1 constant_dynamic-slice_fusion.2
  35.4 1.0 concatenate.30.pack_ref
  36.3 1.8 fusion.34
  38.2 5.8 fusion.21
  44.1 3.7 convolution_convert_fusion.2.part_ref
  47.8 109.4 %exchange_tokens.1 = (f32[128,2048]{1,0:T(8,128)}, bf16[8,128,2048]{2,1,0:T(8,128)(2,1)}, bf16[8,128,2176]{2,1,0:T(8,128)(2,1)}) custom-call(bf16[512,2048]{1,0:T(8,128)(2,1)} %convolution_convert_fusion.2.part_ref, bf16[128,2048]{1,0:T(8,128)(2,1)} %get-tuple-element.71.token_ref, bf16[128,2176]{1,0:T(8,128)(2,1)} %concatenate.30.pack_ref, f32[1,2048]{1,0:T(1,128)} %bitcast.176), custom_call_target="tpu_custom_call" | custom-call | tf_op jit(solution)/shard_map/exchange_tokens/pallas_call | solution.py:254
  157.2 0.6 compare_convert_fusion.member_ref
  157.8 109.9 %run_experts.1 = (bf16[128,2048]{1,0:T(8,128)(2,1)}, bf16[2,3,384,2048]{3,2,1,0:T(8,128)(2,1)}, bf16[2,3,384,2048]{3,2,1,0:T(8,128)(2,1)}, f32[128,2048]{1,0:T(8...) custom-call(bf16[1024,2048]{1,0:T(8,128)(2,1)} %bitcast.171, bf16[1024,2176]{1,0:T(8,128)(2,1)} %bitcast.170, ...), custom_call_target="tpu_custom_call" | custom-call | tf_op jit(solution)/shard_map/run_experts/pallas_call | solution.py:607
  267.7 5.2 convolution_convert_fusion.3
  273.0 0.5 copy.173
  273.6 4.9 fusion
  278.5 0.9 slice-done.2
  279.4 2.9 fusion.2
  282.3 1.9 multiply_bitcast_fusion
  284.3 1.4 fusion.27
  285.7 1.6 fusion.31
  287.3 0.2 copy-done.54
  287.5 4.4 convolution_convert_fusion.1.out_ref
  291.9 1.0 multiply_add_fusion
  292.9 0.6 copy-done.4
  293.5 2.8 fusion.36
  296.4 0.6 mul.316
  297.0 0.6 mul.272.clone
  297.6 0.4 copy-done.5
  298.0 1.5 fusion.19
  299.6 1.5 fusion.49
  301.1 0.3 multiply_reduce_fusion.2
  301.4 0.6 reshape.276.gains_ref
  302.0 2.4 fusion.71
  304.4 0.3 multiply_convert_fusion
  304.7 0.7 fusion.72
  305.4 0.5 copy-done.14
  306.0 4.9 convolution_convert_fusion.qkv_ref
  310.9 6.8 %fusion.7.cross_ref = bf16[3,384,2048]{2,1,0:T(8,128)(2,1)} fusion(bf16[2,3,384,2048]{3,2,1,0:T(8,128)(2,1)} %get-tuple-element.34, bf16[2,3,384,2048]{3,2,1,0:T(8,128)(2,1)S(1)} %bitcast.163), kind=kLoop, calls=%fused_computation.18 | loop fusion | flops 9437184 | bytes 14155776 | tf_op jit(solution)/shard_map/convert_element_type | solution.py:1071
  317.7 2.1 add_convert_fusion.1.normed_ref
  319.8 282.6 %finish_sums.1 = (bf16[512,2048]{1,0:T(8,128)(2,1)}, bf16[3,384,2048]{2,1,0:T(8,128)(2,1)}, bf16[512,2048]{1,0:T(8,128)(2,1)}, bf16[8,256,1280]{2,1,0:T(8,128)(2...) custom-call(bf16[2048,1280]{1,0:T(8,128)(2,1)} %convolution_convert_fusion.qkv_ref, ...), custom_call_target="tpu_custom_call" | custom-call | tf_op jit(solution)/shard_map/finish_sums/pallas_call | solution.py:867
  602.4 8.4 %bitcast_add_fusion = f32[3,384,2048]{2,1,0:T(8,128)S(1)} fusion(bf16[3,384,2048]{2,1,0:T(8,128)(2,1)} %get-tuple-element.41, bf16[2,3,384,2048]{3,2,1,0:T(8,128)(2,1)} %get-tuple-element.34, bf16[2,3,384,2048]{3,2,1,0:T(8,128)(2,1)} %get-tuple-element.33), kind=kLoop, calls=%fused_computation | loop fusion | flops 11796480 | bytes 23592960 | tf_op jit(solution)/shard_map/add | solution.py:1129
  610.8 3.6 copy-done.2
  614.5 2.0 slice.112
  616.5 1.6 copy-done.6
  618.1 4.7 slice_convert_fusion
  622.8 1.5 slice_convert_fusion.1
  624.3 0.6 fusion.70
  624.9 0.5 slice_bitcast_fusion
  625.4 3.5 copy.190
  628.9 0.7 copy-done.7
  629.6 4.7 bitcast_convert_fusion
  634.3 1.3 copy.193
  635.7 1.0 copy-done.21
  636.7 1.3 copy.194
  (144 shorter events, 1.7 us)
Async XLA Ops:
  7.2 5.0 copy-start
  7.2 2.4 copy-start.23
  7.2 150.6 %all-gather.3.cloned.1.call-start = ((), (), s32[]{:S(2)}) async-start(), calls=%async_computation | async-start | bytes 23592960 | tf_op jit(solution)/shard_map/all_gather | solution.py:1029
  12.1 1.9 copy-start.12
  12.2 2.4 copy-start.25
  12.2 2.4 copy-start.38
  12.2 3.5 copy-start.49
  14.6 6.5 %copy-start.47 = (f32[512]{0:T(512)}, f32[512]{0:T(512)S(1)}, u32[]{:S(2)}) copy-start(f32[512]{0:T(512)S(1)} %add_rsqrt_fusion.2) | copy-start | bytes 6148
  21.0 4.3 copy-start.3
  21.1 2.4 copy-start.41
  21.1 4.3 copy-start.43
  23.1 3.7 copy-start.45
  23.2 3.6 copy-start.33
  23.3 3.6 copy-start.35
  23.4 14.7 %copy-start.15 = (pred[512,512]{0,1:T(8,128)(4,1)}, pred[512,512]{0,1:T(8,128)(4,1)S(1)}, u32[]{:S(2)}) copy-start(pred[512,512]{0,1:T(8,128)(4,1)S(1)} %fusion.35) | copy-start | bytes 786436
  25.3 1.6 copy-start.17
  25.4 1.6 copy-start.19
  25.4 1.6 copy-start.28
  26.9 6.3 copy-start.8
  26.9 6.3 copy-start.10
  27.0 6.3 copy-start.30
  27.0 6.3 copy-start.13
  38.1 5.9 copy-start.31
  38.2 5.9 copy-start.50
  44.0 3.7 copy-start.53
  44.1 113.1 %copy-start.44 = (f32[128]{0:T(128)S(1)}, f32[128]{0:T(128)}, u32[]{:S(2)}) copy-start(f32[128]{0:T(128)} %param.21) | copy-start | bytes 1540
  267.7 5.8 copy-start.16
  267.7 5.8 copy-start.32
  273.5 5.0 slice-start.1
  273.5 5.9 slice-start.2
  279.4 2.9 copy-start.29
  282.3 1.9 copy-start.9
  282.3 1.9 copy-start.11
  285.6 1.6 copy-start.52
  285.7 1.8 copy-start.54
  287.5 4.4 copy-start.18
  287.5 4.4 copy-start.20
  291.9 1.6 copy-start.4
  293.5 3.5 copy-start.24
  296.4 1.6 copy-start.5
  298.0 1.6 copy-start.36
  298.0 1.6 copy-start.46
  298.0 3.0 copy-start.34
  298.0 3.1 copy-start.42
  298.0 3.4 copy-start.40
  298.0 4.0 copy-start.51
  302.0 2.7 copy-start.26
  304.4 1.6 copy-start.14
  304.4 1.6 copy-start.39
  304.4 1.6 copy-start.48
  304.7 6.2 slice-start.3
  306.0 4.9 slice-start.4
  306.0 4.9 slice-start.5
  310.9 6.8 %copy-start.27 = (bf16[2048,128]{1,0:T(8,128)(2,1)S(1)}, bf16[2048,128]{1,0:T(8,128)(2,1)}, u32[]{:S(2)}) copy-start(bf16[2048,128]{1,0:T(8,128)(2,1)} %param.20) | copy-start | bytes 1572868
  610.8 3.7 copy-start.2
  614.5 3.6 copy-start.6
  618.1 6.2 copy-start.37
  618.1 7.3 %slice-start = ((f32[3,384,2048]{2,1,0:T(8,128)}), f32[2,384,2048]{2,1,0:T(8,128)S(1)}, s32[]{:S(2)}) async-start(f32[3,384,2048]{2,1,0:T(8,128)} %copy-done.2), calls=%async_computation.1 | async-start | bytes 12582912 | tf_op jit(solution)/shard_map/slice | solution.py:1131
  625.4 4.2 copy-start.7
  629.6 4.8 copy-start.22
  634.3 2.3 copy-start.21
  634.3 3.7 copy-start.1
Sparse Core Ops, SparseCore 0:
  12.3 133.9 all-gather.2

commit v5 on v4

--- a/solution.py
+++ b/solution.py
@@ -38,19 +38,6 @@
         [
             first_half * cosine_table - second * sine_table,
             second * cosine_table + first_half * sine_table,
-        ],
-        axis=-1,
-    )
-
-
-def rotate_back(gradient, cosine_table, sine_table):
-    middle_index = gradient.shape[-1] // 2
-    first_half = gradient[..., :middle_index]
-    second = gradient[..., middle_index:]
-    return jnp.concatenate(
-        [
-            first_half * cosine_table + second * sine_table,
-            second * cosine_table - first_half * sine_table,
         ],
         axis=-1,
     )
@@ -640,11 +627,35 @@
     )(inputs, packs, weights, member, middle, gain.reshape(1, -1))
 
 
-def finish_sums_body(
+def back_through_head(grads, raw, gain, cosine, sine):
+    hat_grads = grads * cosine - pltpu.roll(grads, grads.shape[1] // 2, 1) * sine
+    inverse = lax.rsqrt(jnp.mean(raw * raw, axis=-1, keepdims=True) + EPSILON)
+    hat = raw * inverse
+    terms = hat_grads * hat
+    scaled = hat_grads * gain
+    back = inverse * (scaled - hat * jnp.mean(scaled * hat, axis=-1, keepdims=True))
+    return back.astype(jnp.bfloat16), terms
+
+
+def finish_layer_body(
     size,
-    qkv_ref,
-    out_ref,
+    gmid_low_ref,
+    out_weight_ref,
+    mixed_ref,
+    query_ref,
+    key_ref,
+    value_ref,
+    raw_query_ref,
+    raw_key_ref,
     normed_ref,
+    query_weight_ref,
+    key_weight_ref,
+    value_weight_ref,
+    cosine_ref,
+    sine_ref,
+    start_ref,
+    query_gain_ref,
+    key_gain_ref,
     middle_ref,
     token_ref,
     hidden_ref,
@@ -657,12 +668,21 @@
     gather_a,
     gather_b,
     gains_out,
+    qkv_ref,
+    out_ref,
     slots_a,
     slots_b,
+    grad_mixed,
+    grad_heads,
+    key_sums,
+    value_sums,
+    turned,
+    partial,
     from_partner,
     from_across,
     joined,
     totals,
+    head_totals,
     pair_gains,
     ring_gains,
     sems_a,
@@ -675,6 +695,11 @@
     own, partner, across = tensor_peers()
     far_partner = (partner + 2) % 4
     quarter, width = token_ref.shape
+    tokens = normed_ref.shape[0]
+    head_dim = key_ref.shape[1]
+    lead = query_ref.shape[1]
+    heads = lead // head_dim
+    scale = head_dim**-0.5
     place = ring_place(dp, size)
     forward = (ring_index(place + 1, size), own)
     backward = (ring_index(place + size - 1, size), own)
@@ -701,23 +726,6 @@
         return (value + 2 * size) % size
 
     live = {}
-
-    def reduce_send(step):
-        for which, (ref, slots, _, sems) in enumerate(sets):
-            for way, (device, sign) in enumerate(ways):
-                if step == 0:
-                    source = ref.at[block_of(ref, wrap(place - sign), way)]
-                else:
-                    add_own(which, way, step - 1)
-                    source = slots.at[way, step - 1]
-                live[which, way, step] = start(
-                    push(
-                        source,
-                        slots.at[way, step],
-                        (sems.at[0, way, step], sems.at[1, way, step]),
-                        device,
-                    )
-                )
 
     def add_own(which, way, step):
         ref, slots, blocks, _ = sets[which]
@@ -736,25 +744,27 @@
 
         row_loop(ref.shape[0] // size, 16, add)
 
-    gather = {}
-
-    def gather_send(step):
-        for which, (ref, _, blocks, sems) in enumerate(sets):
-            cut = ref.shape[1] // 2
-            for way, (device, sign) in enumerate(ways):
-                if step == 0:
-                    add_own(which, way, size - 2)
-                else:
-                    gather[which, way, step - 1].wait_recv()
-                source = blocks.at[wrap(place - sign * step), :, pl.ds(way * cut, cut)]
-                gather[which, way, step] = start(
-                    push(
-                        source,
-                        source,
-                        (sems.at[0, way, size - 1 + step], sems.at[1, way, size - 1 + step]),
-                        device,
-                    )
-                )
+    def ring_event(which, step):
+        ref, slots, blocks, sems = sets[which]
+        cut = ref.shape[1] // 2
+        for way, (device, sign) in enumerate(ways):
+            if step == 0:
+                source = ref.at[block_of(ref, wrap(place - sign), way)]
+            elif step < size:
+                add_own(which, way, step - 1)
+                source = slots.at[way, step - 1] if step < size - 1 else None
+            else:
+                live[which, way, step - 1].wait_recv()
+            if step >= 2 * size - 2:
+                continue
+            if step >= size - 1:
+                block = wrap(place - sign * (step - size + 1))
+                source = blocks.at[block, :, pl.ds(way * cut, cut)]
+                target = source
+            else:
+                target = slots.at[way, step]
+            sem = (sems.at[0, way, step], sems.at[1, way, step])
+            live[which, way, step] = start(push(source, target, sem, device))
 
     def part_rows(index):
         return pl.ds(pl.multiple_of(index * quarter, quarter), quarter)
@@ -762,37 +772,117 @@
     def side(index):
         return (side_sems.at[0, index], side_sems.at[1, index])
 
-    reduce_send(0)
-    first = start(
-        push(normed_ref.at[part_rows(far_partner)], from_partner.at[1], side(0), (dp, partner))
-    )
-    second = start(
-        push(normed_ref.at[part_rows(partner)], from_partner.at[0], side(1), (dp, partner))
-    )
     mine = part_rows(own)
-    crossing = start(push(cross_ref, crossed_ref, side(8), (dp, across)))
     home = own * quarter
+
+    step_rows = 2 * LANES
+    wide = 4 * LANES
+
+    def out_rows(index, carry):
+        rows = pl.ds(pl.multiple_of(index * step_rows, step_rows), step_rows)
+        turned[...] = mixed_ref[:, rows].T
+
+        def columns(tile, carry):
+            here = pl.ds(pl.multiple_of(tile * wide, wide), wide)
+            out_ref[rows, here] = matmul(turned[...], gmid_low_ref[:, here]).astype(bf)
+            return carry
+
+        return lax.fori_loop(0, width // wide, columns, carry)
+
+    lax.fori_loop(0, lead // step_rows, out_rows, 0)
+    ring_event(1, 0)
 
     def keep(rows):
         hidden_all[pl.ds(pl.multiple_of(home + rows.start, 16), rows.size), :] = hidden_ref[rows, :]
 
     row_loop(quarter, 16, keep)
-    spread = []
     shown = [start(push(hidden_ref, hidden_all.at[mine], side(9), (dp, across)))]
     shown.append(start(push(hidden_ref, hidden_all.at[mine], side(10), (dp, partner))))
-    reduce_send(1)
+
+    def mixed_columns(tile, carry):
+        here = pl.ds(pl.multiple_of(tile * wide, wide), wide)
+        grad_mixed[:, here] = matmul_nt(gmid_low_ref[...], out_weight_ref[here, :]).astype(bf)
+        return carry
+
+    lax.fori_loop(0, lead // wide, mixed_columns, 0)
+    key_sums[...] = jnp.zeros_like(key_sums)
+    value_sums[...] = jnp.zeros_like(value_sums)
+    head_totals[...] = jnp.zeros_like(head_totals)
+    block = tokens // 2
+
+    def do_head(head, carry):
+        lanes = pl.ds(pl.multiple_of(head * head_dim, head_dim), head_dim)
+        for part in (0, 1):
+            rows = pl.ds(part * block, block)
+            count = (part + 1) * block
+            keys = pl.ds(0, count)
+            queries = query_ref[rows, lanes]
+            outer = grad_mixed[rows, lanes]
+            scores = matmul_nt(key_ref[keys, :], queries)
+            key_at = lax.broadcasted_iota(jnp.int32, scores.shape, 0)
+            query_at = lax.broadcasted_iota(jnp.int32, scores.shape, 1) + part * block
+            seen = (key_at <= query_at) & (key_at >= start_ref[:, rows])
+            exponent = jnp.where(seen, jnp.exp(scores * scale), 0.0)
+            soft = exponent * (1.0 / jnp.sum(exponent, axis=0, keepdims=True))
+            grad_soft = matmul_nt(value_ref[keys, :], outer)
+            inner = jnp.sum(soft * grad_soft, axis=0, keepdims=True)
+            grad_scores = (soft * (grad_soft - inner)).astype(bf)
+            value_sums[keys, :] += matmul(soft.astype(bf), outer)
+            key_sums[keys, :] += matmul(grad_scores, queries)
+            grad_query = scale * lax.dot_general(
+                grad_scores, key_ref[keys, :], (((0,), (0,)), ((), ())), preferred_element_type=f32
+            )
+            low, terms = back_through_head(
+                grad_query, raw_query_ref[rows, lanes], query_gain_ref[...], cosine_ref[rows, :], sine_ref[rows, :]
+            )
+            grad_heads[rows, lanes] = low
+            head_totals[0] += jnp.sum(terms.reshape(-1, 8, head_dim), axis=0)
+        return carry
+
+    lax.fori_loop(0, heads // 2, do_head, 0)
+    ring_event(1, 1)
+    lax.fori_loop(heads // 2, heads, do_head, 0)
+    ring_event(1, 2)
+    low, terms = back_through_head(
+        scale * key_sums[...], raw_key_ref[...], key_gain_ref[...], cosine_ref[...], sine_ref[...]
+    )
+    grad_heads[:, pl.ds(lead, head_dim)] = low
+    head_totals[1] += jnp.sum(terms.reshape(-1, 8, head_dim), axis=0)
+    grad_heads[:, pl.ds(lead + head_dim, head_dim)] = value_sums[...].astype(bf)
+
+    def in_rows(index, carry):
+        rows = pl.ds(pl.multiple_of(index * step_rows, step_rows), step_rows)
+        turned[...] = normed_ref[:, rows].T
+        qkv_ref[rows, :] = matmul(turned[...], grad_heads[...]).astype(bf)
+        return carry
+
+    lax.fori_loop(0, width // step_rows, in_rows, 0)
+    ring_event(1, 3)
+    ring_event(0, 0)
+
+    def token_columns(tile, carry):
+        here = pl.ds(pl.multiple_of(tile * wide, wide), wide)
+        sums = matmul_nt(grad_heads[:, :lead], query_weight_ref[here, :])
+        sums = sums + matmul_nt(grad_heads[:, lead : lead + head_dim], key_weight_ref[here, :])
+        sums = sums + matmul_nt(grad_heads[:, lead + head_dim :], value_weight_ref[here, :])
+        partial[:, here] = sums.astype(bf)
+        return carry
+
+    lax.fori_loop(0, width // wide, token_columns, 0)
+    first = start(push(partial.at[part_rows(far_partner)], from_partner.at[1], side(0), (dp, partner)))
+    second = start(push(partial.at[part_rows(partner)], from_partner.at[0], side(1), (dp, partner)))
+    ring_event(1, 4)
     first.wait_recv()
     away = across * quarter
 
     def join(rows):
         there = pl.ds(pl.multiple_of(away + rows.start, 16), rows.size)
-        joined[rows, :] = (
-            normed_ref[there, :].astype(f32) + from_partner[1, rows, :].astype(f32)
-        ).astype(bf)
+        joined[rows, :] = (partial[there, :].astype(f32) + from_partner[1, rows, :].astype(f32)).astype(bf)
 
     row_loop(quarter, 16, join)
     third = start(push(joined, from_across, side(2), (dp, across)))
-    reduce_send(2)
+    ring_event(0, 1)
+    ring_event(1, 5)
     second.wait_recv()
     third.wait_recv()
     totals[...] = jnp.zeros_like(totals)
@@ -800,7 +890,7 @@
     def finish(rows):
         there = pl.ds(pl.multiple_of(home + rows.start, 16), rows.size)
         grads = (
-            normed_ref[there, :].astype(f32)
+            partial[there, :].astype(f32)
             + from_partner[0, rows, :].astype(f32)
             + from_across[rows, :].astype(f32)
         )
@@ -808,19 +898,21 @@
         inverse = lax.rsqrt(jnp.mean(hidden * hidden, axis=-1, keepdims=True) + EPSILON)
         hat = hidden * inverse
         product = grads * hat
-        totals[:, :width] += jnp.sum(product.reshape(-1, 8, width), axis=0)
+        totals[...] += product[:8] + product[8:]
         scaled = grads * gain_ref[...]
         back = inverse * (scaled - hat * jnp.mean(scaled * hat, axis=-1, keepdims=True))
-        joined_grad = (middle_ref[rows, :] + back).astype(bf)
-        grad_all[there, :] = joined_grad
+        grad_all[there, :] = (middle_ref[rows, :] + back).astype(bf)
 
     row_loop(quarter, 16, finish)
-    spread.append(start(push(grad_all.at[mine], grad_all.at[mine], side(3), (dp, across))))
+    spread = [start(push(grad_all.at[mine], grad_all.at[mine], side(3), (dp, across)))]
     spread.append(start(push(grad_all.at[mine], grad_all.at[mine], side(4), (dp, partner))))
-    pair_gains[0, :, :width] = jnp.sum(totals[:, :width], axis=0, keepdims=True)
-    pair_gains[0, :, width:] = gains_ref[...]
+    pair_gains[0, :, :width] = jnp.sum(totals[...], axis=0, keepdims=True)
+    pair_gains[0, :, width : 2 * width] = gains_ref[...]
+    pair_gains[0, :, 2 * width : 2 * width + head_dim] = jnp.sum(head_totals[0], axis=0, keepdims=True)
+    pair_gains[0, :, 2 * width + head_dim :] = jnp.sum(head_totals[1], axis=0, keepdims=True)
     swap = start(push(pair_gains.at[0], pair_gains.at[1], side(5), (dp, partner)))
-    reduce_send(3)
+    ring_event(0, 2)
+    ring_event(1, 6)
     far = part_rows(across)
     shown[0].wait_recv()
     shown.append(start(push(hidden_all.at[far], hidden_all.at[far], side(11), (dp, partner))))
@@ -829,22 +921,23 @@
     swap.wait_recv()
     pair_gains[2] = pair_gains[0] + pair_gains[1]
     swap = start(push(pair_gains.at[2], pair_gains.at[3], side(7), (dp, across)))
-    for step in range(4, size - 1):
-        reduce_send(step)
+    ring_event(0, 3)
+    ring_event(1, 7)
     swap.wait_recv()
+    crossing = start(push(cross_ref, crossed_ref, side(8), (dp, across)))
     ring_gains[place] = pair_gains[2] + pair_gains[3]
-    gather_send(0)
     small = None
-    for step in range(size - 1):
-        if small is not None:
-            small.wait_recv()
-        ref = ring_gains.at[wrap(place - step)]
-        small = start(push(ref, ref, (ring_sems.at[0, step], ring_sems.at[1, step]), forward))
-        if step > 0:
-            gather_send(step)
+    for step in range(4, 2 * size - 1):
+        ring_event(0, step)
+        if step + 4 < 2 * size - 1:
+            ring_event(1, step + 4)
+        if step - 4 < size - 1:
+            if small is not None:
+                small.wait_recv()
+            ref = ring_gains.at[wrap(place - step + 4)]
+            sem = (ring_sems.at[0, step - 4], ring_sems.at[1, step - 4])
+            small = start(push(ref, ref, sem, forward))
     small.wait_recv()
-    for copy in (gather[which, way, size - 2] for which in (0, 1) for way in (0, 1)):
-        copy.wait_recv()
     gains_out[...] = jnp.sum(ring_gains[...], axis=0)
     for copy in (spread[1], spread[2], shown[1], shown[2], crossing):
         copy.wait_recv()
@@ -852,37 +945,49 @@
         copy.wait_send()
 
 
-def finish_sums(
-    size, grad_in, grad_out, grad_normed, grad_middle, token_rows, hidden_rows, cross, gain, gains
-):
+def finish_layer(size, *arguments):
     bf, f32 = jnp.bfloat16, jnp.float32
+    (
+        _, out_weight, mixed, query, key, _, _, _, normed, query_weight, _, _, _, _, _, _, _, _, token_rows, _,
+        cross, _, _,
+    ) = arguments
     quarter, width = token_rows.shape
-    tokens = grad_normed.shape[0]
+    tokens = normed.shape[0]
+    lead, head_dim = query.shape[1], key.shape[1]
     vmem = pl.BlockSpec(memory_space=pltpu.VMEM)
     anywhere = pl.BlockSpec(memory_space=pl.ANY)
     dma = pltpu.SemaphoreType.DMA
-    rows_a, rows_b = grad_in.shape[0] // size, grad_out.shape[0] // size
-    cut_a, cut_b = grad_in.shape[1] // 2, grad_out.shape[1] // 2
-    count = width + gains.shape[1]
+    columns = lead + 2 * head_dim
+    rows_a, rows_b = width // size, lead // size
+    count = 2 * width + 2 * head_dim
     return pl.pallas_call(
-        functools.partial(finish_sums_body, size),
+        functools.partial(finish_layer_body, size),
         out_shape=(
             jax.ShapeDtypeStruct((tokens, width), bf),
             jax.ShapeDtypeStruct(cross.shape, bf),
             jax.ShapeDtypeStruct((tokens, width), bf),
-            jax.ShapeDtypeStruct((size, rows_a, 2 * cut_a), bf),
-            jax.ShapeDtypeStruct((size, rows_b, 2 * cut_b), bf),
+            jax.ShapeDtypeStruct((size, rows_a, columns), bf),
+            jax.ShapeDtypeStruct((size, rows_b, width), bf),
             jax.ShapeDtypeStruct((1, count), f32),
         ),
-        in_specs=[vmem] * 6 + [anywhere, vmem, vmem],
+        in_specs=[anywhere if argument is cross else vmem for argument in arguments],
         out_specs=(vmem, anywhere) + (vmem,) * 4,
         scratch_shapes=[
-            pltpu.VMEM((2, size - 1, rows_a, cut_a), bf),
-            pltpu.VMEM((2, size - 1, rows_b, cut_b), bf),
+            pltpu.VMEM((width, columns), bf),
+            pltpu.VMEM((lead, width), bf),
+            pltpu.VMEM((2, size - 1, rows_a, columns // 2), bf),
+            pltpu.VMEM((2, size - 1, rows_b, width // 2), bf),
+            pltpu.VMEM((tokens, lead), bf),
+            pltpu.VMEM((tokens, columns), bf),
+            pltpu.VMEM((tokens, head_dim), f32),
+            pltpu.VMEM((tokens, head_dim), f32),
+            pltpu.VMEM((2 * LANES, tokens), bf),
+            pltpu.VMEM((tokens, width), bf),
             pltpu.VMEM((2, quarter, width), bf),
             pltpu.VMEM((quarter, width), bf),
             pltpu.VMEM((quarter, width), bf),
             pltpu.VMEM((8, width), f32),
+            pltpu.VMEM((2, 8, head_dim), f32),
             pltpu.VMEM((4, 1, count), f32),
             pltpu.VMEM((size, 1, count), f32),
             dma((2, 2, 2 * size - 2)),
@@ -893,18 +998,8 @@
         compiler_params=pltpu.CompilerParams(
             collective_id=1, has_side_effects=True, vmem_limit_bytes=VMEM_LIMIT
         ),
-        name="finish_sums",
-    )(
-        grad_in,
-        grad_out,
-        grad_normed,
-        grad_middle,
-        token_rows,
-        hidden_rows,
-        cross,
-        gain.reshape(1, -1),
-        gains,
-    )
+        name="finish_layer",
+    )(*arguments)
 
 
 def large_experts(size, inputs, packs, all_weights, middle, gain, experts):
@@ -1028,7 +1123,7 @@
     )
     all_weights = lax.all_gather(own_weights, "tensor")
     hidden = hidden_in.astype(f32)
-    hat_one, inv_one = rms_parts(hidden)
+    hat_one, _ = rms_parts(hidden)
     normed = (hat_one * norm1_gain).astype(bf)
     query_proj = jnp.dot(normed, query_weight, preferred_element_type=f32).reshape(
         tokens, local_heads, head_dim
@@ -1037,17 +1132,16 @@
     value_low = jnp.dot(normed, value_weight, preferred_element_type=f32).astype(bf)
     places, starts = sequence_layout(seq_lens[0], tokens)
     cosine_table, sine_table = rotary_tables(places - starts, head_dim)
-    query_hat, query_inv = rms_parts(query_proj)
+    query_hat, _ = rms_parts(query_proj)
     query_low = rotate(
         query_hat * query_gain, cosine_table[:, None, :], sine_table[:, None, :]
     ).astype(bf)
-    key_hat, key_inv = rms_parts(key_proj)
+    key_hat, _ = rms_parts(key_proj)
     key_low = rotate(key_hat * key_gain, cosine_table, sine_table).astype(bf)
     visible = (places[None, :] <= places[:, None]) & (places[None, :] >= starts[:, None])
     scores = jnp.einsum("thd,sd->hts", query_low, key_low, preferred_element_type=f32) * score_scale
     exponent = jnp.where(visible[None], jnp.exp(scores), 0.0)
     totals = jnp.sum(exponent, axis=-1, keepdims=True)
-    log_totals = jnp.log(totals)
     soft_low = (exponent / totals).astype(bf)
     mixed_low = (
         jnp.einsum("hts,sd->thd", soft_low, value_low, preferred_element_type=f32)
@@ -1067,64 +1161,34 @@
         norm2_gain,
         experts,
     )
-    grad_gain_two = grad_gain_two.reshape(-1)
     joined = (kept[0].astype(f32) + given[1].astype(f32)).astype(bf)
-    grad_out_weight = jnp.einsum("ti,td->id", mixed_low, grad_mid_low, preferred_element_type=f32)
-    grad_mixed = (
-        jnp.einsum("td,id->ti", grad_mid_low, out_weight, preferred_element_type=f32)
-        .astype(bf)
-        .reshape(tokens, local_heads, head_dim)
-    )
-    scores_again = (
-        jnp.einsum("thd,sd->hts", query_low, key_low, preferred_element_type=f32) * score_scale
-    )
-    soft_again = jnp.where(visible[None], jnp.exp(scores_again - log_totals), 0.0)
-    grad_soft = jnp.einsum("thd,sd->hts", grad_mixed, value_low, preferred_element_type=f32)
-    grad_scores = (
-        soft_again * (grad_soft - jnp.sum(soft_again * grad_soft, axis=-1, keepdims=True))
-    ).astype(bf)
-    grad_values = jnp.einsum(
-        "hts,thd->sd", soft_again.astype(bf), grad_mixed, preferred_element_type=f32
-    ).astype(bf)
-    grad_query_rot = score_scale * jnp.einsum(
-        "hts,sd->thd", grad_scores, key_low, preferred_element_type=f32
-    )
-    grad_key_rot = score_scale * jnp.einsum(
-        "hts,thd->sd", grad_scores, query_low, preferred_element_type=f32
-    )
-    grad_query_norm = rotate_back(grad_query_rot, cosine_table[:, None, :], sine_table[:, None, :])
-    grad_query_gain = jnp.sum(grad_query_norm * query_hat, axis=(0, 1))
-    grad_query_low = (
-        rms_back(grad_query_norm * query_gain, query_hat, query_inv)
-        .reshape(tokens, local_heads * head_dim)
-        .astype(bf)
-    )
-    grad_key_norm = rotate_back(grad_key_rot, cosine_table, sine_table)
-    grad_key_gain = jnp.sum(grad_key_norm * key_hat, axis=0)
-    grad_key_low = rms_back(grad_key_norm * key_gain, key_hat, key_inv).astype(bf)
-    grad_all_low = jnp.concatenate([grad_query_low, grad_key_low, grad_values], axis=1)
-    grad_in_weights = jnp.einsum(
-        "ti,tj->ij", normed, grad_all_low, preferred_element_type=f32
-    ).astype(bf)
-    grad_normed_one = jnp.einsum("tj,ij->ti", grad_query_low, query_weight, preferred_element_type=f32)
-    grad_normed_one = grad_normed_one + jnp.einsum(
-        "tj,ij->ti", grad_key_low, key_weight, preferred_element_type=f32
-    )
-    grad_normed_one = grad_normed_one + jnp.einsum(
-        "tj,ij->ti", grad_values, value_weight, preferred_element_type=f32
-    )
-    gains = jnp.concatenate([grad_gain_two, grad_query_gain, grad_key_gain]).reshape(1, -1)
-    hidden_out, crossed, grad_hidden, in_low, out_low, gains = finish_sums(
+    both = jnp.concatenate([cosine_table, cosine_table], axis=1)
+    signed = jnp.concatenate([-sine_table, sine_table], axis=1)
+    hidden_out, crossed, grad_hidden, in_low, out_low, gains = finish_layer(
         data_size,
-        grad_in_weights,
-        grad_out_weight.astype(bf),
-        grad_normed_one.astype(bf),
+        grad_mid_low,
+        out_weight,
+        mixed_low,
+        query_low.reshape(tokens, -1),
+        key_low,
+        value_low,
+        query_proj.reshape(tokens, -1),
+        key_proj,
+        normed,
+        query_weight,
+        key_weight,
+        value_weight,
+        both,
+        signed,
+        starts.reshape(1, -1).astype(jnp.int32),
+        query_gain.reshape(1, -1),
+        key_gain.reshape(1, -1),
         grad_middle,
         hidden_q,
         hidden_out,
         joined,
-        norm1_gain,
-        gains,
+        norm1_gain.reshape(1, -1),
+        grad_gain_two.reshape(1, -1),
     )
     own_grads = kept[1].astype(f32) + given[0].astype(f32) + crossed.astype(f32)
     grad_w_gate_up = jnp.transpose(

time: 650 us -> 534 us (0.82)
  Pallas kernels: 502 us -> 425 us
  matrix products: 53.1 us -> 18.1 us
  local copies, waits for them, and re-layouts: 30.3 us -> 23.2 us
    pallas_call x1, Pallas kernels: 283 us -> 206 us  [finish_layer(): pl.pallas_call(functools.partial(finish_layer_body, size), out_shape=(jax...]
    dot_general x10 -> x0, matrix products: 29.4 us -> none  [the longest x1 5.23 us: local(): jnp.einsum('td,id->ti', grad_mid_low, out_weight, preferred_element_type=...]
    unnamed x125 -> x48, local copies, waits for them, and re-layouts: 16.1 us -> 8.66 us
  transfers between devices with their start and end apart: 1 -> 1, of which waited for: 0 -> 0; matrix products, arithmetic and copies ran while one was open for 6% -> 7% of each run, Pallas kernels for 17% -> 21%
where the time goes in v5:
time: 534 us; the launch traced here: 528 us
  Pallas kernels  425 us (80%)
  other arithmetic  46.9 us (9%)
  local copies, waits for them, and re-layouts  23.2 us (4%)
  matrix products  18.1 us (3%)
  between operations  14.9 us (3%)
    pallas_call x1, Pallas kernels, finish_layer(): pl.pallas_call(functools.partial(finish_layer_body, size), out_shape=(jax...  206 us
    pallas_call x1, Pallas kernels, run_experts(): pl.pallas_call(functools.partial(run_experts_body, size, local_experts, e...  110 us
    pallas_call x1, Pallas kernels, exchange_tokens(): pl.pallas_call(functools.partial(exchange_tokens_body, size), out_shape=(...  109 us
  transfers between devices with their start and end apart: 1, of which 0 were waited for; matrix products, arithmetic and copies ran while one was open for 7% of the time, Pallas kernels for 21%

profile of v5, /device:TPU:0, one launch (start us, length us, event | category | flops | bytes accessed | tf_op | source)
XLA Modules:
  0.0 528.4 jit_solution(17443362195516018609)
XLA Ops:
  7.2 0.0 copy-start
  7.2 0.0 all-gather.3.cloned.1.call-start
  7.3 2.2 copy.76
  9.5 0.1 copy-done.14
  9.6 2.6 pad_maximum_fusion
  12.2 0.0 all-gather.3.cloned.1.call-update
  12.2 0.0 copy-start.11
  12.2 0.8 constant_dynamic-slice_fusion
  13.1 0.1 copy.73
  13.2 0.1 copy.75
  13.3 0.1 copy.74
  13.4 0.0 copy-done.21
  13.4 0.2 reduce-window.8
  13.6 0.1 copy-done.5
  13.8 0.5 fusion.2
  14.3 2.1 fusion.4.normed_ref
  16.4 0.0 copy-done.11
  16.4 0.0 copy-start.2
  16.4 0.8 multiply_reduce_fusion.1
  17.3 0.1 copy.68.raw_key_ref
  17.4 4.6 fusion.27.raw_query_ref
  22.0 0.0 copy-start.3
  22.0 0.0 copy-start.19
  22.1 1.3 copy-done.3
  23.4 0.5 copy.84
  23.8 0.0 copy-start.20
  23.8 0.6 multiply_reduce_fusion
  24.5 0.1 copy.69
  24.6 0.1 select_reduce_fusion.1
  24.7 0.1 multiply_multiply_fusion
  24.8 2.0 fusion.9
  26.9 0.1 pad_maximum_fusion.3.key_ref
  27.0 0.1 fusion.8
  27.2 1.8 fusion.26.value_ref
  29.0 0.7 fusion.6
  29.8 0.8 multiply_subtract_fusion
  30.5 0.0 copy-start.7
  30.6 0.0 copy-start.8
  30.6 2.6 fusion
  33.2 2.4 fusion.7
  35.6 1.3 copy.81.mixed_ref
  36.9 2.1 constant_dynamic-slice_fusion.2
  39.0 1.0 concatenate.21.pack_ref
  40.0 5.9 %convolution_convert_fusion.part_ref = bf16[512,2048]{1,0:T(8,128)(2,1)} fusion(bf16[512,1024]{0,1:T(8,128)(2,1)S(1)} %bitcast.89, bf16[1024,2048]{1,0:T(8,128)(2,1)} %out_weight_ref.1), kind=kOutput, calls=%fused_computation.16 | convolution fusion | flops 2148532224 | bytes 7340032 | tf_op jit(solution)/shard_map/dot_general | solution.py:1152
  45.8 109.5 %exchange_tokens.1 = (f32[128,2048]{1,0:T(8,128)}, bf16[8,128,2048]{2,1,0:T(8,128)(2,1)}, bf16[8,128,2176]{2,1,0:T(8,128)(2,1)}) custom-call(bf16[512,2048]{1,0:T(8,128)(2,1)} %convolution_convert_fusion.part_ref, bf16[128,2048]{1,0:T(8,128)(2,1)} %get-tuple-element.64.token_ref, bf16[128,2176]{1,0:T(8,128)(2,1)} %concatenate.21.pack_ref, f32[1,2048]{1,0:T(1,128)} %bitcast.90), custom_call_target="tpu_custom_call" | custom-call | tf_op jit(solution)/shard_map/exchange_tokens/pallas_call | solution.py:241
  155.3 2.1 pad_maximum_fusion.1
  157.4 3.1 copy_bitcast_fusion.1.query_ref
  160.5 0.6 compare_convert_fusion.member_ref
  161.1 110.1 %run_experts.1 = (bf16[128,2048]{1,0:T(8,128)(2,1)}, bf16[2,3,384,2048]{3,2,1,0:T(8,128)(2,1)}, bf16[2,3,384,2048]{3,2,1,0:T(8,128)(2,1)}, f32[128,2048]{1,0:T(8...) custom-call(bf16[1024,2048]{1,0:T(8,128)(2,1)} %bitcast.85, bf16[1024,2176]{1,0:T(8,128)(2,1)} %bitcast.84, ...), custom_call_target="tpu_custom_call" | custom-call | tf_op jit(solution)/shard_map/run_experts/pallas_call | solution.py:594
  271.2 8.6 %fusion.1.cross_ref = bf16[3,384,2048]{2,1,0:T(8,128)(2,1)} fusion(bf16[2,3,384,2048]{3,2,1,0:T(8,128)(2,1)} %get-tuple-element.34, bf16[2,3,384,2048]{3,2,1,0:T(8,128)(2,1)} %get-tuple-element.33), kind=kLoop, calls=%fused_computation.8 | loop fusion | flops 9437184 | bytes 14155776 | tf_op jit(solution)/shard_map/convert_element_type | solution.py:1164
  279.8 205.7 %finish_layer.1 = (bf16[512,2048]{1,0:T(8,128)(2,1)}, bf16[3,384,2048]{2,1,0:T(8,128)(2,1)}, bf16[512,2048]{1,0:T(8,128)(2,1)}, bf16[8,256,1280]{2,1,0:T(8,128)(...) custom-call(bf16[512,2048]{1,0:T(8,128)(2,1)} %get-tuple-element.30.gmid_low_ref, ...), custom_call_target="tpu_custom_call" | custom-call | tf_op jit(solution)/shard_map/finish_layer/pallas_call | solution.py:963
  485.5 1.2 slice_bitcast_fusion
  486.7 1.3 fusion.24
  488.0 2.7 slice_convert_fusion.1
  490.7 6.6 %slice_convert_fusion = f32[2048,1024]{1,0:T(8,128)} fusion(bf16[2048,1280]{1,0:T(8,128)(2,1)} %bitcast.83), kind=kLoop, calls=%fused_computation.13 | loop fusion | flops 2097152 | bytes 12582912 | tf_op jit(solution)/shard_map/convert_element_type | solution.py:1205
  497.3 8.4 %bitcast_add_fusion = f32[3,384,2048]{2,1,0:T(8,128)S(1)} fusion(bf16[3,384,2048]{2,1,0:T(8,128)(2,1)} %get-tuple-element.41, bf16[2,3,384,2048]{3,2,1,0:T(8,128)(2,1)} %get-tuple-element.34, bf16[2,3,384,2048]{3,2,1,0:T(8,128)(2,1)} %get-tuple-element.33), kind=kLoop, calls=%fused_computation | loop fusion | flops 11796480 | bytes 23592960 | tf_op jit(solution)/shard_map/add | solution.py:1193
  505.8 2.0 slice.92
  507.8 0.7 slice.91
  508.5 3.5 copy.88
  512.0 0.7 copy-done.6
  512.7 4.7 bitcast_convert_fusion
  517.5 1.3 copy.91
  518.8 1.0 copy-done.12
  519.8 1.3 copy.92
  (41 shorter events, 0.2 us)
Async XLA Ops:
  7.2 5.0 copy-start
  7.2 2.4 copy-start.14
  7.2 153.9 %all-gather.3.cloned.1.call-start = ((), (), s32[]{:S(2)}) async-start(), calls=%async_computation | async-start | bytes 23592960 | tf_op jit(solution)/shard_map/all_gather | solution.py:1124
  12.1 1.3 copy-start.21
  12.1 1.6 copy-start.5
  12.2 2.1 copy-start.17
  12.2 4.2 copy-start.11
  16.4 10.7 %copy-start.2 = (bf16[512,2048]{1,0:T(8,128)(2,1)}, bf16[512,2048]{1,0:T(8,128)(2,1)S(1)}, u32[]{:S(2)}) copy-start(bf16[512,2048]{1,0:T(8,128)(2,1)S(1)} %fusion.4.normed_ref) | copy-start | bytes 6291460
  17.4 7.3 %copy-start.9 = (f32[512,128]{1,0:T(8,128)}, f32[512,128]{1,0:T(8,128)S(1)}, u32[]{:S(2)}) copy-start(f32[512,128]{1,0:T(8,128)S(1)} %copy.68.raw_key_ref) | copy-start | bytes 786436
  22.0 1.3 copy-start.3
  22.0 2.6 copy-start.19
  23.8 5.2 copy-start.20
  24.5 4.5 copy-start.4
  24.7 5.1 copy-start.18
  26.9 3.7 copy-start.10
  27.0 3.6 copy-start.15
  29.0 4.1 copy-start.16
  30.5 2.6 copy-start.7
  30.6 2.6 copy-start.8
  508.5 4.2 copy-start.6
  512.7 4.8 copy-start.13
  517.5 2.3 copy-start.12
  517.5 3.7 copy-start.1
Sparse Core Ops, SparseCore 0:
  12.3 133.9 all-gather.2

commit v6 on v5

--- a/solution.py
+++ b/solution.py
@@ -28,19 +28,6 @@
     inverse = jnp.exp(halves * (-2.0 * math.log(ROPE_BASE) / head_dim))
     angles = positions.astype(jnp.float32)[:, None] * inverse[None, :]
     return (jnp.cos(angles), jnp.sin(angles))
-
-
-def rotate(values, cosine_table, sine_table):
-    middle_index = values.shape[-1] // 2
-    first_half = values[..., :middle_index]
-    second = values[..., middle_index:]
-    return jnp.concatenate(
-        [
-            first_half * cosine_table - second * sine_table,
-            second * cosine_table + first_half * sine_table,
-        ],
-        axis=-1,
-    )
 
 
 def sequence_layout(lengths, token_count):
@@ -148,31 +135,237 @@
     lax.fori_loop(0, total // rows, run, 0)
 
 
-def exchange_tokens_body(
+def matmul_nt(left, right):
+    return lax.dot_general(left, right, (((1,), (1,)), ((), ())), preferred_element_type=jnp.float32)
+
+
+def matmul(left, right):
+    return lax.dot_general(left, right, (((1,), (0,)), ((), ())), preferred_element_type=jnp.float32)
+
+
+def rms_rows(values):
+    return lax.rsqrt(jnp.mean(values * values, axis=-1, keepdims=True) + EPSILON)
+
+
+def turn(values, cosine, sine):
+    return values * cosine + pltpu.roll(values, values.shape[1] // 2, 1) * sine
+
+
+def start_layer_body(
     size,
-    part_ref,
+    experts,
     token_ref,
-    pack_ref,
-    gain_ref,
+    above_ref,
+    route_ref,
+    share_ref,
+    query_weight_ref,
+    key_weight_ref,
+    value_weight_ref,
+    out_weight_ref,
+    gate_up_ref,
+    down_ref,
+    cosine_ref,
+    sine_ref,
+    start_ref,
+    first_gain_ref,
+    second_gain_ref,
+    query_gain_ref,
+    key_gain_ref,
     middle_ref,
     inputs_ref,
     packs_ref,
+    others_ref,
+    mixed_ref,
+    query_ref,
+    key_ref,
+    value_ref,
+    raw_query_ref,
+    raw_key_ref,
+    normed_ref,
+    query_weight,
+    key_weight,
+    value_weight,
+    out_weight,
+    part_ref,
     from_partner,
     from_across,
     joined,
     ring_sems,
     pack_sems,
     side_sems,
-    local_sem,
+    load_sems,
+    near_sems,
+    far_sems,
+    pass_sems,
 ):
-    f32 = jnp.float32
+    f32, bf = jnp.float32, jnp.bfloat16
     dp = lax.axis_index("dp")
     own, partner, across = tensor_peers()
     far_partner = (partner + 2) % 4
-    quarter = token_ref.shape[0]
+    quarter, width = middle_ref.shape
+    tokens = token_ref.shape[0]
+    head_dim = key_ref.shape[1]
+    lead = query_ref.shape[1]
+    heads = lead // head_dim
     place = ring_place(dp, size)
+    loads = []
+    for index, (source, target) in enumerate(
+        (
+            (query_weight_ref, query_weight),
+            (key_weight_ref, key_weight),
+            (value_weight_ref, value_weight),
+            (out_weight_ref, out_weight),
+        )
+    ):
+        copy = pltpu.make_async_copy(source, target, load_sems.at[index])
+        copy.start()
+        loads.append(copy)
+    mine = pl.ds(pl.multiple_of(own * quarter, quarter), quarter)
+    base = own * quarter
+    above = pltpu.make_async_copy(
+        above_ref.at[mine], packs_ref.at[size - 1, :, pl.ds(0, width)], load_sems.at[4]
+    )
+    above.start()
     neighbours = [(ring_index(place + 1, size), own), (ring_index(place + size - 1, size), own)]
     greet(neighbours + [(dp, partner), (dp, across)])
+
+    halves = 2
+    pieces = []
+    for kind in range(3):
+        for expert in range(gate_up_ref.shape[0]):
+            for half in range(halves):
+                pieces.append((kind, expert, half))
+    span = gate_up_ref.shape[2] // halves
+
+    def piece_of(number):
+        kind, expert, half = pieces[number]
+        rows = pl.ds(half * span, span)
+        source = gate_up_ref.at[expert, kind, rows] if kind < 2 else down_ref.at[expert, rows]
+        return source, (kind, expert, rows)
+
+    near = []
+    for kind in range(3):
+        for expert in range(gate_up_ref.shape[0]):
+            number = len(near)
+            source = gate_up_ref.at[expert, kind] if kind < 2 else down_ref.at[expert]
+            copy = push(
+                source,
+                others_ref.at[0, kind, expert],
+                (near_sems.at[0, number], near_sems.at[1, number]),
+                (dp, partner),
+            )
+            copy.start()
+            near.append(copy)
+    far, passed = [], []
+
+    def pump(passing=True):
+        number = len(far)
+        if number >= 2:
+            old = far[number - 2]
+            if number - 2 < len(pieces):
+                old.wait_recv()
+                kind, expert, rows = piece_of(number - 2)[1]
+                copy = push(
+                    others_ref.at[1, kind, expert, rows],
+                    others_ref.at[2, kind, expert, rows],
+                    (pass_sems.at[0, number - 2], pass_sems.at[1, number - 2]),
+                    (dp, partner),
+                )
+                copy.start()
+                passed.append(copy)
+                old.wait_send()
+        if number < len(pieces):
+            source, (kind, expert, rows) = piece_of(number)
+            copy = push(
+                source,
+                others_ref.at[1, kind, expert, rows],
+                (far_sems.at[0, number], far_sems.at[1, number]),
+                (dp, across),
+            )
+            copy.start()
+            far.append(copy)
+        else:
+            far.append(None)
+
+    pump()
+    pump()
+
+    tail = packs_ref.shape[2] - width
+    lane = lax.broadcasted_iota(jnp.int32, (quarter, tail), 1)
+    name = jnp.where(lane < experts, lane, lane - experts)
+    dense = jnp.zeros((quarter, tail), f32)
+    for choice in range(route_ref.shape[1]):
+        named = route_ref[mine, choice : choice + 1]
+        dense = dense + jnp.where(named == name, share_ref[mine, choice : choice + 1], 0.0)
+    high = dense.astype(bf)
+    low = (dense - high.astype(f32)).astype(bf)
+    packs_ref[size - 1, :, width:] = jnp.where(
+        lane < experts, high.astype(f32), jnp.where(lane < 2 * experts, low.astype(f32), 0.0)
+    ).astype(bf)
+    above.wait()
+    packs = GatherRing(size, packs_ref, pack_sems)
+    packs.send(0)
+
+    def norm_first(rows):
+        hidden = token_ref[rows, :].astype(f32)
+        normed_ref[rows, :] = (hidden * rms_rows(hidden) * first_gain_ref[...]).astype(bf)
+
+    row_loop(tokens, 16, norm_first)
+    loads[0].wait()
+    wide = 4 * LANES
+
+    def project(tile, carry):
+        here = pl.ds(pl.multiple_of(tile * wide, wide), wide)
+        raw_query_ref[:, here] = matmul(normed_ref[...], query_weight[:, here])
+        return carry
+
+    lax.fori_loop(0, lead // wide, project, 0)
+    loads[1].wait()
+    loads[2].wait()
+    raw_key = matmul(normed_ref[...], key_weight[...])
+    raw_key_ref[...] = raw_key
+    key_ref[...] = turn(
+        raw_key * rms_rows(raw_key) * key_gain_ref[...], cosine_ref[...], sine_ref[...]
+    ).astype(bf)
+    value_ref[...] = matmul(normed_ref[...], value_weight[...]).astype(bf)
+    packs.step(0)
+    scale = head_dim**-0.5
+    block = tokens // 2
+
+    def do_head(head, carry):
+        lanes = pl.ds(pl.multiple_of(head * head_dim, head_dim), head_dim)
+        for part in (0, 1):
+            rows = pl.ds(part * block, block)
+            keys = pl.ds(0, (part + 1) * block)
+            raw = raw_query_ref[rows, lanes]
+            queries = turn(
+                raw * rms_rows(raw) * query_gain_ref[...], cosine_ref[rows, :], sine_ref[rows, :]
+            ).astype(bf)
+            query_ref[rows, lanes] = queries
+            scores = matmul_nt(key_ref[keys, :], queries)
+            key_at = lax.broadcasted_iota(jnp.int32, scores.shape, 0)
+            query_at = lax.broadcasted_iota(jnp.int32, scores.shape, 1) + part * block
+            seen = (key_at <= query_at) & (key_at >= start_ref[:, rows])
+            exponent = jnp.where(seen, jnp.exp(scores * scale), 0.0)
+            soft = (exponent * (1.0 / jnp.sum(exponent, axis=0, keepdims=True))).astype(bf)
+            mixed_ref[rows, lanes] = lax.dot_general(
+                soft, value_ref[keys, :], (((0,), (0,)), ((), ())), preferred_element_type=f32
+            ).astype(bf)
+        return carry
+
+    lax.fori_loop(0, heads // 2, do_head, 0)
+    packs.step(1)
+    pump()
+    lax.fori_loop(heads // 2, heads, do_head, 0)
+    packs.step(2)
+    loads[3].wait()
+
+    def share(tile, carry):
+        here = pl.ds(pl.multiple_of(tile * wide, wide), wide)
+        part_ref[:, here] = matmul(mixed_ref[...], out_weight[:, here]).astype(bf)
+        return carry
+
+    lax.fori_loop(0, width // wide, share, 0)
 
     def part_rows(index):
         return pl.ds(pl.multiple_of(index * quarter, quarter), quarter)
@@ -184,91 +377,101 @@
     second = push(part_ref.at[part_rows(partner)], from_partner.at[0], side(1), (dp, partner))
     first.start()
     second.start()
-    keep = pltpu.make_async_copy(pack_ref, packs_ref.at[size - 1], local_sem)
-    keep.start()
-    keep.wait()
-    packs = GatherRing(size, packs_ref, pack_sems)
-    packs.send(0)
+    packs.step(3)
     first.wait_recv()
-    base = across * quarter
+    away = across * quarter
 
     def join(rows):
-        there = pl.ds(pl.multiple_of(base + rows.start, 16), rows.size)
-        joined[rows, :] = (
-            part_ref[there, :].astype(f32) + from_partner[1, rows, :].astype(f32)
-        ).astype(jnp.bfloat16)
+        there = pl.ds(pl.multiple_of(away + rows.start, 16), rows.size)
+        joined[rows, :] = (part_ref[there, :].astype(f32) + from_partner[1, rows, :].astype(f32)).astype(bf)
 
     row_loop(quarter, 16, join)
     third = push(joined, from_across, side(2), (dp, across))
     third.start()
-    packs.step(0)
+    pump()
     second.wait_recv()
     third.wait_recv()
-    mine = own * quarter
-
-    def norm(rows):
-        there = pl.ds(pl.multiple_of(mine + rows.start, 16), rows.size)
+
+    def norm_second(rows):
+        there = pl.ds(pl.multiple_of(base + rows.start, 16), rows.size)
         middle = (
-            token_ref[rows, :].astype(f32)
+            token_ref[there, :].astype(f32)
             + part_ref[there, :].astype(f32)
             + from_partner[0, rows, :].astype(f32)
             + from_across[rows, :].astype(f32)
         )
         middle_ref[rows, :] = middle
-        inverse = lax.rsqrt(jnp.mean(middle * middle, axis=-1, keepdims=True) + EPSILON)
-        inputs_ref[size - 1, rows, :] = (middle * inverse * gain_ref[...]).astype(jnp.bfloat16)
-
-    row_loop(quarter, 16, norm)
-    tokens = GatherRing(size, inputs_ref, ring_sems)
-    tokens.send(0)
-    for step in range(1, size - 1):
-        packs.step(step)
-        tokens.step(step - 1)
-    tokens.step(size - 2)
+        inputs_ref[size - 1, rows, :] = (middle * rms_rows(middle) * second_gain_ref[...]).astype(bf)
+
+    row_loop(quarter, 16, norm_second)
+    ring = GatherRing(size, inputs_ref, ring_sems)
+    ring.send(0)
+    for step in range(size - 1):
+        if step + 4 < size - 1:
+            packs.step(step + 4)
+        pump()
+        ring.step(step)
+    while len(far) < len(pieces) + 2:
+        pump()
     packs.finish()
-    tokens.finish()
+    ring.finish()
     first.wait_send()
     second.wait_send()
     third.wait_send()
-
-
-def exchange_tokens(size, partial, token_rows, packed, gain):
-    quarter, width = token_rows.shape
-    columns = packed.shape[1]
-    bf = jnp.bfloat16
+    for copy in near + passed:
+        copy.wait()
+
+
+def start_layer(size, experts, *arguments):
+    tokens_rows, _, _, _, query_weight, key_weight, value_weight, out_weight, gate_up = arguments[:9]
+    bf, f32 = jnp.bfloat16, jnp.float32
+    tokens, width = tokens_rows.shape
+    quarter = tokens // 4
+    lead, head_dim = query_weight.shape[1], key_weight.shape[1]
+    columns = width + -(-2 * experts // LANES) * LANES
+    local, _, units, _ = gate_up.shape
     vmem = pl.BlockSpec(memory_space=pltpu.VMEM)
+    anywhere = pl.BlockSpec(memory_space=pl.ANY)
     dma = pltpu.SemaphoreType.DMA
     return pl.pallas_call(
-        functools.partial(exchange_tokens_body, size),
+        functools.partial(start_layer_body, size, experts),
         out_shape=(
-            jax.ShapeDtypeStruct((quarter, width), jnp.float32),
+            jax.ShapeDtypeStruct((quarter, width), f32),
             jax.ShapeDtypeStruct((size, quarter, width), bf),
             jax.ShapeDtypeStruct((size, quarter, columns), bf),
+            jax.ShapeDtypeStruct((3, 3, local, units, width), bf),
+            jax.ShapeDtypeStruct((tokens, lead), bf),
+            jax.ShapeDtypeStruct((tokens, lead), bf),
+            jax.ShapeDtypeStruct((tokens, head_dim), bf),
+            jax.ShapeDtypeStruct((tokens, head_dim), bf),
+            jax.ShapeDtypeStruct((tokens, lead), f32),
+            jax.ShapeDtypeStruct((tokens, head_dim), f32),
+            jax.ShapeDtypeStruct((tokens, width), bf),
         ),
-        in_specs=[vmem] * 4,
-        out_specs=(vmem,) * 3,
+        in_specs=[vmem, anywhere, vmem, vmem] + [anywhere] * 6 + [vmem] * 7,
+        out_specs=(vmem, vmem, vmem, anywhere) + (vmem,) * 7,
         scratch_shapes=[
+            pltpu.VMEM(query_weight.shape, bf),
+            pltpu.VMEM(key_weight.shape, bf),
+            pltpu.VMEM(value_weight.shape, bf),
+            pltpu.VMEM(out_weight.shape, bf),
+            pltpu.VMEM((tokens, width), bf),
             pltpu.VMEM((2, quarter, width), bf),
             pltpu.VMEM((quarter, width), bf),
             pltpu.VMEM((quarter, width), bf),
             dma((2, 2, size - 1, 2)),
             dma((2, 2, size - 1, 2)),
             dma((2, 3)),
-            dma(()),
+            dma((5,)),
+            dma((2, 3 * local)),
+            dma((2, 6 * local)),
+            dma((2, 6 * local)),
         ],
         compiler_params=pltpu.CompilerParams(
             collective_id=0, has_side_effects=True, vmem_limit_bytes=VMEM_LIMIT
         ),
-        name="exchange_tokens",
-    )(partial, token_rows, packed, gain.reshape(1, -1))
-
-
-def matmul_nt(left, right):
-    return lax.dot_general(left, right, (((1,), (1,)), ((), ())), preferred_element_type=jnp.float32)
-
-
-def matmul(left, right):
-    return lax.dot_general(left, right, (((1,), (0,)), ((), ())), preferred_element_type=jnp.float32)
+        name="start_layer",
+    )(*arguments)
 
 
 def run_experts_body(
@@ -277,7 +480,9 @@
     experts,
     inputs_ref,
     packs_ref,
-    weights_ref,
+    gate_up_ref,
+    down_ref,
+    others_ref,
     member_ref,
     middle_ref,
     gain_ref,
@@ -311,7 +516,7 @@
     pair = 2 * quarter
     half = size // 2
     units = weights.shape[1]
-    members = weights_ref.shape[0]
+    members = others_ref.shape[0] + 1
     span = units // members
     cut = width // 2
     wide = 512
@@ -319,16 +524,24 @@
     forward = (ring_index(place + 1, size), own)
     backward = (ring_index(place + size - 1, size), own)
     greet([forward, backward, (dp, partner), (dp, across)])
-    pieces = units // LANES
-    each = pieces // members
-
-    def load(piece):
-        source = weights_ref.at[piece // each, :, pl.ds((piece % each) * LANES, LANES), :]
-        target = weights.at[:, pl.ds(piece * LANES, LANES), :]
-        return pltpu.make_async_copy(source, target, load_sems.at[piece])
-
-    for piece in range(pieces):
-        load(piece).start()
+    part_units = span // local_experts
+    loads = []
+    for expert in range(local_experts):
+        rows = pl.ds(expert * part_units, part_units)
+        for kind in range(3):
+            source = gate_up_ref.at[expert, kind] if kind < 2 else down_ref.at[expert]
+            loads.append((expert * part_units, source, weights.at[kind, rows]))
+    for other in range(members - 1):
+        for first in range(0, span, LANES):
+            at = (other + 1) * span + first
+            source = others_ref.at[other, :, pl.ds(first, LANES)]
+            loads.append((at, source, weights.at[:, pl.ds(at, LANES)]))
+    loads = [
+        (at, pltpu.make_async_copy(source, target, load_sems.at[number]))
+        for number, (at, source, target) in enumerate(loads)
+    ]
+    for _, copy in loads:
+        copy.start()
 
     grad_ring = (grad_parts, grad_slots, grad_sems)
     mix_ring = (mix_parts, mix_slots, mix_sems)
@@ -374,10 +587,13 @@
         def do_units(tile, carry):
             here = pl.ds(pl.multiple_of(tile * wide, wide), wide)
 
-            @pl.when(index == 0)
-            def _():
-                for piece in range(wide // LANES):
-                    load(tile * (wide // LANES) + piece).wait()
+            for number in range(units // wide):
+
+                @pl.when((index == 0) & (tile == number))
+                def _():
+                    for at, copy in loads:
+                        if at // wide == number:
+                            copy.wait()
 
             scale = shares[0] * member_ref[0:1, here]
             for expert in range(1, local_experts):
@@ -429,8 +645,6 @@
         return carry
 
     lax.fori_loop(0, half, do_pair, 0)
-    far_partner = (partner + 2) % 4
-
     def keep(index, slot):
         target = kept_ref.at[index % members - 2, index // members]
         return pltpu.make_async_copy(stage.at[slot], target, store_sems.at[slot])
@@ -447,7 +661,7 @@
             kind = index // members
             whose = index % members
             slot = index % 2
-            member = jnp.where(whose < 2, partner + 2 * whose, own + 2 * (3 - whose)) % members
+            member = jnp.where(whose < 2, 1 + 2 * whose, 2 * (3 - whose))
 
             @pl.when((index >= 2) & (whose < 2))
             def _():
@@ -579,10 +793,11 @@
                 ring_copy(ring, way, step, ring[1].at[way, step]).wait_send()
 
 
-def run_experts(size, inputs, packs, weights, middle, gain, experts):
+def run_experts(size, inputs, packs, gate_up, down, others, middle, gain, experts):
     bf, f32 = jnp.bfloat16, jnp.float32
-    members, _, span, width = weights.shape
-    local_experts = experts // size
+    local_experts, _, part_units, width = gate_up.shape
+    others = others.reshape(3, 3, local_experts * part_units, width)
+    members, span = 4, local_experts * part_units
     rows = inputs.shape[0]
     quarter = rows // size
     units = members * span
@@ -601,7 +816,7 @@
             jax.ShapeDtypeStruct((members * quarter, width), bf),
             jax.ShapeDtypeStruct((1, width), f32),
         ),
-        in_specs=[vmem, vmem, anywhere, vmem, vmem, vmem],
+        in_specs=[vmem, vmem, anywhere, anywhere, anywhere, vmem, vmem, vmem],
         out_specs=(vmem, anywhere, anywhere, vmem, vmem, vmem),
         scratch_shapes=[
             pltpu.VMEM((3, units, width), bf),
@@ -613,7 +828,7 @@
             pltpu.VMEM((span, rows), bf),
             pltpu.VMEM((2, span, width), bf),
             pltpu.VMEM((8, width), f32),
-            dma((units // LANES,)),
+            dma((3 * local_experts + 3 * span // LANES,)),
             dma((2, 2, size - 1)),
             dma((2, 2, size - 1)),
             dma((2, 3)),
@@ -624,7 +839,7 @@
             collective_id=2, has_side_effects=True, vmem_limit_bytes=VMEM_LIMIT
         ),
         name="run_experts",
-    )(inputs, packs, weights, member, middle, gain.reshape(1, -1))
+    )(inputs, packs, gate_up, down, others, member, middle, gain.reshape(1, -1))
 
 
 def back_through_head(grads, raw, gain, cosine, sine):
@@ -1002,9 +1217,15 @@
     )(*arguments)
 
 
-def large_experts(size, inputs, packs, all_weights, middle, gain, experts):
+def large_experts(size, inputs, packs, gate_up, down, others, middle, gain, experts):
     f32, bf = jnp.float32, jnp.bfloat16
-    members, _, units, model_width = all_weights.shape
+    model_width = inputs.shape[1]
+    own_weights = jnp.stack([gate_up[:, 0], gate_up[:, 1], down])
+    all_weights = jnp.concatenate([own_weights[None], others])
+    members = all_weights.shape[0]
+    order = jnp.arange(members, dtype=jnp.int32) ^ lax.axis_index("tensor")
+    all_weights = all_weights.reshape(members, 3, -1, model_width)[order]
+    units = all_weights.shape[2]
     local_experts = experts // size
     indices = jnp.arange(size, dtype=jnp.int32)
     half = size // 2
@@ -1090,97 +1311,80 @@
     local_experts = w_gate_up.shape[0]
     hidden_part = w_gate_up.shape[3]
     head_dim = query_gain.shape[0]
-    local_heads = query_weight.shape[1] // head_dim
     data_size = lax.axis_size("dp")
-    tensor_size = lax.axis_size("tensor")
-    quarter = tokens // tensor_size
+    quarter = tokens // lax.axis_size("tensor")
     experts = local_experts * data_size
-    score_scale = head_dim ** (-0.5)
-    row0 = lax.axis_index("tensor") * quarter
-
-    def mine(array):
-        return lax.dynamic_slice_in_dim(array, row0, quarter, 0)
-
-    expert_ids = jnp.arange(experts, dtype=jnp.int32)
-    dense = jnp.sum(
-        jnp.where(mine(routes)[:, :, None] == expert_ids[None, None, :], mine(route_weights)[:, :, None], 0.0),
-        axis=1,
-    )
-    dense_high = dense.astype(bf)
-    dense_low = (dense - dense_high.astype(f32)).astype(bf)
-    spare = -2 * experts % LANES
-    packed = jnp.concatenate(
-        [mine(out_grad), dense_high, dense_low, jnp.zeros((quarter, spare), bf)], axis=1
-    )
     rows = data_size * quarter
-    units = local_experts * hidden_part
-    own_weights = jnp.concatenate(
-        [
-            jnp.transpose(w_gate_up, (2, 0, 3, 1)).reshape(2, units, model_width),
-            w_down.reshape(1, units, model_width),
-        ],
-        axis=0,
-    )
-    all_weights = lax.all_gather(own_weights, "tensor")
-    hidden = hidden_in.astype(f32)
-    hat_one, _ = rms_parts(hidden)
-    normed = (hat_one * norm1_gain).astype(bf)
-    query_proj = jnp.dot(normed, query_weight, preferred_element_type=f32).reshape(
-        tokens, local_heads, head_dim
-    )
-    key_proj = jnp.dot(normed, key_weight, preferred_element_type=f32)
-    value_low = jnp.dot(normed, value_weight, preferred_element_type=f32).astype(bf)
     places, starts = sequence_layout(seq_lens[0], tokens)
     cosine_table, sine_table = rotary_tables(places - starts, head_dim)
-    query_hat, _ = rms_parts(query_proj)
-    query_low = rotate(
-        query_hat * query_gain, cosine_table[:, None, :], sine_table[:, None, :]
-    ).astype(bf)
-    key_hat, _ = rms_parts(key_proj)
-    key_low = rotate(key_hat * key_gain, cosine_table, sine_table).astype(bf)
-    visible = (places[None, :] <= places[:, None]) & (places[None, :] >= starts[:, None])
-    scores = jnp.einsum("thd,sd->hts", query_low, key_low, preferred_element_type=f32) * score_scale
-    exponent = jnp.where(visible[None], jnp.exp(scores), 0.0)
-    totals = jnp.sum(exponent, axis=-1, keepdims=True)
-    soft_low = (exponent / totals).astype(bf)
-    mixed_low = (
-        jnp.einsum("hts,sd->thd", soft_low, value_low, preferred_element_type=f32)
-        .reshape(tokens, local_heads * head_dim)
-        .astype(bf)
+    cosines = jnp.concatenate([cosine_table, cosine_table], axis=1)
+    sines = jnp.concatenate([-sine_table, sine_table], axis=1)
+    starts = starts.reshape(1, -1).astype(jnp.int32)
+    gate_up = jnp.transpose(w_gate_up, (0, 2, 3, 1))
+    (
+        middle,
+        inputs,
+        gathered,
+        others,
+        mixed_low,
+        query_low,
+        key_low,
+        value_low,
+        raw_query,
+        raw_key,
+        normed,
+    ) = start_layer(
+        data_size,
+        experts,
+        hidden_in,
+        out_grad,
+        routes,
+        route_weights,
+        query_weight,
+        key_weight,
+        value_weight,
+        out_weight,
+        gate_up,
+        w_down,
+        cosines,
+        sines,
+        starts,
+        norm1_gain.reshape(1, -1),
+        norm2_gain.reshape(1, -1),
+        query_gain.reshape(1, -1),
+        key_gain.reshape(1, -1),
     )
-    hidden_q = mine(hidden_in)
-    partial = jnp.dot(mixed_low, out_weight, preferred_element_type=f32).astype(bf)
-    middle, inputs, gathered = exchange_tokens(data_size, partial, hidden_q, packed, norm2_gain)
     stage = run_experts if data_size <= 8 else large_experts
     hidden_out, kept, given, grad_middle, grad_mid_low, grad_gain_two = stage(
         data_size,
         inputs.reshape(rows, model_width),
         gathered.reshape(rows, -1),
-        all_weights,
+        gate_up,
+        w_down,
+        others,
         middle,
         norm2_gain,
         experts,
     )
     joined = (kept[0].astype(f32) + given[1].astype(f32)).astype(bf)
-    both = jnp.concatenate([cosine_table, cosine_table], axis=1)
-    signed = jnp.concatenate([-sine_table, sine_table], axis=1)
+    hidden_q = lax.dynamic_slice_in_dim(hidden_in, lax.axis_index("tensor") * quarter, quarter, 0)
     hidden_out, crossed, grad_hidden, in_low, out_low, gains = finish_layer(
         data_size,
         grad_mid_low,
         out_weight,
         mixed_low,
-        query_low.reshape(tokens, -1),
+        query_low,
         key_low,
         value_low,
-        query_proj.reshape(tokens, -1),
-        key_proj,
+        raw_query,
+        raw_key,
         normed,
         query_weight,
         key_weight,
         value_weight,
-        both,
-        signed,
-        starts.reshape(1, -1).astype(jnp.int32),
+        cosines,
+        sines,
+        starts,
         query_gain.reshape(1, -1),
         key_gain.reshape(1, -1),
         grad_middle,
@@ -1196,7 +1400,7 @@
     )
     grad_w_down = own_grads[2].reshape(local_experts, hidden_part, model_width)
     in_low = in_low.reshape(model_width, -1)
-    lead = local_heads * head_dim
+    lead = query_weight.shape[1]
     gains = gains.reshape(-1)
     return (
         hidden_out,

time: 534 us -> 501 us (0.938)
  Pallas kernels: 425 us -> 452 us
  matrix products: 18.1 us -> 0 us
  other arithmetic: 46.9 us -> 32.1 us
  between operations: 14.9 us -> 0.72 us
  local copies, waits for them, and re-layouts: 23.2 us -> 16 us
    pallas_call x1, Pallas kernels: 109 us -> 133 us  [start_layer(): pl.pallas_call(functools.partial(start_layer_body, size, experts), out_sh...]
    dot_general x6 -> x0, matrix products: 18.1 us -> none  [the longest x1 5.88 us: local(): jnp.dot(mixed_low, out_weight, preferred_element_type=f32).astype(bf)]
  transfers between devices with their start and end apart: 1 -> 0, of which waited for: 0 -> 0; matrix products, arithmetic and copies ran while one was open for 7% -> 0% of each run, Pallas kernels for 21% -> 0%
where the time goes in v6:
time: 501 us; the launch traced here: 500 us
  Pallas kernels  452 us (90%)
  other arithmetic  32.1 us (6%)
  local copies, waits for them, and re-layouts  16 us (3%)
    pallas_call x1, Pallas kernels, finish_layer(): pl.pallas_call(functools.partial(finish_layer_body, size), out_shape=(jax...  206 us
    pallas_call x1, Pallas kernels, start_layer(): pl.pallas_call(functools.partial(start_layer_body, size, experts), out_sh...  133 us
    pallas_call x1, Pallas kernels, run_experts(): pl.pallas_call(functools.partial(run_experts_body, size, local_experts, e...  113 us

profile of v6, /device:TPU:0, one launch (start us, length us, event | category | flops | bytes accessed | tf_op | source)
XLA Modules:
  0.0 500.4 jit_solution(11195327762426843744)
XLA Ops:
  0.6 0.8 reduce-window.8
  1.5 0.7 select_reduce_fusion
  2.2 0.0 copy-start.3
  2.2 1.0 fusion.1
  3.2 1.0 pad_maximum_fusion
  4.2 1.6 copy.30.route_ref
  5.8 1.6 copy.31.share_ref
  7.3 0.0 copy-done.3
  7.3 132.8 %start_layer.1 = (f32[128,2048]{1,0:T(8,128)}, bf16[8,128,2048]{2,1,0:T(8,128)(2,1)}, bf16[8,128,2176]{2,1,0:T(8,128)(2,1)}, bf16[3,3,2,192,2048]{4,3,2,1,0:T(8,...) custom-call(bf16[512,2048]{1,0:T(8,128)(2,1)} %token_ref.1, ...), custom_call_target="tpu_custom_call" | custom-call | tf_op jit(solution)/shard_map/start_layer/pallas_call | solution.py:436
  140.2 0.6 compare_convert_fusion.member_ref
  140.8 113.1 %run_experts.1 = (bf16[128,2048]{1,0:T(8,128)(2,1)}, bf16[2,3,384,2048]{3,2,1,0:T(8,128)(2,1)}, bf16[2,3,384,2048]{3,2,1,0:T(8,128)(2,1)}, f32[128,2048]{1,0:T(8...) custom-call(bf16[1024,2048]{1,0:T(8,128)(2,1)} %bitcast.41, bf16[1024,2176]{1,0:T(8,128)(2,1)} %bitcast.40, ...), custom_call_target="tpu_custom_call" | custom-call | tf_op jit(solution)/shard_map/run_experts/pallas_call | solution.py:809
  253.9 8.6 %fusion.cross_ref = bf16[3,384,2048]{2,1,0:T(8,128)(2,1)} fusion(bf16[2,3,384,2048]{3,2,1,0:T(8,128)(2,1)} %get-tuple-element.50, bf16[2,3,384,2048]{3,2,1,0:T(8,128)(2,1)} %get-tuple-element.49), kind=kLoop, calls=%fused_computation.3 | loop fusion | flops 9437184 | bytes 14155776 | tf_op jit(solution)/shard_map/convert_element_type | solution.py:1369
  262.5 1.9 constant_dynamic-slice_fusion.token_ref
  264.4 205.7 %finish_layer.1 = (bf16[512,2048]{1,0:T(8,128)(2,1)}, bf16[3,384,2048]{2,1,0:T(8,128)(2,1)}, bf16[512,2048]{1,0:T(8,128)(2,1)}, bf16[8,256,1280]{2,1,0:T(8,128)(...) custom-call(bf16[512,2048]{1,0:T(8,128)(2,1)} %get-tuple-element.39.gmid_low_ref, ...), custom_call_target="tpu_custom_call" | custom-call | tf_op jit(solution)/shard_map/finish_layer/pallas_call | solution.py:1178
  470.1 8.5 %bitcast_add_fusion = f32[3,384,2048]{2,1,0:T(8,128)S(1)} fusion(bf16[3,384,2048]{2,1,0:T(8,128)(2,1)} %get-tuple-element.57, bf16[2,3,384,2048]{3,2,1,0:T(8,128)(2,1)} %get-tuple-element.50, bf16[2,3,384,2048]{3,2,1,0:T(8,128)(2,1)} %get-tuple-element.49), kind=kLoop, calls=%fused_computation | loop fusion | flops 11796480 | bytes 23592960 | tf_op jit(solution)/shard_map/add | solution.py:1397
  478.6 0.7 slice.71
  479.4 3.1 copy.34
  482.5 0.0 copy-start
  482.5 0.0 slice-start
  482.5 2.0 slice.72
  484.5 1.3 copy-done
  485.8 0.0 slice-start.1
  485.8 4.7 bitcast_convert_fusion
  490.6 0.0 slice-done
  490.6 0.0 slice-done.1
  490.6 0.0 copy-start.4
  490.6 0.0 copy-start.2
  490.6 4.6 slice_convert_fusion
  495.2 0.0 copy-start.1
  495.2 1.5 slice_convert_fusion.1
  496.6 0.0 copy-done.4
  496.6 0.6 fusion.6
  497.2 0.5 slice_bitcast_fusion
  497.8 0.0 copy-done.2
  497.8 1.3 copy.37
  499.1 0.0 copy-done.1
  499.1 1.3 copy.38
  (4 shorter events, 0.0 us)
Async XLA Ops:
  2.2 5.1 %copy-start.3 = (s32[512]{0:T(512)}, s32[512]{0:T(512)S(1)}, u32[]{:S(2)}) copy-start(s32[512]{0:T(512)S(1)} %select_reduce_fusion) | copy-start | bytes 6148
  482.5 3.3 copy-start
  482.5 8.1 %slice-start = ((s8[5242880]{0:T(1024)(128)(4,1)}), s8[4194304]{0:T(1024)(128)(4,1)S(1)}, s32[]{:S(2)}) async-start(s8[5242880]{0:T(1024)(128)(4,1)} %bitcast.36), calls=%async_computation | async-start | bytes 8388608
  485.8 4.8 slice-start.1
  490.6 6.0 %copy-start.4 = (f32[1,4352]{1,0:T(1,128)S(1)}, f32[1,4352]{1,0:T(1,128)}, u32[]{:S(2)}) copy-start(f32[1,4352]{1,0:T(1,128)} %get-tuple-element.54) | copy-start | bytes 52228
  490.6 7.2 %copy-start.2 = (bf16[512,2048]{1,0:T(8,128)(2,1)S(1)}, bf16[512,2048]{1,0:T(8,128)(2,1)}, u32[]{:S(2)}) copy-start(bf16[512,2048]{1,0:T(8,128)(2,1)} %get-tuple-element.81) | copy-start | bytes 6291460
  495.2 3.9 copy-start.1

commit v7 on v6

--- a/solution.py
+++ b/solution.py
@@ -260,15 +260,15 @@
 
     def pump(passing=True):
         number = len(far)
-        if number >= 2:
-            old = far[number - 2]
-            if number - 2 < len(pieces):
+        if number >= 3:
+            old = far[number - 3]
+            if number - 3 < len(pieces):
                 old.wait_recv()
-                kind, expert, rows = piece_of(number - 2)[1]
+                kind, expert, rows = piece_of(number - 3)[1]
                 copy = push(
                     others_ref.at[1, kind, expert, rows],
                     others_ref.at[2, kind, expert, rows],
-                    (pass_sems.at[0, number - 2], pass_sems.at[1, number - 2]),
+                    (pass_sems.at[0, number - 3], pass_sems.at[1, number - 3]),
                     (dp, partner),
                 )
                 copy.start()
@@ -287,6 +287,7 @@
         else:
             far.append(None)
 
+    pump()
     pump()
     pump()
 
@@ -411,7 +412,9 @@
             packs.step(step + 4)
         pump()
         ring.step(step)
-    while len(far) < len(pieces) + 2:
+        if step % 2 == 1:
+            pump()
+    while len(far) < len(pieces) + 3:
         pump()
     packs.finish()
     ring.finish()
@@ -478,8 +481,8 @@
     size,
     local_experts,
     experts,
-    inputs_ref,
-    packs_ref,
+    inputs_hbm,
+    packs_hbm,
     gate_up_ref,
     down_ref,
     others_ref,
@@ -489,6 +492,8 @@
     hidden_out,
     kept_ref,
     given_ref,
+    cross_ref,
+    landing_ref,
     gmid_ref,
     gmid_all,
     gain_out,
@@ -500,6 +505,7 @@
     mix_slots,
     turned,
     stage,
+    landed,
     totals,
     load_sems,
     grad_sems,
@@ -507,6 +513,10 @@
     side_sems,
     store_sems,
     give_sems,
+    land_sems,
+    token_sems,
+    inputs_ref,
+    packs_ref,
 ):
     f32, bf = jnp.float32, jnp.bfloat16
     dp = lax.axis_index("dp")
@@ -521,6 +531,16 @@
     cut = width // 2
     wide = 512
     place = ring_place(dp, size)
+
+    def token_loads(index):
+        rows = pl.ds(pl.multiple_of(index * pair, pair), pair)
+        return (
+            pltpu.make_async_copy(inputs_hbm.at[rows], inputs_ref.at[rows], token_sems.at[0, index]),
+            pltpu.make_async_copy(packs_hbm.at[rows], packs_ref.at[rows], token_sems.at[1, index]),
+        )
+
+    for copy in token_loads(0):
+        copy.start()
     forward = (ring_index(place + 1, size), own)
     backward = (ring_index(place + size - 1, size), own)
     greet([forward, backward, (dp, partner), (dp, across)])
@@ -542,15 +562,25 @@
     ]
     for _, copy in loads:
         copy.start()
+    for index in range(1, half):
+        for copy in token_loads(index):
+            copy.start()
 
     grad_ring = (grad_parts, grad_slots, grad_sems)
     mix_ring = (mix_parts, mix_slots, mix_sems)
 
-    def ring_copy(ring, way, step, source):
+    ring_parts = 2
+    piece_rows = quarter // ring_parts
+
+    def ring_copy(ring, way, step, part, source):
         device = forward if way == 0 else backward
         _, slots, sems = ring
+        rows = pl.ds(part * piece_rows, piece_rows)
         return push(
-            source, slots.at[way, step], (sems.at[0, way, step], sems.at[1, way, step]), device
+            source.at[rows],
+            slots.at[way, step, rows],
+            (sems.at[0, way, step, part], sems.at[1, way, step, part]),
+            device,
         )
 
     def columns_of(way):
@@ -558,24 +588,33 @@
 
     def ring_step(ring, step, blocks, first=False):
         parts, slots, _ = ring
-        for way in (0, 1):
-            if first:
-                source = parts.at[blocks[way], :, columns_of(way)]
-            else:
-                source = slots.at[way, step - 1]
-                ring_copy(ring, way, step - 1, source).wait_recv()
-
-                def add(rows):
-                    slots[way, step - 1, rows, :] = (
-                        slots[way, step - 1, rows, :].astype(f32)
-                        + parts[blocks[way], rows, columns_of(way)].astype(f32)
-                    ).astype(bf)
-
-                row_loop(quarter, 16, add)
-            ring_copy(ring, way, step, source).start()
+        for part in range(ring_parts):
+            for way in (0, 1):
+                if first:
+                    source = parts.at[blocks[way], :, columns_of(way)]
+                else:
+                    source = slots.at[way, step - 1]
+                    ring_copy(ring, way, step - 1, part, source).wait_recv()
+
+                    def add(rows):
+                        rows = pl.ds(pl.multiple_of(rows.start + part * piece_rows, 16), rows.size)
+                        slots[way, step - 1, rows, :] = (
+                            slots[way, step - 1, rows, :].astype(f32)
+                            + parts[blocks[way], rows, columns_of(way)].astype(f32)
+                        ).astype(bf)
+
+                    row_loop(piece_rows, 16, add)
+                ring_copy(ring, way, step, part, source).start()
+
+    def ring_last(ring):
+        for part in range(ring_parts):
+            for way in (0, 1):
+                ring_copy(ring, way, size - 2, part, ring[1].at[way, size - 2]).wait_recv()
 
     def do_pair(index, carry):
         rows = pl.ds(pl.multiple_of(index * pair, pair), pair)
+        for copy in token_loads(index):
+            copy.wait()
         tail = packs_ref[rows, width:].astype(f32)
         lane = lax.broadcasted_iota(jnp.int32, tail.shape, 1)
         shares = []
@@ -645,61 +684,97 @@
         return carry
 
     lax.fori_loop(0, half, do_pair, 0)
-    def keep(index, slot):
-        target = kept_ref.at[index % members - 2, index // members]
-        return pltpu.make_async_copy(stage.at[slot], target, store_sems.at[slot])
-
-    def give(index, slot):
-        target = given_ref.at[index % members, index // members]
-        number = 2 * (index // members) + index % members
-        return push(
-            stage.at[slot], target, (give_sems.at[0, number], give_sems.at[1, number]), (dp, partner)
-        )
-
-    def weight_grads(first, last):
-        def run(index, carry):
-            kind = index // members
-            whose = index % members
-            slot = index % 2
-            member = jnp.where(whose < 2, 1 + 2 * whose, 2 * (3 - whose))
-
-            @pl.when((index >= 2) & (whose < 2))
-            def _():
-                keep(index - 2, slot).wait()
-
-            @pl.when(whose >= 2)
-            def _():
-                give(index - 2, slot).wait_send()
-
-            rows = pl.ds(pl.multiple_of(member * span, span), span)
-            for chunk in range(half):
-                some = pl.ds(chunk * pair, pair)
-                turned[:, some] = hidden[kind, some, rows].T
-
-            def do_columns(tile, carry):
-                here = pl.ds(pl.multiple_of(tile * wide, wide), wide)
-                source = inputs_ref if first < 2 * members else packs_ref
-                stage[slot, :, here] = matmul(turned[...], source[:, here]).astype(bf)
-                return carry
-
-            lax.fori_loop(0, width // wide, do_columns, 0)
-
-            @pl.when(whose < 2)
-            def _():
-                give(index, slot).start()
-
-            @pl.when(whose >= 2)
-            def _():
-                keep(index, slot).start()
-
+    group_units = (3, 1, 2, 0)
+    targets = (landing_ref, given_ref, cross_ref, kept_ref)
+
+    def tile_copies(group, kind, slot):
+        copies = []
+        for expert in range(local_experts):
+            at = expert + 2 * local_experts if isinstance(kind, int) else 2 * expert + kind
+            source = stage.at[slot, pl.ds(expert * part_units, part_units)]
+            target = targets[group].at[at]
+            if group < 2:
+                sems = (give_sems.at[0, group, at], give_sems.at[1, group, at])
+                copies.append(push(source, target, sems, (dp, partner)))
+            else:
+                copies.append(pltpu.make_async_copy(source, target, store_sems.at[group - 2, at]))
+        return copies
+
+    def tile_left(group, kind, slot):
+        for copy in tile_copies(group, kind, slot):
+            if group < 2:
+                copy.wait_send()
+            else:
+                copy.wait()
+
+    def land(kind):
+        copies = []
+        for expert in range(local_experts):
+            at = expert + 2 * local_experts if isinstance(kind, int) else 2 * expert + kind
+            rows = pl.ds(expert * part_units, part_units)
+            copies.append(
+                pltpu.make_async_copy(landing_ref.at[at], landed.at[rows], land_sems.at[expert])
+            )
+        return copies
+
+    def tile(group, kind, source, before):
+        number = 3 * group + kind
+        slot = number % 2
+        if before is not None:
+            before(slot)
+        if group == 2:
+            for copy in tile_copies(0, kind, slot):
+                copy.wait_recv()
+            for copy in land(kind):
+                copy.start()
+        rows = pl.ds(group_units[group] * span, span)
+        for chunk in range(half):
+            some = pl.ds(chunk * pair, pair)
+            turned[:, some] = hidden[kind, some, rows].T
+        if group == 2:
+            for copy in land(kind):
+                copy.wait()
+
+        def do_columns(tile, carry):
+            here = pl.ds(pl.multiple_of(tile * wide, wide), wide)
+            sums = matmul(turned[...], source[:, here])
+            if group == 2:
+                sums = sums + landed[:, here].astype(f32)
+            stage[slot, :, here] = sums.astype(bf)
             return carry
 
-        lax.fori_loop(first, last, run, 0)
+        lax.fori_loop(0, width // wide, do_columns, 0)
+        for copy in tile_copies(group, kind, slot):
+            copy.start()
+
+    def token_tiles(group):
+        def run(kind, carry):
+            if group == 0:
+                before = None
+            else:
+                def before(slot):
+                    @pl.when(kind == 0)
+                    def _():
+                        tile_left(group - 1, kind + 1, slot)
+
+                    @pl.when(kind == 1)
+                    def _():
+                        tile_left(group - 1, 2, slot)
+
+            tile(group, kind, inputs_ref, before)
+            return carry
+
+        lax.fori_loop(0, 2, run, 0)
+
+    def grad_tile(group):
+        def before(slot):
+            tile_left(group, jnp.int32(0), slot)
+
+        tile(group, 2, packs_ref, before)
 
     def final_sum():
         totals[...] = jnp.zeros_like(totals)
-        for way in (0, 1):
-            ring_copy(grad_ring, way, size - 2, grad_slots.at[way, size - 2]).wait_recv()
+        ring_last(grad_ring)
         base = own * quarter
 
         def finish(rows):
@@ -743,8 +818,7 @@
         spread(2, across, (dp, partner)).start()
 
     def final_mix():
-        for way in (0, 1):
-            ring_copy(mix_ring, way, size - 2, mix_slots.at[way, size - 2]).wait_recv()
+        ring_last(mix_ring)
 
         def finish(rows):
             for way in (0, 1):
@@ -770,7 +844,10 @@
     events = grad_events[:-1]
     events += [grad_events[-1], mix_events[0], closing] + mix_events[1:2] + [second_spread]
     events += mix_events[2:] + [final_mix]
-    work = [functools.partial(weight_grads, first, first + 2) for first in range(0, 3 * members, 2)]
+    work = []
+    for group in range(4):
+        work.append(functools.partial(token_tiles, group))
+        work.append(functools.partial(grad_tile, group))
     done = 0
     for number, piece in enumerate(work):
         piece()
@@ -778,11 +855,11 @@
         while done < upto:
             events[done]()
             done += 1
-    for slot in (0, 1):
-        keep(3 * members - 2 + slot, slot).wait()
-    for kind in range(3):
-        for whose in (0, 1):
-            give(kind * members + whose, 0).wait_recv()
+    tile_left(3, jnp.int32(1), 0)
+    tile_left(3, 2, 1)
+    for kind in (jnp.int32(0), jnp.int32(1), 2):
+        for copy in tile_copies(1, kind, 0):
+            copy.wait_recv()
     spread(1, own, (dp, partner)).wait_recv()
     spread(2, across, (dp, partner)).wait_recv()
     for index, device in ((0, across), (1, partner), (2, partner)):
@@ -790,7 +867,8 @@
     for ring in (grad_ring, mix_ring):
         for way in (0, 1):
             for step in range(size - 1):
-                ring_copy(ring, way, step, ring[1].at[way, step]).wait_send()
+                for part in range(ring_parts):
+                    ring_copy(ring, way, step, part, ring[1].at[way, step]).wait_send()
 
 
 def run_experts(size, inputs, packs, gate_up, down, others, middle, gain, experts):
@@ -810,14 +888,16 @@
         functools.partial(run_experts_body, size, local_experts, experts),
         out_shape=(
             jax.ShapeDtypeStruct((quarter, width), bf),
-            jax.ShapeDtypeStruct((2, 3, span, width), bf),
-            jax.ShapeDtypeStruct((2, 3, span, width), bf),
+            jax.ShapeDtypeStruct((3 * local_experts, part_units, width), bf),
+            jax.ShapeDtypeStruct((3 * local_experts, part_units, width), bf),
+            jax.ShapeDtypeStruct((3 * local_experts, part_units, width), bf),
+            jax.ShapeDtypeStruct((3 * local_experts, part_units, width), bf),
             jax.ShapeDtypeStruct((quarter, width), f32),
             jax.ShapeDtypeStruct((members * quarter, width), bf),
             jax.ShapeDtypeStruct((1, width), f32),
         ),
-        in_specs=[vmem, vmem, anywhere, anywhere, anywhere, vmem, vmem, vmem],
-        out_specs=(vmem, anywhere, anywhere, vmem, vmem, vmem),
+        in_specs=[anywhere] * 5 + [vmem] * 3,
+        out_specs=(vmem,) + (anywhere,) * 4 + (vmem,) * 3,
         scratch_shapes=[
             pltpu.VMEM((3, units, width), bf),
             pltpu.VMEM((3, rows, units), bf),
@@ -827,13 +907,18 @@
             pltpu.VMEM((2, size - 1, quarter, width // 2), bf),
             pltpu.VMEM((span, rows), bf),
             pltpu.VMEM((2, span, width), bf),
+            pltpu.VMEM((span, width), bf),
             pltpu.VMEM((8, width), f32),
             dma((3 * local_experts + 3 * span // LANES,)),
-            dma((2, 2, size - 1)),
-            dma((2, 2, size - 1)),
+            dma((2, 2, size - 1, 2)),
+            dma((2, 2, size - 1, 2)),
             dma((2, 3)),
-            dma((2,)),
-            dma((2, 6)),
+            dma((2, 3 * local_experts)),
+            dma((2, 2, 3 * local_experts)),
+            dma((local_experts,)),
+            dma((2, size // 2)),
+            pltpu.VMEM(inputs.shape, bf),
+            pltpu.VMEM(packs.shape, bf),
         ],
         compiler_params=pltpu.CompilerParams(
             collective_id=2, has_side_effects=True, vmem_limit_bytes=VMEM_LIMIT
@@ -854,25 +939,25 @@
 
 def finish_layer_body(
     size,
-    gmid_low_ref,
-    out_weight_ref,
-    mixed_ref,
-    query_ref,
-    key_ref,
-    value_ref,
-    raw_query_ref,
-    raw_key_ref,
-    normed_ref,
-    query_weight_ref,
-    key_weight_ref,
-    value_weight_ref,
+    gmid_low_hbm,
+    out_weight_hbm,
+    mixed_hbm,
+    query_hbm,
+    key_hbm,
+    value_hbm,
+    raw_query_hbm,
+    raw_key_hbm,
+    normed_hbm,
+    query_weight_hbm,
+    key_weight_hbm,
+    value_weight_hbm,
     cosine_ref,
     sine_ref,
     start_ref,
     query_gain_ref,
     key_gain_ref,
     middle_ref,
-    token_ref,
+    token_hbm,
     hidden_ref,
     cross_ref,
     gain_ref,
@@ -880,8 +965,10 @@
     hidden_all,
     crossed_ref,
     grad_all,
-    gather_a,
-    gather_b,
+    query_out,
+    key_out,
+    value_out,
+    gather_b_hbm,
     gains_out,
     qkv_ref,
     out_ref,
@@ -904,6 +991,23 @@
     sems_b,
     ring_sems,
     side_sems,
+    load_sems,
+    store_sems,
+    gather_a,
+    gather_b,
+    token_ref,
+    gmid_low_ref,
+    out_weight_ref,
+    mixed_ref,
+    query_ref,
+    key_ref,
+    value_ref,
+    raw_query_ref,
+    raw_key_ref,
+    normed_ref,
+    query_weight_ref,
+    key_weight_ref,
+    value_weight_ref,
 ):
     f32, bf = jnp.float32, jnp.bfloat16
     dp = lax.axis_index("dp")
@@ -919,6 +1023,32 @@
     forward = (ring_index(place + 1, size), own)
     backward = (ring_index(place + size - 1, size), own)
     ways = ((forward, 1), (backward, -1))
+    mine = pl.ds(pl.multiple_of(own * quarter, quarter), quarter)
+    home = own * quarter
+    loads = {}
+    for source, target in (
+        (gmid_low_hbm, gmid_low_ref),
+        (mixed_hbm, mixed_ref),
+        (out_weight_hbm, out_weight_ref),
+        (query_hbm, query_ref),
+        (key_hbm, key_ref),
+        (value_hbm, value_ref),
+        (raw_query_hbm, raw_query_ref),
+        (raw_key_hbm, raw_key_ref),
+        (normed_hbm, normed_ref),
+        (query_weight_hbm, query_weight_ref),
+        (key_weight_hbm, key_weight_ref),
+        (value_weight_hbm, value_weight_ref),
+        (token_hbm.at[mine], token_ref),
+    ):
+        copy = pltpu.make_async_copy(source, target, load_sems.at[len(loads)])
+        copy.start()
+        loads[id(target)] = copy
+
+    def loaded(*targets):
+        for target in targets:
+            loads[id(target)].wait()
+
     greet([forward, backward, (dp, partner), (dp, across)])
     waits = []
 
@@ -942,14 +1072,19 @@
 
     live = {}
 
-    def add_own(which, way, step):
+    ring_parts = 2
+    stores = []
+
+    def add_own(which, way, step, part):
         ref, slots, blocks, _ = sets[which]
-        live[which, way, step].wait_recv()
+        live[which, way, step, part].wait_recv()
         sign = ways[way][1]
         rows, columns = block_of(ref, wrap(place - sign * (2 + step)), way)
         base = rows.start
+        count = ref.shape[0] // size // ring_parts
 
         def add(inner):
+            inner = pl.ds(pl.multiple_of(inner.start + part * count, 16), inner.size)
             there = pl.ds(pl.multiple_of(base + inner.start, 16), inner.size)
             sums = (slots[way, step, inner, :].astype(f32) + ref[there, columns].astype(f32)).astype(bf)
             if step == size - 2:
@@ -957,38 +1092,64 @@
             else:
                 slots[way, step, inner, :] = sums
 
-        row_loop(ref.shape[0] // size, 16, add)
+        row_loop(count, 16, add)
+
+    def keep_block(which, way, block, part):
+        ref, _, blocks, _ = sets[which]
+        count, cut = ref.shape[0] // size // ring_parts, ref.shape[1] // 2
+        inner = pl.ds(part * count, count)
+        at = pl.multiple_of(block * (ref.shape[0] // size) + part * count, 16)
+        rows = pl.ds(at, count)
+        if which == 1:
+            targets = [(gather_b_hbm.at[rows, pl.ds(way * cut, cut)], way * cut, cut)]
+        elif way == 0:
+            targets = [(query_out.at[rows, pl.ds(0, cut)], 0, cut)]
+        else:
+            targets = [
+                (query_out.at[rows, pl.ds(cut, lead - cut)], cut, lead - cut),
+                (key_out.at[rows], lead, head_dim),
+                (value_out.at[rows], lead + head_dim, head_dim),
+            ]
+        for target, first, columns in targets:
+            source = blocks.at[block, inner, pl.ds(first, columns)]
+            copy = pltpu.make_async_copy(source, target, store_sems.at[len(stores)])
+            copy.start()
+            stores.append(copy)
 
     def ring_event(which, step):
         ref, slots, blocks, sems = sets[which]
         cut = ref.shape[1] // 2
-        for way, (device, sign) in enumerate(ways):
-            if step == 0:
-                source = ref.at[block_of(ref, wrap(place - sign), way)]
-            elif step < size:
-                add_own(which, way, step - 1)
-                source = slots.at[way, step - 1] if step < size - 1 else None
-            else:
-                live[which, way, step - 1].wait_recv()
-            if step >= 2 * size - 2:
-                continue
-            if step >= size - 1:
+        count = ref.shape[0] // size // ring_parts
+        for part in range(ring_parts):
+            inner = pl.ds(part * count, count)
+            for way, (device, sign) in enumerate(ways):
+                if step == 0:
+                    rows, columns = block_of(ref, wrap(place - sign), way)
+                    rows = pl.ds(pl.multiple_of(rows.start + part * count, 16), count)
+                    source = ref.at[rows, columns]
+                elif step < size:
+                    add_own(which, way, step - 1, part)
+                    source = slots.at[way, step - 1, inner] if step < size - 1 else None
+                else:
+                    live[which, way, step - 1, part].wait_recv()
                 block = wrap(place - sign * (step - size + 1))
-                source = blocks.at[block, :, pl.ds(way * cut, cut)]
-                target = source
-            else:
-                target = slots.at[way, step]
-            sem = (sems.at[0, way, step], sems.at[1, way, step])
-            live[which, way, step] = start(push(source, target, sem, device))
+                if step >= size - 1:
+                    keep_block(which, way, block, part)
+                if step >= 2 * size - 2:
+                    continue
+                if step >= size - 1:
+                    source = blocks.at[block, inner, pl.ds(way * cut, cut)]
+                    target = source
+                else:
+                    target = slots.at[way, step, inner]
+                sem = (sems.at[0, way, step, part], sems.at[1, way, step, part])
+                live[which, way, step, part] = start(push(source, target, sem, device))
 
     def part_rows(index):
         return pl.ds(pl.multiple_of(index * quarter, quarter), quarter)
 
     def side(index):
         return (side_sems.at[0, index], side_sems.at[1, index])
-
-    mine = part_rows(own)
-    home = own * quarter
 
     step_rows = 2 * LANES
     wide = 4 * LANES
@@ -1004,6 +1165,7 @@
 
         return lax.fori_loop(0, width // wide, columns, carry)
 
+    loaded(gmid_low_ref, mixed_ref)
     lax.fori_loop(0, lead // step_rows, out_rows, 0)
     ring_event(1, 0)
 
@@ -1019,7 +1181,9 @@
         grad_mixed[:, here] = matmul_nt(gmid_low_ref[...], out_weight_ref[here, :]).astype(bf)
         return carry
 
+    loaded(out_weight_ref)
     lax.fori_loop(0, lead // wide, mixed_columns, 0)
+    loaded(query_ref, key_ref, value_ref, raw_query_ref, raw_key_ref)
     key_sums[...] = jnp.zeros_like(key_sums)
     value_sums[...] = jnp.zeros_like(value_sums)
     head_totals[...] = jnp.zeros_like(head_totals)
@@ -1071,6 +1235,7 @@
         qkv_ref[rows, :] = matmul(turned[...], grad_heads[...]).astype(bf)
         return carry
 
+    loaded(normed_ref)
     lax.fori_loop(0, width // step_rows, in_rows, 0)
     ring_event(1, 3)
     ring_event(0, 0)
@@ -1083,6 +1248,7 @@
         partial[:, here] = sums.astype(bf)
         return carry
 
+    loaded(query_weight_ref, key_weight_ref, value_weight_ref)
     lax.fori_loop(0, width // wide, token_columns, 0)
     first = start(push(partial.at[part_rows(far_partner)], from_partner.at[1], side(0), (dp, partner)))
     second = start(push(partial.at[part_rows(partner)], from_partner.at[0], side(1), (dp, partner)))
@@ -1118,6 +1284,7 @@
         back = inverse * (scaled - hat * jnp.mean(scaled * hat, axis=-1, keepdims=True))
         grad_all[there, :] = (middle_ref[rows, :] + back).astype(bf)
 
+    loaded(token_ref)
     row_loop(quarter, 16, finish)
     spread = [start(push(grad_all.at[mine], grad_all.at[mine], side(3), (dp, across)))]
     spread.append(start(push(grad_all.at[mine], grad_all.at[mine], side(4), (dp, partner))))
@@ -1158,6 +1325,8 @@
         copy.wait_recv()
     for copy in waits:
         copy.wait_send()
+    for copy in stores:
+        copy.wait()
 
 
 def finish_layer(size, *arguments):
@@ -1166,8 +1335,8 @@
         _, out_weight, mixed, query, key, _, _, _, normed, query_weight, _, _, _, _, _, _, _, _, token_rows, _,
         cross, _, _,
     ) = arguments
-    quarter, width = token_rows.shape
-    tokens = normed.shape[0]
+    tokens, width = token_rows.shape
+    quarter = tokens // 4
     lead, head_dim = query.shape[1], key.shape[1]
     vmem = pl.BlockSpec(memory_space=pltpu.VMEM)
     anywhere = pl.BlockSpec(memory_space=pl.ANY)
@@ -1181,12 +1350,14 @@
             jax.ShapeDtypeStruct((tokens, width), bf),
             jax.ShapeDtypeStruct(cross.shape, bf),
             jax.ShapeDtypeStruct((tokens, width), bf),
-            jax.ShapeDtypeStruct((size, rows_a, columns), bf),
-            jax.ShapeDtypeStruct((size, rows_b, width), bf),
+            jax.ShapeDtypeStruct((width, lead), bf),
+            jax.ShapeDtypeStruct((width, head_dim), bf),
+            jax.ShapeDtypeStruct((width, head_dim), bf),
+            jax.ShapeDtypeStruct((lead, width), bf),
             jax.ShapeDtypeStruct((1, count), f32),
         ),
-        in_specs=[anywhere if argument is cross else vmem for argument in arguments],
-        out_specs=(vmem, anywhere) + (vmem,) * 4,
+        in_specs=[anywhere] * 12 + [vmem] * 6 + [anywhere, vmem, anywhere, vmem, vmem],
+        out_specs=(vmem, anywhere, vmem) + (anywhere,) * 4 + (vmem,),
         scratch_shapes=[
             pltpu.VMEM((width, columns), bf),
             pltpu.VMEM((lead, width), bf),
@@ -1205,11 +1376,17 @@
             pltpu.VMEM((2, 8, head_dim), f32),
             pltpu.VMEM((4, 1, count), f32),
             pltpu.VMEM((size, 1, count), f32),
-            dma((2, 2, 2 * size - 2)),
-            dma((2, 2, 2 * size - 2)),
+            dma((2, 2, 2 * size - 2, 2)),
+            dma((2, 2, 2 * size - 2, 2)),
             dma((2, size - 1)),
             dma((2, 12)),
-        ],
+            dma((13,)),
+            dma((12 * size,)),
+            pltpu.VMEM((size, rows_a, columns), bf),
+            pltpu.VMEM((size, rows_b, width), bf),
+            pltpu.VMEM((quarter, width), bf),
+        ]
+        + [pltpu.VMEM(argument.shape, argument.dtype) for argument in arguments[:12]],
         compiler_params=pltpu.CompilerParams(
             collective_id=1, has_side_effects=True, vmem_limit_bytes=VMEM_LIMIT
         ),
@@ -1281,11 +1458,13 @@
     grad_mid_low = lax.all_gather(grad_middle.astype(bf), "tensor", tiled=True)
     mixture = lax.psum_scatter(mixture_part, "dp", tiled=True).astype(f32)
     hidden_out = (middle + mixture).astype(bf)
-    zero = jnp.zeros(weight_grads.shape[1:], bf)
     sums = lax.psum_scatter(weight_grads.reshape(-1, model_width), "tensor", tiled=True)
-    kept = jnp.stack([zero, sums.reshape(zero.shape)])
-    given = jnp.stack([zero, zero])
-    return (hidden_out, kept, given, grad_middle, grad_mid_low, grad_gain_two)
+    sums = sums.reshape(3, local_experts, -1, model_width)
+    kept = jnp.concatenate(
+        [jnp.swapaxes(sums[:2], 0, 1).reshape(2 * local_experts, -1, model_width), sums[2]]
+    )
+    zero = jnp.zeros_like(kept)
+    return (hidden_out, kept, zero, zero, zero, grad_middle, grad_mid_low, grad_gain_two)
 
 
 def local(
@@ -1355,7 +1534,7 @@
         key_gain.reshape(1, -1),
     )
     stage = run_experts if data_size <= 8 else large_experts
-    hidden_out, kept, given, grad_middle, grad_mid_low, grad_gain_two = stage(
+    hidden_out, kept, given, joined, _, grad_middle, grad_mid_low, grad_gain_two = stage(
         data_size,
         inputs.reshape(rows, model_width),
         gathered.reshape(rows, -1),
@@ -1366,9 +1545,7 @@
         norm2_gain,
         experts,
     )
-    joined = (kept[0].astype(f32) + given[1].astype(f32)).astype(bf)
-    hidden_q = lax.dynamic_slice_in_dim(hidden_in, lax.axis_index("tensor") * quarter, quarter, 0)
-    hidden_out, crossed, grad_hidden, in_low, out_low, gains = finish_layer(
+    hidden_out, crossed, grad_hidden, query_sum, key_sum, value_sum, out_sum, gains = finish_layer(
         data_size,
         grad_mid_low,
         out_weight,
@@ -1388,30 +1565,31 @@
         query_gain.reshape(1, -1),
         key_gain.reshape(1, -1),
         grad_middle,
-        hidden_q,
+        hidden_in,
         hidden_out,
         joined,
         norm1_gain.reshape(1, -1),
         grad_gain_two.reshape(1, -1),
     )
-    own_grads = kept[1].astype(f32) + given[0].astype(f32) + crossed.astype(f32)
+    def whole(first, last):
+        parts = (kept[first:last], given[first:last], crossed[first:last])
+        return parts[0].astype(f32) + parts[1].astype(f32) + parts[2].astype(f32)
+
     grad_w_gate_up = jnp.transpose(
-        own_grads[:2].reshape(2, local_experts, hidden_part, model_width), (1, 3, 0, 2)
+        whole(0, 2 * local_experts).reshape(local_experts, 2, hidden_part, model_width), (0, 3, 1, 2)
     )
-    grad_w_down = own_grads[2].reshape(local_experts, hidden_part, model_width)
-    in_low = in_low.reshape(model_width, -1)
-    lead = query_weight.shape[1]
+    grad_w_down = whole(2 * local_experts, 3 * local_experts)
     gains = gains.reshape(-1)
     return (
         hidden_out,
         grad_hidden,
         gains[:model_width],
-        in_low[:, :lead].astype(f32),
-        in_low[:, lead : lead + head_dim].astype(f32),
-        in_low[:, lead + head_dim :].astype(f32),
+        query_sum.astype(f32),
+        key_sum.astype(f32),
+        value_sum.astype(f32),
         gains[2 * model_width : 2 * model_width + head_dim],
         gains[2 * model_width + head_dim :],
-        out_low.reshape(-1, model_width).astype(f32),
+        out_sum.astype(f32),
         gains[model_width : 2 * model_width],
         grad_w_gate_up,
         grad_w_down,

time: 501 us -> 483 us (0.964)
  Pallas kernels: 452 us -> 445 us
  local copies, waits for them, and re-layouts: 16 us -> 9.26 us
    pallas_call x1, Pallas kernels: 206 us -> 197 us  [finish_layer(): pl.pallas_call(functools.partial(finish_layer_body, size), out_shape=(jax...]
    convert_element_type x4, other arithmetic: 19.4 us -> 13.2 us  [the longest x1 4.45 us: local(): out_sum.astype(f32)]
    pallas_call x1, Pallas kernels: 113 us -> 119 us  [run_experts(): pl.pallas_call(functools.partial(run_experts_body, size, local_experts, e...]
    add x1 -> x2, other arithmetic: 8.53 us -> 10.1 us  [whole(): return parts[0].astype(f32) + parts[1].astype(f32) + parts[2].astype(f32)]
where the time goes in v7:
time: 483 us; the launch traced here: 482 us
  Pallas kernels  445 us (92%)
  other arithmetic  27.5 us (6%)
  local copies, waits for them, and re-layouts  9.26 us (2%)
    pallas_call x1, Pallas kernels, finish_layer(): pl.pallas_call(functools.partial(finish_layer_body, size), out_shape=(jax...  197 us
    pallas_call x1, Pallas kernels, start_layer(): pl.pallas_call(functools.partial(start_layer_body, size, experts), out_sh...  129 us
    pallas_call x1, Pallas kernels, run_experts(): pl.pallas_call(functools.partial(run_experts_body, size, local_experts, e...  119 us
    add x2, other arithmetic, whole(): return parts[0].astype(f32) + parts[1].astype(f32) + parts[2].astype(f32)  10.1 us

profile of v7, /device:TPU:0, one launch (start us, length us, event | category | flops | bytes accessed | tf_op | source)
XLA Modules:
  0.0 482.4 jit_solution(5601044397905765115)
XLA Ops:
  0.6 0.8 reduce-window.8
  1.5 0.7 select_reduce_fusion
  2.2 0.0 copy-start.5
  2.3 0.6 compare_convert_fusion.member_ref
  2.9 1.6 copy.29.route_ref
  4.4 1.6 copy.30.share_ref
  6.0 1.0 fusion
  7.0 1.0 pad_maximum_fusion
  8.0 0.0 copy-done.5
  8.0 128.6 %start_layer.1 = (f32[128,2048]{1,0:T(8,128)}, bf16[8,128,2048]{2,1,0:T(8,128)(2,1)}, bf16[8,128,2176]{2,1,0:T(8,128)(2,1)}, bf16[3,3,2,192,2048]{4,3,2,1,0:T(8,...) custom-call(bf16[512,2048]{1,0:T(8,128)(2,1)} %token_hbm.1, ...), custom_call_target="tpu_custom_call" | custom-call | tf_op jit(solution)/shard_map/start_layer/pallas_call | solution.py:439
  136.6 118.9 %run_experts.1 = (bf16[128,2048]{1,0:T(8,128)(2,1)}, bf16[6,192,2048]{2,1,0:T(8,128)(2,1)}, bf16[6,192,2048]{2,1,0:T(8,128)(2,1)}, bf16[6,192,2048]{2,1,0:T(8,12...) custom-call(bf16[1024,2048]{1,0:T(8,128)(2,1)} %bitcast.28, ...), custom_call_target="tpu_custom_call" | custom-call | tf_op jit(solution)/shard_map/run_experts/pallas_call | solution.py:887
  255.5 197.4 %finish_layer.1 = (bf16[512,2048]{1,0:T(8,128)(2,1)}, bf16[6,192,2048]{2,1,0:T(8,128)(2,1)}, bf16[512,2048]{1,0:T(8,128)(2,1)}, bf16[2048,1024]{1,0:T(8,128)(2,1...) custom-call(bf16[512,2048]{1,0:T(8,128)(2,1)} %get-tuple-element.42.g, ...), custom_call_target="tpu_custom_call" | custom-call | tf_op jit(solution)/shard_map/finish_layer/pallas_call | solution.py:1347
  452.9 1.1 slice_bitcast_fusion
  454.1 1.3 fusion.5
  455.4 2.1 convert_element_type.43
  457.5 0.0 slice-start
  457.5 2.2 convert_element_type.44
  459.7 0.0 slice-start.1
  459.7 0.0 copy-start
  459.7 5.0 %convert_add_fusion.1 = f32[2,192,2048]{2,1,0:T(8,128)} fusion(bf16[6,192,2048]{2,1,0:T(8,128)(2,1)} %get-tuple-element.63, bf16[6,192,2048]{2,1,0:T(8,128)(2,1)} %get-tuple-element.62, bf16[6,192,2048]{2,1,0:T(8,128)(2,1)} %get-tuple-element.61), kind=kLoop, calls=%fused_computation.1 | loop fusion | flops 3932160 | bytes 7864320 | tf_op jit(solution)/shard_map/add | solution.py:1576
  464.7 0.0 slice-done
  464.8 0.0 slice-done.1
  464.8 0.0 copy-done
  464.8 0.0 copy-start.2
  464.8 5.1 %convert_add_fusion = f32[4,192,2048]{2,1,0:T(8,128)} fusion(bf16[6,192,2048]{2,1,0:T(8,128)(2,1)} %get-tuple-element.63, bf16[6,192,2048]{2,1,0:T(8,128)(2,1)S(1)} %copy-done, bf16[6,192,2048]{2,1,0:T(8,128)(2,1)S(1)} %bitcast.26), kind=kLoop, calls=%fused_computation | loop fusion | flops 7864320 | bytes 15728640 | tf_op jit(solution)/shard_map/add | solution.py:1576
  469.9 0.0 copy-done.2
  469.9 0.0 copy-start.1
  469.9 4.4 convert_element_type.42
  474.3 0.0 copy-done.1
  474.3 0.0 copy-start.4
  474.3 4.4 convert_element_type.45
  478.7 0.0 copy-done.4
  478.8 0.0 copy-start.3
  478.8 1.3 copy.33
  480.1 1.0 copy-done.3
  481.1 1.3 copy.34
  (4 shorter events, 0.0 us)
Async XLA Ops:
  2.2 5.7 %copy-start.5 = (s32[512]{0:T(512)}, s32[512]{0:T(512)S(1)}, u32[]{:S(2)}) copy-start(s32[512]{0:T(512)S(1)} %select_reduce_fusion) | copy-start | bytes 6148
  457.5 7.3 %slice-start = ((s8[4718592]{0:T(1024)(128)(4,1)}), s8[4194304]{0:T(1024)(128)(4,1)S(1)}, s32[]{:S(2)}) async-start(s8[4718592]{0:T(1024)(128)(4,1)} %bitcast.25), calls=%async_computation | async-start | bytes 8388608
  459.7 5.0 %slice-start.1 = ((s8[4718592]{0:T(1024)(128)(4,1)}), s8[524288]{0:T(1024)(128)(4,1)S(1)}, s32[]{:S(2)}) async-start(s8[4718592]{0:T(1024)(128)(4,1)} %bitcast.25), calls=%async_computation.1 | async-start | bytes 1048576
  459.7 5.0 %copy-start = (bf16[6,192,2048]{2,1,0:T(8,128)(2,1)S(1)}, bf16[6,192,2048]{2,1,0:T(8,128)(2,1)}, u32[]{:S(2)}) copy-start(bf16[6,192,2048]{2,1,0:T(8,128)(2,1)} %get-tuple-element.62) | copy-start | bytes 14155780
  464.8 5.1 %copy-start.2 = (bf16[2048,1024]{1,0:T(8,128)(2,1)S(1)}, bf16[2048,1024]{1,0:T(8,128)(2,1)}, u32[]{:S(2)}) copy-start(bf16[2048,1024]{1,0:T(8,128)(2,1)} %get-tuple-element.57) | copy-start | bytes 12582916
  469.9 4.4 copy-start.1
  474.3 4.5 copy-start.4
  478.8 2.3 copy-start.3

commit v8 on v7

--- a/solution.py
+++ b/solution.py
@@ -172,16 +172,16 @@
     query_gain_ref,
     key_gain_ref,
     middle_ref,
-    inputs_ref,
-    packs_ref,
+    inputs_out,
+    packs_out,
     others_ref,
-    mixed_ref,
-    query_ref,
+    mixed_out,
+    query_out,
     key_ref,
     value_ref,
-    raw_query_ref,
+    raw_query_out,
     raw_key_ref,
-    normed_ref,
+    normed_out,
     query_weight,
     key_weight,
     value_weight,
@@ -197,6 +197,13 @@
     near_sems,
     far_sems,
     pass_sems,
+    store_sems,
+    inputs_ref,
+    packs_ref,
+    mixed_ref,
+    query_ref,
+    raw_query_ref,
+    normed_ref,
 ):
     f32, bf = jnp.float32, jnp.bfloat16
     dp = lax.axis_index("dp")
@@ -205,7 +212,7 @@
     quarter, width = middle_ref.shape
     tokens = token_ref.shape[0]
     head_dim = key_ref.shape[1]
-    lead = query_ref.shape[1]
+    lead = query_weight_ref.shape[1]
     heads = lead // head_dim
     place = ring_place(dp, size)
     loads = []
@@ -292,17 +299,15 @@
     pump()
 
     tail = packs_ref.shape[2] - width
-    lane = lax.broadcasted_iota(jnp.int32, (quarter, tail), 1)
-    name = jnp.where(lane < experts, lane, lane - experts)
-    dense = jnp.zeros((quarter, tail), f32)
-    for choice in range(route_ref.shape[1]):
-        named = route_ref[mine, choice : choice + 1]
-        dense = dense + jnp.where(named == name, share_ref[mine, choice : choice + 1], 0.0)
-    high = dense.astype(bf)
-    low = (dense - high.astype(f32)).astype(bf)
-    packs_ref[size - 1, :, width:] = jnp.where(
-        lane < experts, high.astype(f32), jnp.where(lane < 2 * experts, low.astype(f32), 0.0)
-    ).astype(bf)
+    line = lax.broadcasted_iota(jnp.int32, (tail, quarter), 0)
+    name = jnp.where(line < experts, line, line - experts)
+    dense = jnp.zeros((tail, quarter), f32)
+    for choice in range(route_ref.shape[0]):
+        named = route_ref[choice : choice + 1, mine]
+        dense = dense + jnp.where(named == name, share_ref[choice : choice + 1, mine], 0.0)
+    high = dense.astype(bf).astype(f32)
+    both = jnp.where(line < experts, high, jnp.where(line < 2 * experts, dense - high, 0.0))
+    packs_ref[size - 1, :, width:] = both.T.astype(bf)
     above.wait()
     packs = GatherRing(size, packs_ref, pack_sems)
     packs.send(0)
@@ -358,6 +363,16 @@
     packs.step(1)
     pump()
     lax.fori_loop(heads // 2, heads, do_head, 0)
+    stores = []
+
+    def leave(*pairs):
+        for source, target in pairs:
+            copy = pltpu.make_async_copy(source, target, store_sems.at[len(stores)])
+            copy.start()
+            stores.append(copy)
+
+    leave((raw_query_ref, raw_query_out), (query_ref, query_out))
+    leave((normed_ref, normed_out), (mixed_ref, mixed_out))
     packs.step(2)
     loads[3].wait()
 
@@ -410,10 +425,13 @@
     for step in range(size - 1):
         if step + 4 < size - 1:
             packs.step(step + 4)
+        if step + 4 == size - 1:
+            leave((packs_ref, packs_out))
         pump()
         ring.step(step)
         if step % 2 == 1:
             pump()
+    leave((inputs_ref, inputs_out))
     while len(far) < len(pieces) + 3:
         pump()
     packs.finish()
@@ -421,7 +439,7 @@
     first.wait_send()
     second.wait_send()
     third.wait_send()
-    for copy in near + passed:
+    for copy in near + passed + stores:
         copy.wait()
 
 
@@ -452,7 +470,7 @@
             jax.ShapeDtypeStruct((tokens, width), bf),
         ),
         in_specs=[vmem, anywhere, vmem, vmem] + [anywhere] * 6 + [vmem] * 7,
-        out_specs=(vmem, vmem, vmem, anywhere) + (vmem,) * 7,
+        out_specs=(vmem,) + (anywhere,) * 5 + (vmem, vmem, anywhere, vmem, anywhere),
         scratch_shapes=[
             pltpu.VMEM(query_weight.shape, bf),
             pltpu.VMEM(key_weight.shape, bf),
@@ -469,6 +487,13 @@
             dma((2, 3 * local)),
             dma((2, 6 * local)),
             dma((2, 6 * local)),
+            dma((6,)),
+            pltpu.VMEM((size, quarter, width), bf),
+            pltpu.VMEM((size, quarter, columns), bf),
+            pltpu.VMEM((tokens, lead), bf),
+            pltpu.VMEM((tokens, lead), bf),
+            pltpu.VMEM((tokens, lead), f32),
+            pltpu.VMEM((tokens, width), bf),
         ],
         compiler_params=pltpu.CompilerParams(
             collective_id=0, has_side_effects=True, vmem_limit_bytes=VMEM_LIMIT
@@ -528,7 +553,6 @@
     units = weights.shape[1]
     members = others_ref.shape[0] + 1
     span = units // members
-    cut = width // 2
     wide = 512
     place = ring_place(dp, size)
 
@@ -570,7 +594,8 @@
     mix_ring = (mix_parts, mix_slots, mix_sems)
 
     ring_parts = 2
-    piece_rows = quarter // ring_parts
+    way_rows = quarter // 2
+    piece_rows = way_rows // ring_parts
 
     def ring_copy(ring, way, step, part, source):
         device = forward if way == 0 else backward
@@ -583,24 +608,22 @@
             device,
         )
 
-    def columns_of(way):
-        return pl.ds(way * cut, cut)
-
     def ring_step(ring, step, blocks, first=False):
         parts, slots, _ = ring
         for part in range(ring_parts):
             for way in (0, 1):
                 if first:
-                    source = parts.at[blocks[way], :, columns_of(way)]
+                    source = parts.at[blocks[way], pl.ds(way * way_rows, way_rows)]
                 else:
                     source = slots.at[way, step - 1]
                     ring_copy(ring, way, step - 1, part, source).wait_recv()
 
                     def add(rows):
                         rows = pl.ds(pl.multiple_of(rows.start + part * piece_rows, 16), rows.size)
+                        there = pl.ds(pl.multiple_of(rows.start + way * way_rows, 16), rows.size)
                         slots[way, step - 1, rows, :] = (
                             slots[way, step - 1, rows, :].astype(f32)
-                            + parts[blocks[way], rows, columns_of(way)].astype(f32)
+                            + parts[blocks[way], there, :].astype(f32)
                         ).astype(bf)
 
                     row_loop(piece_rows, 16, add)
@@ -777,14 +800,11 @@
         ring_last(grad_ring)
         base = own * quarter
 
-        def finish(rows):
-            sums = jnp.concatenate(
-                [
-                    grad_slots[0, size - 2, rows, :].astype(f32),
-                    grad_slots[1, size - 2, rows, :].astype(f32),
-                ],
-                axis=-1,
-            ) + grad_parts[size - 1, rows, :].astype(f32)
+        def finish(way, inner):
+            rows = pl.ds(pl.multiple_of(inner.start + way * way_rows, 16), inner.size)
+            sums = grad_slots[way, size - 2, inner, :].astype(f32) + grad_parts[
+                size - 1, rows, :
+            ].astype(f32)
             middle = middle_ref[rows, :]
             inverse = lax.rsqrt(jnp.mean(middle * middle, axis=-1, keepdims=True) + EPSILON)
             hat = middle * inverse
@@ -799,7 +819,8 @@
             gmid_ref[rows, :] = grad
             gmid_all[pl.ds(pl.multiple_of(base + rows.start, 16), rows.size), :] = grad.astype(bf)
 
-        row_loop(quarter, 16, finish)
+        for way in (0, 1):
+            row_loop(way_rows, 16, functools.partial(finish, way))
         gain_out[...] = jnp.sum(totals[...], axis=0, keepdims=True)
 
     def rows_of(index):
@@ -820,16 +841,16 @@
     def final_mix():
         ring_last(mix_ring)
 
-        def finish(rows):
-            for way in (0, 1):
-                columns = columns_of(way)
-                hidden_out[rows, columns] = (
-                    middle_ref[rows, columns]
-                    + mix_slots[way, size - 2, rows, :].astype(f32)
-                    + mix_parts[size - 1, rows, columns].astype(f32)
-                ).astype(bf)
-
-        row_loop(quarter, 16, finish)
+        def finish(way, inner):
+            rows = pl.ds(pl.multiple_of(inner.start + way * way_rows, 16), inner.size)
+            hidden_out[rows, :] = (
+                middle_ref[rows, :]
+                + mix_slots[way, size - 2, inner, :].astype(f32)
+                + mix_parts[size - 1, rows, :].astype(f32)
+            ).astype(bf)
+
+        for way in (0, 1):
+            row_loop(way_rows, 16, functools.partial(finish, way))
 
     def closing():
         final_sum()
@@ -903,8 +924,8 @@
             pltpu.VMEM((3, rows, units), bf),
             pltpu.VMEM((size, quarter, width), bf),
             pltpu.VMEM((size, quarter, width), bf),
-            pltpu.VMEM((2, size - 1, quarter, width // 2), bf),
-            pltpu.VMEM((2, size - 1, quarter, width // 2), bf),
+            pltpu.VMEM((2, size - 1, quarter // 2, width), bf),
+            pltpu.VMEM((2, size - 1, quarter // 2, width), bf),
             pltpu.VMEM((span, rows), bf),
             pltpu.VMEM((2, span, width), bf),
             pltpu.VMEM((span, width), bf),
@@ -968,8 +989,11 @@
     query_out,
     key_out,
     value_out,
-    gather_b_hbm,
-    gains_out,
+    outer_out,
+    first_out,
+    second_out,
+    query_gain_out,
+    key_gain_out,
     qkv_ref,
     out_ref,
     slots_a,
@@ -1062,33 +1086,31 @@
         (out_ref, slots_b, gather_b, sems_b),
     )
 
-    def block_of(ref, block, way):
-        rows = ref.shape[0] // size
-        cut = ref.shape[1] // 2
-        return (pl.ds(pl.multiple_of(block * rows, rows), rows), pl.ds(way * cut, cut))
-
     def wrap(value):
         return (value + 2 * size) % size
 
     live = {}
 
-    ring_parts = 2
+    ring_parts = 2 if lead // size % 64 == 0 else 1
     stores = []
+
+    def ring_rows(ref):
+        rows = ref.shape[0] // size
+        return rows, rows // 2, rows // 2 // ring_parts
 
     def add_own(which, way, step, part):
         ref, slots, blocks, _ = sets[which]
         live[which, way, step, part].wait_recv()
-        sign = ways[way][1]
-        rows, columns = block_of(ref, wrap(place - sign * (2 + step)), way)
-        base = rows.start
-        count = ref.shape[0] // size // ring_parts
+        rows, half, count = ring_rows(ref)
+        base = wrap(place - ways[way][1] * (2 + step)) * rows + way * half
 
         def add(inner):
             inner = pl.ds(pl.multiple_of(inner.start + part * count, 16), inner.size)
             there = pl.ds(pl.multiple_of(base + inner.start, 16), inner.size)
-            sums = (slots[way, step, inner, :].astype(f32) + ref[there, columns].astype(f32)).astype(bf)
+            sums = (slots[way, step, inner, :].astype(f32) + ref[there, :].astype(f32)).astype(bf)
             if step == size - 2:
-                blocks[place, inner, columns] = sums
+                final = pl.ds(pl.multiple_of(inner.start + way * half, 16), inner.size)
+                blocks[place, final, :] = sums
             else:
                 slots[way, step, inner, :] = sums
 
@@ -1096,37 +1118,32 @@
 
     def keep_block(which, way, block, part):
         ref, _, blocks, _ = sets[which]
-        count, cut = ref.shape[0] // size // ring_parts, ref.shape[1] // 2
-        inner = pl.ds(part * count, count)
-        at = pl.multiple_of(block * (ref.shape[0] // size) + part * count, 16)
-        rows = pl.ds(at, count)
+        rows, half, count = ring_rows(ref)
+        inner = pl.ds(way * half + part * count, count)
+        there = pl.ds(pl.multiple_of(block * rows + way * half + part * count, 16), count)
         if which == 1:
-            targets = [(gather_b_hbm.at[rows, pl.ds(way * cut, cut)], way * cut, cut)]
-        elif way == 0:
-            targets = [(query_out.at[rows, pl.ds(0, cut)], 0, cut)]
+            targets = [(outer_out, 0, width)]
         else:
             targets = [
-                (query_out.at[rows, pl.ds(cut, lead - cut)], cut, lead - cut),
-                (key_out.at[rows], lead, head_dim),
-                (value_out.at[rows], lead + head_dim, head_dim),
+                (query_out, 0, lead),
+                (key_out, lead, head_dim),
+                (value_out, lead + head_dim, head_dim),
             ]
         for target, first, columns in targets:
             source = blocks.at[block, inner, pl.ds(first, columns)]
-            copy = pltpu.make_async_copy(source, target, store_sems.at[len(stores)])
+            copy = pltpu.make_async_copy(source, target.at[there], store_sems.at[len(stores)])
             copy.start()
             stores.append(copy)
 
     def ring_event(which, step):
         ref, slots, blocks, sems = sets[which]
-        cut = ref.shape[1] // 2
-        count = ref.shape[0] // size // ring_parts
+        rows, half, count = ring_rows(ref)
         for part in range(ring_parts):
             inner = pl.ds(part * count, count)
             for way, (device, sign) in enumerate(ways):
                 if step == 0:
-                    rows, columns = block_of(ref, wrap(place - sign), way)
-                    rows = pl.ds(pl.multiple_of(rows.start + part * count, 16), count)
-                    source = ref.at[rows, columns]
+                    at = wrap(place - sign) * rows + way * half + part * count
+                    source = ref.at[pl.ds(pl.multiple_of(at, 16), count)]
                 elif step < size:
                     add_own(which, way, step - 1, part)
                     source = slots.at[way, step - 1, inner] if step < size - 1 else None
@@ -1138,7 +1155,7 @@
                 if step >= 2 * size - 2:
                     continue
                 if step >= size - 1:
-                    source = blocks.at[block, inner, pl.ds(way * cut, cut)]
+                    source = blocks.at[block, pl.ds(way * half + part * count, count)]
                     target = source
                 else:
                     target = slots.at[way, step, inner]
@@ -1320,7 +1337,11 @@
             sem = (ring_sems.at[0, step - 4], ring_sems.at[1, step - 4])
             small = start(push(ref, ref, sem, forward))
     small.wait_recv()
-    gains_out[...] = jnp.sum(ring_gains[...], axis=0)
+    gains = jnp.sum(ring_gains[...], axis=0)
+    first_out[...] = gains[:, :width]
+    second_out[...] = gains[:, width : 2 * width]
+    query_gain_out[...] = gains[:, 2 * width : 2 * width + head_dim]
+    key_gain_out[...] = gains[:, 2 * width + head_dim :]
     for copy in (spread[1], spread[2], shown[1], shown[2], crossing):
         copy.wait_recv()
     for copy in waits:
@@ -1354,15 +1375,18 @@
             jax.ShapeDtypeStruct((width, head_dim), bf),
             jax.ShapeDtypeStruct((width, head_dim), bf),
             jax.ShapeDtypeStruct((lead, width), bf),
-            jax.ShapeDtypeStruct((1, count), f32),
+            jax.ShapeDtypeStruct((1, width), f32),
+            jax.ShapeDtypeStruct((1, width), f32),
+            jax.ShapeDtypeStruct((1, head_dim), f32),
+            jax.ShapeDtypeStruct((1, head_dim), f32),
         ),
         in_specs=[anywhere] * 12 + [vmem] * 6 + [anywhere, vmem, anywhere, vmem, vmem],
-        out_specs=(vmem, anywhere, vmem) + (anywhere,) * 4 + (vmem,),
+        out_specs=(vmem, anywhere, vmem) + (anywhere,) * 4 + (vmem,) * 4,
         scratch_shapes=[
             pltpu.VMEM((width, columns), bf),
             pltpu.VMEM((lead, width), bf),
-            pltpu.VMEM((2, size - 1, rows_a, columns // 2), bf),
-            pltpu.VMEM((2, size - 1, rows_b, width // 2), bf),
+            pltpu.VMEM((2, size - 1, rows_a // 2, columns), bf),
+            pltpu.VMEM((2, size - 1, rows_b // 2, width), bf),
             pltpu.VMEM((tokens, lead), bf),
             pltpu.VMEM((tokens, columns), bf),
             pltpu.VMEM((tokens, head_dim), f32),
@@ -1381,7 +1405,7 @@
             dma((2, size - 1)),
             dma((2, 12)),
             dma((13,)),
-            dma((12 * size,)),
+            dma((16 * size,)),
             pltpu.VMEM((size, rows_a, columns), bf),
             pltpu.VMEM((size, rows_b, width), bf),
             pltpu.VMEM((quarter, width), bf),
@@ -1392,6 +1416,45 @@
         ),
         name="finish_layer",
     )(*arguments)
+
+
+def widen_body(refs):
+    f32 = jnp.float32
+    for source, target in zip(refs[:4], refs[12:16]):
+        target[...] = source[...].astype(f32)
+    for first, target in ((4, refs[16]), (7, refs[17])):
+        sums = refs[first][...].astype(f32) + refs[first + 1][...].astype(f32)
+        target[...] = sums + refs[first + 2][...].astype(f32)
+    refs[18][...] = refs[10][...]
+    refs[19][...] = refs[11][...]
+
+
+def widen(query, key, value, outer, shares, split, hidden, grads):
+    f32 = jnp.float32
+    steps = 8
+    width = outer.shape[1]
+    shares = [share.reshape(-1, width) for share in shares]
+    rest = shares[0].shape[0] - split
+
+    def rows(count, columns, first=0):
+        block = count // steps
+        assert count % steps == 0 and block % 16 == 0 and first % block == 0
+        return pl.BlockSpec((block, columns), lambda step: (step + first // block, 0))
+
+    plain = [rows(*array.shape) for array in (query, key, value, outer)]
+    pair = [rows(*array.shape) for array in (hidden, grads)]
+    first, second = rows(split, width), rows(rest, width)
+    return pl.pallas_call(
+        lambda *refs: widen_body(refs),
+        grid=(steps,),
+        out_shape=[jax.ShapeDtypeStruct(a.shape, f32) for a in (query, key, value, outer)]
+        + [jax.ShapeDtypeStruct((split, width), f32), jax.ShapeDtypeStruct((rest, width), f32)]
+        + [jax.ShapeDtypeStruct(a.shape, a.dtype) for a in (hidden, grads)],
+        in_specs=plain + [first] * 3 + [rows(rest, width, split)] * 3 + pair,
+        out_specs=plain + [first, second] + pair,
+        compiler_params=pltpu.CompilerParams(vmem_limit_bytes=VMEM_LIMIT),
+        name="widen",
+    )(query, key, value, outer, *shares, *shares, hidden, grads)
 
 
 def large_experts(size, inputs, packs, gate_up, down, others, middle, gain, experts):
@@ -1517,8 +1580,8 @@
         experts,
         hidden_in,
         out_grad,
-        routes,
-        route_weights,
+        routes.T,
+        route_weights.T,
         query_weight,
         key_weight,
         value_weight,
@@ -1545,7 +1608,7 @@
         norm2_gain,
         experts,
     )
-    hidden_out, crossed, grad_hidden, query_sum, key_sum, value_sum, out_sum, gains = finish_layer(
+    hidden_out, crossed, grad_hidden, query_sum, key_sum, value_sum, out_sum, *gains = finish_layer(
         data_size,
         grad_mid_low,
         out_weight,
@@ -1571,26 +1634,26 @@
         norm1_gain.reshape(1, -1),
         grad_gain_two.reshape(1, -1),
     )
-    def whole(first, last):
-        parts = (kept[first:last], given[first:last], crossed[first:last])
-        return parts[0].astype(f32) + parts[1].astype(f32) + parts[2].astype(f32)
-
+    split = 2 * local_experts * hidden_part
+    query_sum, key_sum, value_sum, out_sum, gate_up_sum, down_sum, hidden_out, grad_hidden = widen(
+        query_sum, key_sum, value_sum, out_sum, (kept, given, crossed), split, hidden_out, grad_hidden
+    )
     grad_w_gate_up = jnp.transpose(
-        whole(0, 2 * local_experts).reshape(local_experts, 2, hidden_part, model_width), (0, 3, 1, 2)
+        gate_up_sum.reshape(local_experts, 2, hidden_part, model_width), (0, 3, 1, 2)
     )
-    grad_w_down = whole(2 * local_experts, 3 * local_experts)
-    gains = gains.reshape(-1)
+    grad_w_down = down_sum.reshape(local_experts, hidden_part, model_width)
+    gains = [gain.reshape(-1) for gain in gains]
     return (
         hidden_out,
         grad_hidden,
-        gains[:model_width],
-        query_sum.astype(f32),
-        key_sum.astype(f32),
-        value_sum.astype(f32),
-        gains[2 * model_width : 2 * model_width + head_dim],
-        gains[2 * model_width + head_dim :],
-        out_sum.astype(f32),
-        gains[model_width : 2 * model_width],
+        gains[0],
+        query_sum,
+        key_sum,
+        value_sum,
+        gains[2],
+        gains[3],
+        out_sum,
+        gains[1],
         grad_w_gate_up,
         grad_w_down,
     )

time: 483 us -> 468 us (0.969)
  other arithmetic: 27.5 us -> 4.2 us
  Pallas kernels: 445 us -> 461 us
  local copies, waits for them, and re-layouts: 9.26 us -> 2.24 us
    pallas_call x0 -> x1, Pallas kernels: none -> 20.4 us  [widen(): pl.pallas_call(lambda *refs: widen_body(refs), grid=(steps,), out_shape=[...]
    convert_element_type x4 -> x0, other arithmetic: 13.2 us -> none  [the longest x1 4.45 us: local(): out_sum.astype(f32)]
    add x2 -> x0, other arithmetic: 10.1 us -> none  [whole(): return parts[0].astype(f32) + parts[1].astype(f32) + parts[2].astype(f32)]
where the time goes in v8:
time: 468 us
  Pallas kernels  461 us (99%)
    pallas_call x1, Pallas kernels, finish_layer(): pl.pallas_call(functools.partial(finish_layer_body, size), out_shape=(jax...  198 us
    pallas_call x1, Pallas kernels, start_layer(): pl.pallas_call(functools.partial(start_layer_body, size, experts), out_sh...  124 us
    pallas_call x1, Pallas kernels, run_experts(): pl.pallas_call(functools.partial(run_experts_body, size, local_experts, e...  118 us
    pallas_call x1, Pallas kernels, widen(): pl.pallas_call(lambda *refs: widen_body(refs), grid=(steps,), out_shape=[...  20.4 us

profile of v8, /device:TPU:0, one launch (start us, length us, event | category | flops | bytes accessed | tf_op | source)
XLA Modules:
  0.0 467.8 jit_solution(2185803520690618646)
XLA Ops:
  0.6 0.8 reduce-window.8
  1.5 0.7 select_reduce_fusion
  2.2 0.0 copy-start
  2.3 0.6 compare_convert_fusion.member_ref
  2.9 1.0 fusion
  3.9 1.0 pad_maximum_fusion
  4.9 0.0 copy-done
  4.9 124.2 %start_layer.1 = (f32[128,2048]{1,0:T(8,128)}, bf16[8,128,2048]{2,1,0:T(8,128)(2,1)}, bf16[8,128,2176]{2,1,0:T(8,128)(2,1)}, bf16[3,3,2,192,2048]{4,3,2,1,0:T(8,...) custom-call(bf16[512,2048]{1,0:T(8,128)(2,1)} %token_hbm.1, ...), custom_call_target="tpu_custom_call" | custom-call | tf_op jit(solution)/shard_map/start_layer/pallas_call | solution.py:457
  129.1 118.4 %run_experts.1 = (bf16[128,2048]{1,0:T(8,128)(2,1)}, bf16[6,192,2048]{2,1,0:T(8,128)(2,1)}, bf16[6,192,2048]{2,1,0:T(8,128)(2,1)}, bf16[6,192,2048]{2,1,0:T(8,12...) custom-call(bf16[1024,2048]{1,0:T(8,128)(2,1)} %bitcast.35, ...), custom_call_target="tpu_custom_call" | custom-call | tf_op jit(solution)/shard_map/run_experts/pallas_call | solution.py:908
  247.4 197.7 %finish_layer.1 = (bf16[512,2048]{1,0:T(8,128)(2,1)}, bf16[6,192,2048]{2,1,0:T(8,128)(2,1)}, bf16[512,2048]{1,0:T(8,128)(2,1)}, bf16[2048,1024]{1,0:T(8,128)(2,1...) custom-call(bf16[512,2048]{1,0:T(8,128)(2,1)} %get-tuple-element.53., ...), custom_call_target="tpu_custom_call" | custom-call | tf_op jit(solution)/shard_map/finish_layer/pallas_call | solution.py:1368
  445.1 0.0 copy-start.2
  445.1 0.0 copy-start.4
  445.1 0.0 copy-start.3
  445.1 0.0 copy-start.1
  445.1 20.4 %widen.1 = (f32[2048,1024]{1,0:T(8,128)}, f32[2048,128]{1,0:T(8,128)}, f32[2048,128]{1,0:T(8,128)}, f32[1024,2048]{1,0:T(8,128)}, f32[768,2048]{1,0:T(8,128)}, /...) custom-call(bf16[2048,1024]{1,0:T(8,128)(2,1)} %get-tuple-element.65.refs_0_, ...), custom_call_target="tpu_custom_call" | custom-call | tf_op jit(solution)/shard_map/widen/pallas_call | solution.py:1447
  465.5 0.0 copy-done.2
  465.5 0.6 copy.31
  466.1 0.0 copy-done.4
  466.1 0.5 copy.32
  466.7 0.0 copy-done.3
  466.7 0.5 copy.33
  467.2 0.0 copy-done.1
  467.2 0.6 copy.34
  (3 shorter events, 0.0 us)
Async XLA Ops:
  2.2 2.6 copy-start
  445.1 20.4 %copy-start.2 = (f32[1,2048]{1,0:T(1,128)S(1)}, f32[1,2048]{1,0:T(1,128)}, u32[]{:S(2)}) copy-start(f32[1,2048]{1,0:T(1,128)} %get-tuple-element.76) | copy-start | bytes 24580
  445.1 21.0 %copy-start.4 = (f32[1,128]{1,0:T(1,128)S(1)}, f32[1,128]{1,0:T(1,128)}, u32[]{:S(2)}) copy-start(f32[1,128]{1,0:T(1,128)} %get-tuple-element.80) | copy-start | bytes 1540
  445.1 21.5 %copy-start.3 = (f32[1,128]{1,0:T(1,128)S(1)}, f32[1,128]{1,0:T(1,128)}, u32[]{:S(2)}) copy-start(f32[1,128]{1,0:T(1,128)} %get-tuple-element.81) | copy-start | bytes 1540
  445.1 22.0 %copy-start.1 = (f32[1,2048]{1,0:T(1,128)S(1)}, f32[1,2048]{1,0:T(1,128)}, u32[]{:S(2)}) copy-start(f32[1,2048]{1,0:T(1,128)} %get-tuple-element.83) | copy-start | bytes 24580

commit v9 on v8

--- a/solution.py
+++ b/solution.py
@@ -3,6 +3,7 @@
 
 import jax
 import jax.numpy as jnp
+import numpy as np
 from jax import lax
 from jax.experimental import pallas as pl
 from jax.experimental.pallas import tpu as pltpu
@@ -24,14 +25,17 @@
 
 
 def rotary_tables(positions, head_dim):
-    halves = jnp.arange(head_dim // 2, dtype=jnp.float32)
+    lane = jnp.arange(head_dim, dtype=jnp.int32)
+    halves = (lane % (head_dim // 2)).astype(jnp.float32)
     inverse = jnp.exp(halves * (-2.0 * math.log(ROPE_BASE) / head_dim))
     angles = positions.astype(jnp.float32)[:, None] * inverse[None, :]
-    return (jnp.cos(angles), jnp.sin(angles))
+    sines = jnp.sin(angles)
+    return (jnp.cos(angles), jnp.where(lane[None, :] < head_dim // 2, -sines, sines))
 
 
 def sequence_layout(lengths, token_count):
-    endings = jnp.cumsum(lengths)
+    order = jnp.arange(lengths.shape[0], dtype=jnp.int32)
+    endings = jnp.sum(jnp.where(order[:, None] <= order[None, :], lengths[:, None], 0), axis=0)
     places = jnp.arange(token_count, dtype=jnp.int32)
     starts = jnp.sum(jnp.where(endings[None, :] <= places[:, None], lengths[None, :], 0), axis=1)
     return (places, starts)
@@ -862,9 +866,10 @@
         blocks = (slot_of(delta, size), slot_of(-delta, size))
         grad_events.append(functools.partial(ring_step, grad_ring, step, blocks))
         mix_events.append(functools.partial(ring_step, mix_ring, step, blocks))
-    events = grad_events[:-1]
-    events += [grad_events[-1], mix_events[0], closing] + mix_events[1:2] + [second_spread]
-    events += mix_events[2:] + [final_mix]
+    events = [grad_events[0]]
+    for first, second in zip(grad_events[1:], mix_events):
+        events += [first, second]
+    events += [closing, mix_events[-1], second_spread, final_mix]
     work = []
     for group in range(4):
         work.append(functools.partial(token_tiles, group))
@@ -900,8 +905,8 @@
     rows = inputs.shape[0]
     quarter = rows // size
     units = members * span
-    expert_of = (jnp.arange(units, dtype=jnp.int32) // (span // local_experts)) % local_experts
-    member = (expert_of[None, :] == jnp.arange(local_experts, dtype=jnp.int32)[:, None]).astype(f32)
+    expert_of = (np.arange(units) // (span // local_experts)) % local_experts
+    member = jnp.asarray(expert_of[None, :] == np.arange(local_experts)[:, None], f32)
     vmem = pl.BlockSpec(memory_space=pltpu.VMEM)
     anywhere = pl.BlockSpec(memory_space=pl.ANY)
     dma = pltpu.SemaphoreType.DMA
@@ -1235,10 +1240,12 @@
             head_totals[0] += jnp.sum(terms.reshape(-1, 8, head_dim), axis=0)
         return carry
 
-    lax.fori_loop(0, heads // 2, do_head, 0)
+    lax.fori_loop(0, heads // 4, do_head, 0)
     ring_event(1, 1)
-    lax.fori_loop(heads // 2, heads, do_head, 0)
+    lax.fori_loop(heads // 4, 5 * heads // 8, do_head, 0)
     ring_event(1, 2)
+    lax.fori_loop(5 * heads // 8, heads, do_head, 0)
+    ring_event(1, 3)
     low, terms = back_through_head(
         scale * key_sums[...], raw_key_ref[...], key_gain_ref[...], cosine_ref[...], sine_ref[...]
     )
@@ -1254,7 +1261,7 @@
 
     loaded(normed_ref)
     lax.fori_loop(0, width // step_rows, in_rows, 0)
-    ring_event(1, 3)
+    ring_event(1, 4)
     ring_event(0, 0)
 
     def token_columns(tile, carry):
@@ -1269,7 +1276,7 @@
     lax.fori_loop(0, width // wide, token_columns, 0)
     first = start(push(partial.at[part_rows(far_partner)], from_partner.at[1], side(0), (dp, partner)))
     second = start(push(partial.at[part_rows(partner)], from_partner.at[0], side(1), (dp, partner)))
-    ring_event(1, 4)
+    ring_event(1, 5)
     first.wait_recv()
     away = across * quarter
 
@@ -1280,7 +1287,7 @@
     row_loop(quarter, 16, join)
     third = start(push(joined, from_across, side(2), (dp, across)))
     ring_event(0, 1)
-    ring_event(1, 5)
+    ring_event(1, 6)
     second.wait_recv()
     third.wait_recv()
     totals[...] = jnp.zeros_like(totals)
@@ -1311,7 +1318,7 @@
     pair_gains[0, :, 2 * width + head_dim :] = jnp.sum(head_totals[1], axis=0, keepdims=True)
     swap = start(push(pair_gains.at[0], pair_gains.at[1], side(5), (dp, partner)))
     ring_event(0, 2)
-    ring_event(1, 6)
+    ring_event(1, 7)
     far = part_rows(across)
     shown[0].wait_recv()
     shown.append(start(push(hidden_all.at[far], hidden_all.at[far], side(11), (dp, partner))))
@@ -1321,15 +1328,15 @@
     pair_gains[2] = pair_gains[0] + pair_gains[1]
     swap = start(push(pair_gains.at[2], pair_gains.at[3], side(7), (dp, across)))
     ring_event(0, 3)
-    ring_event(1, 7)
+    ring_event(1, 8)
     swap.wait_recv()
     crossing = start(push(cross_ref, crossed_ref, side(8), (dp, across)))
     ring_gains[place] = pair_gains[2] + pair_gains[3]
     small = None
     for step in range(4, 2 * size - 1):
         ring_event(0, step)
-        if step + 4 < 2 * size - 1:
-            ring_event(1, step + 4)
+        if step + 5 < 2 * size - 1:
+            ring_event(1, step + 5)
         if step - 4 < size - 1:
             if small is not None:
                 small.wait_recv()
@@ -1558,9 +1565,7 @@
     experts = local_experts * data_size
     rows = data_size * quarter
     places, starts = sequence_layout(seq_lens[0], tokens)
-    cosine_table, sine_table = rotary_tables(places - starts, head_dim)
-    cosines = jnp.concatenate([cosine_table, cosine_table], axis=1)
-    sines = jnp.concatenate([-sine_table, sine_table], axis=1)
+    cosines, sines = rotary_tables(places - starts, head_dim)
     starts = starts.reshape(1, -1).astype(jnp.int32)
     gate_up = jnp.transpose(w_gate_up, (0, 2, 3, 1))
     (

time: 468 us -> 463 us (0.989)
  Pallas kernels: 461 us -> 456 us
where the time goes in v9:
time: 463 us
  Pallas kernels  456 us (98%)
    pallas_call x1, Pallas kernels, finish_layer(): pl.pallas_call(functools.partial(finish_layer_body, size), out_shape=(jax...  197 us
    pallas_call x1, Pallas kernels, start_layer(): pl.pallas_call(functools.partial(start_layer_body, size, experts), out_sh...  124 us
    pallas_call x1, Pallas kernels, run_experts(): pl.pallas_call(functools.partial(run_experts_body, size, local_experts, e...  115 us
    pallas_call x1, Pallas kernels, widen(): pl.pallas_call(lambda *refs: widen_body(refs), grid=(steps,), out_shape=[...  20.4 us

profile of v9, /device:TPU:0, one launch (start us, length us, event | category | flops | bytes accessed | tf_op | source)
XLA Modules:
  0.0 462.6 jit_solution(11644831317843219235)
XLA Ops:
  0.6 0.7 select_reduce_fusion.1
  1.4 0.7 select_reduce_fusion
  2.1 0.0 copy-start
  2.1 1.8 negate_select_fusion
  4.0 0.0 copy-done
  4.0 124.2 %start_layer.1 = (f32[128,2048]{1,0:T(8,128)}, bf16[8,128,2048]{2,1,0:T(8,128)(2,1)}, bf16[8,128,2176]{2,1,0:T(8,128)(2,1)}, bf16[3,3,2,192,2048]{4,3,2,1,0:T(8,...) custom-call(bf16[512,2048]{1,0:T(8,128)(2,1)} %token_hbm.1, ...), custom_call_target="tpu_custom_call" | custom-call | tf_op jit(solution)/shard_map/start_layer/pallas_call | solution.py:461
  128.2 114.5 %run_experts.1 = (bf16[128,2048]{1,0:T(8,128)(2,1)}, bf16[6,192,2048]{2,1,0:T(8,128)(2,1)}, bf16[6,192,2048]{2,1,0:T(8,128)(2,1)}, bf16[6,192,2048]{2,1,0:T(8,12...) custom-call(bf16[1024,2048]{1,0:T(8,128)(2,1)} %bitcast.33, ...), custom_call_target="tpu_custom_call" | custom-call | tf_op jit(solution)/shard_map/run_experts/pallas_call | solution.py:913
  242.7 197.2 %finish_layer.1 = (bf16[512,2048]{1,0:T(8,128)(2,1)}, bf16[6,192,2048]{2,1,0:T(8,128)(2,1)}, bf16[512,2048]{1,0:T(8,128)(2,1)}, bf16[2048,1024]{1,0:T(8,128)(2,1...) custom-call(bf16[512,2048]{1,0:T(8,128)(2,1)} %get-tuple-element.53., ...), custom_call_target="tpu_custom_call" | custom-call | tf_op jit(solution)/shard_map/finish_layer/pallas_call | solution.py:1375
  440.0 0.0 copy-start.2
  440.0 0.0 copy-start.4
  440.0 0.0 copy-start.3
  440.0 0.0 copy-start.1
  440.0 20.4 %widen.1 = (f32[2048,1024]{1,0:T(8,128)}, f32[2048,128]{1,0:T(8,128)}, f32[2048,128]{1,0:T(8,128)}, f32[1024,2048]{1,0:T(8,128)}, f32[768,2048]{1,0:T(8,128)}, /...) custom-call(bf16[2048,1024]{1,0:T(8,128)(2,1)} %get-tuple-element.65.refs_0_, ...), custom_call_target="tpu_custom_call" | custom-call | tf_op jit(solution)/shard_map/widen/pallas_call | solution.py:1454
  460.4 0.0 copy-done.2
  460.4 0.6 copy.32
  461.0 0.0 copy-done.4
  461.0 0.5 copy.33
  461.5 0.0 copy-done.3
  461.5 0.5 copy.34
  462.0 0.0 copy-done.1
  462.0 0.6 copy.35
  (3 shorter events, 0.0 us)
Async XLA Ops:
  2.1 1.8 copy-start
  440.0 20.4 %copy-start.2 = (f32[1,2048]{1,0:T(1,128)S(1)}, f32[1,2048]{1,0:T(1,128)}, u32[]{:S(2)}) copy-start(f32[1,2048]{1,0:T(1,128)} %get-tuple-element.76) | copy-start | bytes 24580
  440.0 21.0 %copy-start.4 = (f32[1,128]{1,0:T(1,128)S(1)}, f32[1,128]{1,0:T(1,128)}, u32[]{:S(2)}) copy-start(f32[1,128]{1,0:T(1,128)} %get-tuple-element.80) | copy-start | bytes 1540
  440.0 21.5 %copy-start.3 = (f32[1,128]{1,0:T(1,128)S(1)}, f32[1,128]{1,0:T(1,128)}, u32[]{:S(2)}) copy-start(f32[1,128]{1,0:T(1,128)} %get-tuple-element.81) | copy-start | bytes 1540
  440.0 22.0 %copy-start.1 = (f32[1,2048]{1,0:T(1,128)S(1)}, f32[1,2048]{1,0:T(1,128)}, u32[]{:S(2)}) copy-start(f32[1,2048]{1,0:T(1,128)} %get-tuple-element.83) | copy-start | bytes 24580

commit v10 on v9

--- a/solution.py
+++ b/solution.py
@@ -1438,7 +1438,7 @@
 
 def widen(query, key, value, outer, shares, split, hidden, grads):
     f32 = jnp.float32
-    steps = 8
+    steps = 4
     width = outer.shape[1]
     shares = [share.reshape(-1, width) for share in shares]
     rest = shares[0].shape[0] - split

time: 463 us -> 462 us (level)
  no operation moved by 1% of the time
where the time goes in v10:
time: 462 us; the launch traced here: 461 us
  Pallas kernels  455 us (98%)
    pallas_call x1, Pallas kernels, finish_layer(): pl.pallas_call(functools.partial(finish_layer_body, size), out_shape=(jax...  197 us
    pallas_call x1, Pallas kernels, start_layer(): pl.pallas_call(functools.partial(start_layer_body, size, experts), out_sh...  124 us
    pallas_call x1, Pallas kernels, run_experts(): pl.pallas_call(functools.partial(run_experts_body, size, local_experts, e...  115 us
    pallas_call x1, Pallas kernels, widen(): pl.pallas_call(lambda *refs: widen_body(refs), grid=(steps,), out_shape=[...  19.1 us

profile of v10, /device:TPU:0, one launch (start us, length us, event | category | flops | bytes accessed | tf_op | source)
XLA Modules:
  0.0 461.4 jit_solution(14777750845769965519)
XLA Ops:
  0.6 0.7 select_reduce_fusion.1
  1.4 0.7 select_reduce_fusion
  2.1 0.0 copy-start
  2.1 1.8 negate_select_fusion
  4.0 0.0 copy-done
  4.0 124.2 %start_layer.1 = (f32[128,2048]{1,0:T(8,128)}, bf16[8,128,2048]{2,1,0:T(8,128)(2,1)}, bf16[8,128,2176]{2,1,0:T(8,128)(2,1)}, bf16[3,3,2,192,2048]{4,3,2,1,0:T(8,...) custom-call(bf16[512,2048]{1,0:T(8,128)(2,1)} %token_hbm.1, ...), custom_call_target="tpu_custom_call" | custom-call | tf_op jit(solution)/shard_map/start_layer/pallas_call | solution.py:461
  128.2 114.5 %run_experts.1 = (bf16[128,2048]{1,0:T(8,128)(2,1)}, bf16[6,192,2048]{2,1,0:T(8,128)(2,1)}, bf16[6,192,2048]{2,1,0:T(8,128)(2,1)}, bf16[6,192,2048]{2,1,0:T(8,12...) custom-call(bf16[1024,2048]{1,0:T(8,128)(2,1)} %bitcast.33, ...), custom_call_target="tpu_custom_call" | custom-call | tf_op jit(solution)/shard_map/run_experts/pallas_call | solution.py:913
  242.7 197.2 %finish_layer.1 = (bf16[512,2048]{1,0:T(8,128)(2,1)}, bf16[6,192,2048]{2,1,0:T(8,128)(2,1)}, bf16[512,2048]{1,0:T(8,128)(2,1)}, bf16[2048,1024]{1,0:T(8,128)(2,1...) custom-call(bf16[512,2048]{1,0:T(8,128)(2,1)} %get-tuple-element.53., ...), custom_call_target="tpu_custom_call" | custom-call | tf_op jit(solution)/shard_map/finish_layer/pallas_call | solution.py:1375
  440.0 0.0 copy-start.2
  440.0 0.0 copy-start.4
  440.0 0.0 copy-start.3
  440.0 0.0 copy-start.1
  440.0 19.1 %widen.1 = (f32[2048,1024]{1,0:T(8,128)}, f32[2048,128]{1,0:T(8,128)}, f32[2048,128]{1,0:T(8,128)}, f32[1024,2048]{1,0:T(8,128)}, f32[768,2048]{1,0:T(8,128)}, /...) custom-call(bf16[2048,1024]{1,0:T(8,128)(2,1)} %get-tuple-element.65.refs_0_, ...), custom_call_target="tpu_custom_call" | custom-call | tf_op jit(solution)/shard_map/widen/pallas_call | solution.py:1454
  459.1 0.0 copy-done.2
  459.2 0.6 copy.32
  459.8 0.0 copy-done.4
  459.8 0.5 copy.33
  460.3 0.0 copy-done.3
  460.3 0.5 copy.34
  460.8 0.0 copy-done.1
  460.8 0.6 copy.35
  (3 shorter events, 0.0 us)
Async XLA Ops:
  2.1 1.8 copy-start
  440.0 19.2 %copy-start.2 = (f32[1,2048]{1,0:T(1,128)S(1)}, f32[1,2048]{1,0:T(1,128)}, u32[]{:S(2)}) copy-start(f32[1,2048]{1,0:T(1,128)} %get-tuple-element.76) | copy-start | bytes 24580
  440.0 19.8 %copy-start.4 = (f32[1,128]{1,0:T(1,128)S(1)}, f32[1,128]{1,0:T(1,128)}, u32[]{:S(2)}) copy-start(f32[1,128]{1,0:T(1,128)} %get-tuple-element.80) | copy-start | bytes 1540
  440.0 20.3 %copy-start.3 = (f32[1,128]{1,0:T(1,128)S(1)}, f32[1,128]{1,0:T(1,128)}, u32[]{:S(2)}) copy-start(f32[1,128]{1,0:T(1,128)} %get-tuple-element.81) | copy-start | bytes 1540
  440.0 20.8 %copy-start.1 = (f32[1,2048]{1,0:T(1,128)S(1)}, f32[1,2048]{1,0:T(1,128)}, u32[]{:S(2)}) copy-start(f32[1,2048]{1,0:T(1,128)} %get-tuple-element.83) | copy-start | bytes 24580
